TPU v7x, 256 devices: a whole 4x4x8 slice. The times are simulated.
256 devices in a mesh: dp: 8 (over z_lo, core), expert: 32 (over y, x, z_hi).
Axes of the slice: x: 4, y: 4, z: 8 (z_hi: 2, z_lo: 4; z = z_hi * 4 + z_lo), core: 2. Of those that a mesh axis runs over, the one named last changes fastest.
Arguments:
- tokens: bfloat16 [32768, 3584], P(('dp', 'expert')), may hold values from -6 to 6
- cotangent: bfloat16 [32768, 3584], P(('dp', 'expert')), may hold values from -6 to 6
- gates: float32 [32768, 1], P(('dp', 'expert')), may hold values from 0.1 to 1
- routes: int32 [32768, 1], P(('dp', 'expert')), may hold values from 0 to 31; in each aligned block of 128 rows (0 to 127, 128 to 255, ...) at most 5 rows name the same one
- w_up: bfloat16 [32, 3584, 1024], P('expert', None, 'dp'), may hold values from -0.09375 to 0.09375
- w_down: bfloat16 [32, 1024, 3584], P('expert', 'dp'), may hold values from -0.1875 to 0.1875
- m_up: bfloat16 [32, 3584, 1024], P('expert', None, 'dp'), may hold values from -3 to 3
- v_up: bfloat16 [32, 3584, 1024], P('expert', None, 'dp'), may hold values from 0.099609375 to 1
- m_down: bfloat16 [32, 1024, 3584], P('expert', 'dp'), may hold values from -3 to 3
- v_down: bfloat16 [32, 1024, 3584], P('expert', 'dp'), may hold values from 0.099609375 to 1
- leaving: int32 [1], replicated, may hold values from 0 to 31
- tile_owner: int32 [32], replicated, may hold values from 0 to 31, each once
Outputs:
- update_up: bfloat16 [32, 3584, 1024], P('expert', None, 'dp')
- update_down: bfloat16 [32, 1024, 3584], P('expert', 'dp')
- adopted_up: bfloat16 [32, 112, 1024], P('expert', None, 'dp')
- adopted_down: bfloat16 [32, 112, 1024], P('expert', None, 'dp')
Inputs may be any that keep to these rules, and one draw needn't show every extreme that they name: `routes`: each row names one expert; within the 128 rows of one device no expert is named more than 5 times, a bound that some block reaches in some devices. `tile_owner`: A permutation of the 32 device indices of the expert axis.
All inputs are finite; a program needn't handle non-finite values.
Results may differ from a plain program's by a relative error of at most 0.0041.
Values may be sent and summed in bfloat16 or wider, within the bound.
No kernel may reach another device: no remote copies, remote signals or barrier semaphores. Data moves between devices by JAX's collectives and lax.ppermute only.
A program may use at most 128 MiB of HBM per device.

v0:
```python
import jax
import jax.numpy as jnp
from jax import lax
from jax.sharding import PartitionSpec as P

BETA_ONE = 0.9
BETA_TWO = 0.95
EPSILON = 1e-08


def expert_terms(rows_x, rows_c, up_tile, down_tile):
    preact = jnp.dot(rows_x, up_tile, preferred_element_type=jnp.float32)
    squash = jax.nn.sigmoid(preact)
    hidden = (preact * squash).astype(jnp.bfloat16)
    slope_val = squash * (1.0 + preact * (1.0 - squash))
    back_grad = lax.dot_general(
        rows_c, down_tile, (((1,), (1,)), ((), ())), preferred_element_type=jnp.float32
    )
    pre_grad = (back_grad * slope_val).astype(jnp.bfloat16)
    grad_up = lax.dot_general(
        rows_x, pre_grad, (((0,), (0,)), ((), ())), preferred_element_type=jnp.float32
    )
    grad_cols = lax.dot_general(
        rows_c, hidden, (((0,), (0,)), ((), ())), preferred_element_type=jnp.float32
    )
    return (grad_up, grad_cols)


def adam_step(gradient, moment_one, moment_two):
    new_one = BETA_ONE * moment_one.astype(jnp.float32) + (1.0 - BETA_ONE) * gradient
    new_two = BETA_TWO * moment_two.astype(jnp.float32) + (1.0 - BETA_TWO) * gradient * gradient
    return (new_one / (jnp.sqrt(new_two) + EPSILON)).astype(jnp.bfloat16)


def on_device(
    tokens, cotangent, gates, routes, w_up, w_down, m_up, v_up, m_down, v_down, leaving, tile_owner
):
    experts = lax.axis_size("expert")
    my_index = lax.axis_index("expert")
    tok_count, model_width = tokens.shape
    top_count = routes.shape[1]
    hidden_units = w_up.shape[2]
    capacity = 5 * tok_count * top_count // (4 * experts)
    pair_count = tok_count * top_count
    leaver = leaving[0]
    slot_ids = jnp.arange(experts, dtype=jnp.int32)
    tile_rows = model_width // experts
    adopt = jnp.sum(
        jnp.where(tile_owner[None, :] == slot_ids[:, None], slot_ids[None, :], 0), axis=1
    )
    expert_of = routes.reshape(pair_count)
    member = (expert_of[:, None] == slot_ids[None, :]).astype(jnp.int32)
    slot_rank = jnp.sum((jnp.cumsum(member, axis=0) - 1) * member, axis=1)
    slot_place = expert_of * capacity + slot_rank
    staying = expert_of != leaver
    send_mask = jnp.ones_like(staying)
    pair_x = jnp.repeat(tokens, top_count, axis=0)
    pair_c = (
        gates.reshape(pair_count)[:, None]
        * jnp.repeat(cotangent, top_count, axis=0).astype(jnp.float32)
    ).astype(jnp.bfloat16)
    pair_both = jnp.concatenate([pair_x, pair_c], axis=1)
    targets = jnp.arange(experts * capacity, dtype=jnp.int32)
    picker = ((slot_place[None, :] == targets[:, None]) & send_mask[None, :]).astype(jnp.bfloat16)
    send_both = jnp.dot(picker, pair_both, preferred_element_type=jnp.float32).astype(jnp.bfloat16)
    send_x = send_both[:, :model_width].reshape(experts, capacity, model_width)
    send_c = send_both[:, model_width:].reshape(experts, capacity, model_width)
    recv_x, recv_c = (
        lax.all_to_all(send_x, "expert", split_axis=0, concat_axis=0, tiled=True),
        lax.all_to_all(send_c, "expert", split_axis=0, concat_axis=0, tiled=True),
    )
    recv_x = recv_x.reshape(experts * capacity, model_width)
    recv_c = recv_c.reshape(experts * capacity, model_width)
    grad_up, grad_cols = expert_terms(
        lax.all_gather(recv_x, "dp", axis=0, tiled=True),
        lax.all_gather(recv_c, "dp", axis=0, tiled=True),
        w_up[0],
        w_down[0],
    )
    keep_own = my_index != leaver
    step_up = adam_step(grad_up, m_up[0], v_up[0])
    step_down = adam_step(grad_cols.T, m_down[0], v_down[0])
    both_steps = jnp.concatenate([step_up, step_down.T], axis=1).reshape(
        experts, tile_rows, 2 * hidden_units
    )
    ordered = both_steps[adopt]
    outgoing = jnp.where(keep_own, jnp.zeros_like(ordered), ordered)
    incoming = lax.all_to_all(outgoing, "expert", split_axis=0, concat_axis=0, tiled=True)
    mine = lax.dynamic_index_in_dim(incoming, leaver, 0, keepdims=False)
    adopted_up = mine[:, :hidden_units][None]
    adopted_down = mine[:, hidden_units:][None]
    update_up = jnp.where(keep_own, step_up, jnp.zeros_like(step_up))[None]
    update_down = jnp.where(keep_own, step_down, jnp.zeros_like(step_down))[None]
    return (update_up, update_down, adopted_up, adopted_down)


def solution(mesh):
    placed = (
        P(("dp", "expert"), None),
        P(("dp", "expert"), None),
        P(("dp", "expert"), None),
        P(("dp", "expert"), None),
        P("expert", None, "dp"),
        P("expert", "dp", None),
        P("expert", None, "dp"),
        P("expert", None, "dp"),
        P("expert", "dp", None),
        P("expert", "dp", None),
        P(),
        P(),
    )
    return jax.shard_map(
        on_device,
        mesh=mesh,
        in_specs=placed,
        out_specs=(
            P("expert", None, "dp"),
            P("expert", "dp", None),
            P("expert", None, "dp"),
            P("expert", None, "dp"),
        ),
        check_vma=False,
    )
```

profile of v0, /device:TPU:33, one launch (start us, length us, event | category | flops | bytes accessed | tf_op | source)
XLA Modules:
  0.0 402.2 jit_solution(538637933655754063)
XLA Ops:
  7.2 0.0 copy-start
  7.2 0.0 copy-start.7
  7.2 0.0 all-gather.3.cloned.1.call-start
  7.2 0.9 fusion.19
  8.1 0.2 reduce_window_sum.11
  8.3 0.8 select_reduce_fusion
  9.1 0.7 multiply_add_fusion
  9.8 1.4 multiply_convert_fusion
  11.2 0.0 copy-done.7
  11.2 0.7 convolution_convert_fusion
  11.9 1.5 fusion.25
  13.5 1.5 reshape.61
  15.0 61.8 %all_to_all.15 = bf16[32,5,3584]{2,1,0:T(8,128)(2,1)} all-to-all(bf16[32,5,3584]{2,1,0:T(8,128)(2,1)S(1)} %reshape.61), channel_id=1, replica_groups=mesh['dp'=8,'expert'=32] {'expert'}, dimensions={0} | all-to-all | bytes 2293760 | tf_op jit(solution)/shard_map/all_to_all | solution.py:69
  76.8 2.5 reshape.62
  79.3 0.0 all-gather.3.cloned.1.call-update
  79.3 0.0 all-gather.5.cloned.1.call-start
  79.4 1.5 reshape.63
  80.9 62.4 %all_to_all.16 = bf16[32,5,3584]{2,1,0:T(8,128)(2,1)} all-to-all(bf16[32,5,3584]{2,1,0:T(8,128)(2,1)S(1)} %reshape.63), channel_id=1, replica_groups=mesh['dp'=8,'expert'=32] {'expert'}, dimensions={0} | all-to-all | bytes 2293760 | tf_op jit(solution)/shard_map/all_to_all | solution.py:70
  143.4 2.6 reshape.64
  146.0 0.0 all-gather.5.cloned.1.call-update
  146.7 0.0 copy-done.2
  146.7 0.0 copy-start.9
  146.7 1.3 copy.24
  148.0 0.0 copy-done.3
  148.0 1.3 copy.25
  149.3 0.0 copy-done.9
  149.3 0.1 select_reduce_fusion.1
  149.4 52.1 %all-gather.3.cloned.1.call-done = bf16[1280,3584]{1,0:T(8,128)(2,1)} async-done(((bf16[160,3584]{1,0:T(8,128)(2,1)}), bf16[1280,3584]{1,0:T(8,128)(2,1)}) %all-gather.3.cloned.1.call-update) | async-done | bytes 9175056 | tf_op jit(solution)/shard_map/all_gather | solution.py:75
  201.5 0.0 copy-done.8
  201.5 6.2 %fusion.14 = f32[1280,128]{1,0:T(8,128)S(1)} fusion(bf16[1280,3584]{1,0:T(8,128)(2,1)} %all-gather.3.cloned.1.call-done, bf16[1,3584,128]{2,1,0:T(8,128)(2,1)S(1)} %copy-done.8), kind=kOutput, calls=%fused_computation.24 | convolution fusion | flops 1174405120 | bytes 10747904 | tf_op jit(solution)/shard_map/dot_general | solution.py:12
  207.7 0.0 copy-start.5
  207.7 0.0 copy-start.6
  207.7 96.3 %all-gather.5.cloned.1.call-done = bf16[1280,3584]{1,0:T(8,128)(2,1)} async-done(((bf16[160,3584]{1,0:T(8,128)(2,1)}), bf16[1280,3584]{1,0:T(8,128)(2,1)}) %all-gather.5.cloned.1.call-update) | async-done | bytes 9175056 | tf_op jit(solution)/shard_map/all_gather | solution.py:76
  304.0 7.4 %fusion.12 = bf16[128,3584]{1,0:T(8,128)(2,1)} fusion(bf16[1,128,3584]{2,1,0:T(8,128)(2,1)} %param.21, bf16[1,128,3584]{2,1,0:T(8,128)(2,1)} %param.20, bf16[1280,3584]{1,0:T(8,128)(2,1)} %all-gather.5.cloned.1.call-done, f32[1280,128]{1,0:T(8,128)S(1)} %fusion.14), kind=kOutput, calls=%fused_computation.21 | convolution fusion | flops 1180729344 | bytes 12582912 | tf_op jit(solution)/shard_map/dot_general | solution.py:23
  311.4 0.0 copy-done.6
  311.4 14.3 %select_bitcast_fusion.1 = (bf16[1,3584,128]{1,2,0:T(8,128)(2,1)}, bf16[3584,128]{0,1:T(8,128)(2,1)}) fusion(pred[]{:T(512)S(6)} %ne.3, bf16[1,3584,128]{1,2,0:T(8,128)(2,1)S(1)} %copy-done.6, bf16[1,3584,128]{1,2,0:T(8,128)(2,1)S(1)} %copy-done.5, bf16[1280,3584]{1,0:T(8,128)(2,1)} %all-gather.3.cloned.1.call-done, ...), kind=kOutput, calls=%fused_computation.28 | convolution fusion | flops 2356248576 | bytes 23592960 | tf_op jit(solution)/shard_map/dot_general | solution.py:20
  325.7 1.6 pad_maximum_fusion
  327.3 2.3 copy.26
  329.6 2.2 gather_fusion
  331.7 1.4 broadcast_select_fusion
  333.1 10.5 %all-to-all-start.2 = ((bf16[32,112,256]{2,1,0:T(8,128)(2,1)}), bf16[32,112,256]{2,1,0:T(8,128)(2,1)}, u32[]{:S(2)}, u32[]{:S(2)}) async-start(bf16[32,112,256]{2,1,0:T(8,128)(2,1)} %broadcast_select_fusion), calls=%async_computation.2 | async-start | bytes 3670016 | tf_op jit(solution)/shard_map/all_to_all | solution.py:88
  343.6 0.0 copy-done.4
  343.6 1.3 copy.27
  344.9 0.0 copy-done.1
  344.9 1.0 select_bitcast_fusion
  345.9 48.0 %all-to-all-done.2 = bf16[32,112,256]{2,1,0:T(8,128)(2,1)} async-done(((bf16[32,112,256]{2,1,0:T(8,128)(2,1)}), bf16[32,112,256]{2,1,0:T(8,128)(2,1)}, u32[]{:S(2)}, u32[]{:S(2)}) %all-to-all-start.2) | async-done | bytes 1835040 | tf_op jit(solution)/shard_map/all_to_all | solution.py:88
  393.9 0.8 dynamic-slice_bitcast_fusion
  394.7 0.6 slice_bitcast_fusion
  (9 shorter events, 0.0 us)
Async XLA Ops:
  7.2 304.2 %copy-start = (bf16[1,128,3584]{2,1,0:T(8,128)(2,1)S(1)}, bf16[1,128,3584]{2,1,0:T(8,128)(2,1)}, u32[]{:S(2)}) copy-start(bf16[1,128,3584]{2,1,0:T(8,128)(2,1)} %param.17) | copy-start | bytes 2752516
  7.2 4.0 copy-start.7
  7.2 194.3 %all-gather.3.cloned.1.call-start = ((), (), s32[]{:S(2)}) async-start(), calls=%async_computation.3 | async-start | bytes 10321920 | tf_op jit(solution)/shard_map/all_gather | solution.py:75
  79.3 224.6 %all-gather.5.cloned.1.call-start = ((), (), s32[]{:S(2)}) async-start(), calls=%async_computation.4 | async-start | bytes 10321920 | tf_op jit(solution)/shard_map/all_gather | solution.py:76
  143.3 3.4 copy-start.2
  146.0 2.1 copy-start.3
  146.7 2.6 copy-start.9
  148.0 53.5 %copy-start.8 = (bf16[1,3584,128]{2,1,0:T(8,128)(2,1)S(1)}, bf16[1,3584,128]{2,1,0:T(8,128)(2,1)}, u32[]{:S(2)}) copy-start(bf16[1,3584,128]{2,1,0:T(8,128)(2,1)} %param.16) | copy-start | bytes 2752516
  207.7 103.7 %copy-start.5 = (bf16[1,3584,128]{1,2,0:T(8,128)(2,1)S(1)}, bf16[1,3584,128]{1,2,0:T(8,128)(2,1)}, u32[]{:S(2)}) copy-start(bf16[1,3584,128]{1,2,0:T(8,128)(2,1)} %copy.24) | copy-start | bytes 2752516
  207.7 103.7 %copy-start.6 = (bf16[1,3584,128]{1,2,0:T(8,128)(2,1)S(1)}, bf16[1,3584,128]{1,2,0:T(8,128)(2,1)}, u32[]{:S(2)}) copy-start(bf16[1,3584,128]{1,2,0:T(8,128)(2,1)} %copy.25) | copy-start | bytes 2752516
  333.1 10.5 %copy-start.4 = (bf16[1,3584,128]{1,2,0:T(8,128)(2,1)S(1)}, bf16[1,3584,128]{1,2,0:T(8,128)(2,1)}, u32[]{:S(2)}) copy-start(bf16[1,3584,128]{1,2,0:T(8,128)(2,1)} %get-tuple-element.16) | copy-start | bytes 2752516
  333.1 60.8 %all-to-all-start.2 = ((bf16[32,112,256]{2,1,0:T(8,128)(2,1)}), bf16[32,112,256]{2,1,0:T(8,128)(2,1)}, u32[]{:S(2)}, u32[]{:S(2)}) async-start(bf16[32,112,256]{2,1,0:T(8,128)(2,1)} %broadcast_select_fusion), calls=%async_computation.2 | async-start | bytes 3670016 | tf_op jit(solution)/shard_map/all_to_all | solution.py:88
  343.6 1.3 copy-start.1
Sparse Core Ops, SparseCore 0:
  79.5 122.0 all-gather.2
  203.3 100.6 all-gather.4
where the time goes:
time: 403 us; the launch traced here: 402 us
  waiting for transfers between devices  196 us (49%)
  blocking collectives  124 us (31%)
  matrix products  28.6 us (7%)
  local copies, waits for them, and re-layouts  19.5 us (5%)
  between operations  14.9 us (4%)
  starting transfers between devices  10.6 us (3%)
  other arithmetic  7.97 us (2%)
    all_gather x1, waiting for transfers between devices, on_device(): lax.all_gather(recv_c, 'dp', axis=0, tiled=True)  96.3 us
    all_to_all x1, blocking collectives, on_device(): lax.all_to_all(send_c, 'expert', split_axis=0, concat_axis=0, tiled=True)  62.4 us
    all_to_all x1, blocking collectives, on_device(): lax.all_to_all(send_x, 'expert', split_axis=0, concat_axis=0, tiled=True)  61.8 us
    all_gather x1, waiting for transfers between devices, on_device(): lax.all_gather(recv_x, 'dp', axis=0, tiled=True)  52.1 us
    all_to_all x1, waiting for transfers between devices, on_device(): lax.all_to_all(outgoing, 'expert', split_axis=0, concat_axis=0, tiled=True)  48 us
    dot_general x1, matrix products, expert_terms(): lax.dot_general(rows_x, pre_grad, (((0,), (0,)), ((), ())), preferred_ele...  14.3 us
    all_to_all x1, starting transfers between devices, on_device(): lax.all_to_all(outgoing, 'expert', split_axis=0, concat_axis=0, tiled=True)  10.5 us
  transfers between devices with their start and end apart: 3, of which 3 were waited for; matrix products, arithmetic and copies ran while one was open for 4% of the time, Pallas kernels for 0%

commit v1 on v0

v1 whole, which is shorter than its diff:
```python
import jax
import jax.numpy as jnp
from jax import lax
from jax.experimental import pallas as pl
from jax.experimental.pallas import tpu as pltpu
from jax.sharding import Mesh
from jax.sharding import PartitionSpec as P

BETA_ONE = 0.9
BETA_TWO = 0.95
EPSILON = 1e-08

ALL = ("zl", "co", "y", "x", "zh")
SLOT_GROUPS = ((0, 2), (2, 3))
PIECES = 4
VMEM = pl.BlockSpec(memory_space=pltpu.VMEM)
SMEM = pl.BlockSpec(memory_space=pltpu.SMEM)
LIMIT = 60 * 1024 * 1024


def device_id(z, core, y, x):
    return (((z % 4) * 2 + core) * 4 + y) * 8 + x * 2 + z // 4


def every():
    for z in range(8):
        for core in range(2):
            for y in range(4):
                for x in range(4):
                    yield z, core, y, x


def stream_pairs(places):
    pairs = []
    for z, core, y, x in every():
        place = z % 4 if core == 0 else 3 - z % 4
        if place in places:
            there = (z + (1 if core == 0 else -1)) % 8
            pairs.append((device_id(z, core, y, x), device_id(there, core, y, x)))
    return pairs


def swap_pairs():
    return [(device_id(z, c, y, x), device_id(z, 1 - c, y, x)) for z, c, y, x in every()]


def across_pairs():
    return [(device_id(z, c, y, x), device_id((z + 4) % 8, c, y, x)) for z, c, y, x in every()]


def over(value, divisor):
    if divisor & (divisor - 1) == 0:
        return value >> (divisor.bit_length() - 1)
    return (value * (-(-(1 << 18) // divisor))) >> 18


def prepare(base, tokens, cotangent, gates_row, routes_row, outs_slots):
    tok_count, width = tokens.shape
    piece = width // PIECES
    parts = 2 * PIECES

    def body(base_ref, x_ref, c_ref, g_ref, r_ref, *rest):
        outs, (held,) = rest[:-1], rest[-1:]
        routes = jnp.broadcast_to(r_ref[...], (tok_count, tok_count))
        routes_down = routes.T
        gate_down = jnp.broadcast_to(g_ref[...], (tok_count, tok_count)).T
        at_row = lax.broadcasted_iota(jnp.int32, (tok_count, tok_count), 0)
        at_col = lax.broadcasted_iota(jnp.int32, (tok_count, tok_count), 1)
        before = jnp.where((routes_down == routes) & (at_row < at_col), 1, 0)
        rank = jnp.sum(before, axis=0, keepdims=True)
        code = r_ref[...] * 8 + rank
        for q in range(PIECES):
            held[q * tok_count : (q + 1) * tok_count, :] = x_ref[:, q * piece : (q + 1) * piece]
            for j in range(piece // 128):
                cols = c_ref[:, q * piece + j * 128 : q * piece + (j + 1) * 128]
                held[
                    (PIECES + q) * tok_count : (PIECES + q + 1) * tok_count,
                    j * 128 : (j + 1) * 128,
                ] = (gate_down * cols.astype(jnp.float32)).astype(jnp.bfloat16)
        for out, (first, slots) in zip(outs, outs_slots):
            rows = 32 * parts * slots
            row = lax.broadcasted_iota(jnp.int32, (rows, tok_count), 0)
            group = over(row, slots)
            slot = row - group * slots
            part = group & (parts - 1)
            dest = group >> 3
            expert = ((dest & 15) << 1) | (base_ref[0] ^ (dest >> 4))
            hit = (expert * 8 + (slot + first)) == code
            picker = jnp.concatenate(
                [
                    jnp.where(hit & (part == q), 1.0, 0.0).astype(jnp.bfloat16)
                    for q in range(parts)
                ],
                axis=1,
            )
            out[...] = jnp.dot(
                picker, held[...], preferred_element_type=jnp.float32
            ).astype(jnp.bfloat16)

    return pl.pallas_call(
        body,
        out_shape=[
            jax.ShapeDtypeStruct((32 * parts * slots, piece), jnp.bfloat16)
            for _, slots in outs_slots
        ],
        in_specs=[SMEM, VMEM, VMEM, VMEM, VMEM],
        out_specs=[VMEM] * len(outs_slots),
        scratch_shapes=[pltpu.VMEM((parts * tok_count, piece), jnp.bfloat16)],
        compiler_params=pltpu.CompilerParams(vmem_limit_bytes=LIMIT),
        name="prepare",
    )(base, tokens, cotangent, gates_row, routes_row)


def sorter(slots):
    rows = 16 * 8 * slots
    row = lax.broadcasted_iota(jnp.int32, (rows, rows), 0)
    col = lax.broadcasted_iota(jnp.int32, (rows, rows), 1)
    part = over(row, 16 * slots)
    rest = row - part * (16 * slots)
    sender = over(rest, slots)
    slot = rest - sender * slots
    return jnp.where(col == sender * (8 * slots) + part * slots + slot, 1.0, 0.0).astype(
        jnp.bfloat16
    )


def absorb(place, blocks, w_up, w_down, sums):
    arrays = []
    for _, _, first, second in blocks:
        arrays.append(first)
        if second is not None:
            arrays.append(second)
    width, hidden_units = w_up.shape
    piece = width // PIECES
    total = sum(32 * slots for slots, _, _, _ in blocks)
    have = sums is not None

    def body(place_ref, *refs):
        ins, refs = list(refs[: len(arrays)]), refs[len(arrays) :]
        up_ref, down_ref = refs[:2]
        refs = refs[2:]
        if have:
            old_up, old_down = refs[:2]
            refs = refs[2:]
        out_up, out_down, held = refs
        at = place_ref[0]
        sorters = {}
        offset = 0
        for slots, test, _, second in blocks:
            if slots not in sorters:
                sorters[slots] = sorter(slots)
            first_ref = ins.pop(0)
            second_ref = ins.pop(0) if second is not None else None
            rows, count = 16 * 8 * slots, 16 * slots
            for half in range(2):
                span = slice(half * rows, (half + 1) * rows)
                block = first_ref[span, :]
                if second_ref is not None:
                    block = jnp.where(test(at), block, second_ref[span, :])
                ordered = jnp.dot(sorters[slots], block, preferred_element_type=jnp.float32)
                for q in range(2 * PIECES):
                    part = ordered[q * count : (q + 1) * count, :]
                    if second_ref is None and test is not None and q >= PIECES:
                        part = jnp.where(test(at), part, 0.0)
                    held[q, offset : offset + count, :] = part.astype(jnp.bfloat16)
                offset += count
        preact = sum(
            jnp.dot(
                held[q],
                up_ref[q * piece : (q + 1) * piece, :],
                preferred_element_type=jnp.float32,
            )
            for q in range(PIECES)
        )
        back_grad = sum(
            lax.dot_general(
                held[PIECES + q],
                down_ref[:, q * piece : (q + 1) * piece],
                (((1,), (1,)), ((), ())),
                preferred_element_type=jnp.float32,
            )
            for q in range(PIECES)
        )
        squash = jax.nn.sigmoid(preact)
        hidden = (preact * squash).astype(jnp.bfloat16)
        slope = squash * (1.0 + preact * (1.0 - squash))
        pre_grad = (back_grad * slope).astype(jnp.bfloat16)
        for q in range(PIECES):
            span = slice(q * piece, (q + 1) * piece)
            for left, right, old, out in (
                (pre_grad, held[q], old_up if have else None, out_up),
                (hidden, held[PIECES + q], old_down if have else None, out_down),
            ):
                part = lax.dot_general(
                    left, right, (((0,), (0,)), ((), ())), preferred_element_type=jnp.float32
                )
                out[:, span] = part + old[:, span] if have else part

    shape = jax.ShapeDtypeStruct((hidden_units, width), jnp.float32)
    args = [place, *arrays, w_up, w_down] + (list(sums) if have else [])
    flops = 8 * total * width * hidden_units
    return pl.pallas_call(
        body,
        out_shape=[shape, shape],
        in_specs=[SMEM] + [VMEM] * (len(args) - 1),
        out_specs=[VMEM, VMEM],
        scratch_shapes=[pltpu.VMEM((2 * PIECES, total, piece), jnp.bfloat16)],
        input_output_aliases={len(args) - 2: 0, len(args) - 1: 1} if have else {},
        compiler_params=pltpu.CompilerParams(vmem_limit_bytes=LIMIT),
        cost_estimate=pl.CostEstimate(
            flops=flops, transcendentals=0, bytes_accessed=16 * total * width
        ),
        name="absorb",
    )(*args)


def adam_step(gradient, moment_one, moment_two):
    new_one = BETA_ONE * moment_one.astype(jnp.float32) + (1.0 - BETA_ONE) * gradient
    new_two = BETA_TWO * moment_two.astype(jnp.float32) + (1.0 - BETA_TWO) * gradient * gradient
    return new_one / (jnp.sqrt(new_two) + EPSILON)


def finish(my_index, leaving, tile_owner, sums, m_up, v_up, m_down, v_down):
    width, hidden_units = m_up.shape
    tiles = tile_owner.shape[0]
    tile_rows = width // tiles

    def body(me, leave, owner, gu, gd, mu, vu, md, vd, out_up, out_down, out_tiles, both):
        keep = me[0] != leave[0]
        for j in range(width // 128):
            span = slice(j * 128, (j + 1) * 128)
            step_up = adam_step(gu[:, span].T, mu[span, :], vu[span, :])
            both[span, :hidden_units] = step_up.astype(jnp.bfloat16)
            out_up[span, :] = jnp.where(keep, step_up, 0.0).astype(jnp.bfloat16)
            step_down = adam_step(gd[:, span], md[:, span], vd[:, span])
            both[span, hidden_units:] = step_down.T.astype(jnp.bfloat16)
            out_down[:, span] = jnp.where(keep, step_down, 0.0).astype(jnp.bfloat16)
        for t in range(tiles):
            out_tiles[owner[t]] = both[t * tile_rows : (t + 1) * tile_rows, :]

    return pl.pallas_call(
        body,
        out_shape=[
            jax.ShapeDtypeStruct((width, hidden_units), jnp.bfloat16),
            jax.ShapeDtypeStruct((hidden_units, width), jnp.bfloat16),
            jax.ShapeDtypeStruct((tiles, tile_rows, 2 * hidden_units), jnp.bfloat16),
        ],
        in_specs=[SMEM, SMEM, SMEM] + [VMEM] * 6,
        out_specs=[VMEM] * 3,
        scratch_shapes=[pltpu.VMEM((width, 2 * hidden_units), jnp.bfloat16)],
        compiler_params=pltpu.CompilerParams(vmem_limit_bytes=LIMIT),
        name="finish",
    )(my_index, leaving, tile_owner, *sums, m_up, v_up, m_down, v_down)


def on_device(
    tokens, cotangent, gates, routes, w_up, w_down, m_up, v_up, m_down, v_down, leaving, tile_owner
):
    tok_count, width = tokens.shape
    piece = width // PIECES
    core = lax.axis_index("co")
    low = lax.axis_index("zl")
    half = lax.axis_index("zh")
    column = lax.axis_index(("y", "x"))
    place = jnp.where(core == 0, low, 3 - low)
    base = jnp.where(low <= 1, half, 1 - half)
    place_ref = place.reshape(1)

    outgoing = prepare(
        base.reshape(1),
        tokens,
        cotangent,
        gates.reshape(1, tok_count),
        routes.reshape(1, tok_count),
        SLOT_GROUPS,
    )

    def step(value, places):
        return lax.ppermute(value, ALL, stream_pairs(places))

    def swap(value):
        return lax.ppermute(value, ALL, swap_pairs())

    chunks = []
    for (_, slots), sent in zip(SLOT_GROUPS, outgoing):
        rows = sent.shape[0]
        first = lax.all_to_all(
            sent.reshape(32, rows // 32, piece), ("co", "y", "x"), 0, 0, tiled=True
        ).reshape(rows, piece)
        chunks.append({"slots": slots, 0: first})
    for ch in chunks:
        ch["s0"] = swap(ch[0])
        ch[1] = step(ch[0], (0, 1, 2, 3))
    for ch in chunks:
        ch[2] = step(jnp.where(place == 2, ch["s0"], ch[1]), (0, 1, 2, 3))
        ch["s1"] = swap(ch[1])
    for ch in chunks:
        ch[3] = step(jnp.where(place == 2, ch[1], ch[2]), (0, 1, 2))
        ch["s2"] = swap(ch[2])
    for ch in chunks:
        ch[4] = step(jnp.where(place == 2, ch[2], ch[3]), (1, 2))
        ch["s3"] = swap(ch[3])
    for ch in chunks:
        ch[5] = step(ch[3], (2,))
        ch["s4"] = swap(ch[4])
    for ch in chunks:
        ch[6] = step(ch[4], (2,))
        ch["s5"] = swap(ch[5])
    for ch in chunks:
        ch["s6"] = swap(ch[6])

    groups = [
        [(lambda at: at <= 1, 0, "s0"), (lambda at: at < 3, 1, None), (lambda at: at > 0, "s1", None)],
        [(None, 2, None), (None, "s2", None)],
        [(None, 3, None), (None, "s3", None), (lambda at: at >= 2, 4, "s4")],
        [(lambda at: at == 3, 5, "s5")],
        [(lambda at: at == 3, 6, "s6")],
    ]
    sums = None
    for group in groups:
        blocks = [
            (ch["slots"], test, ch[a], None if b is None else ch[b])
            for ch in chunks
            for test, a, b in group
        ]
        sums = absorb(place_ref, blocks, w_up[0], w_down[0], sums)

    my_index = (column * 2 + half).reshape(1)
    update_up, update_down, tiles = finish(
        my_index, leaving, tile_owner, sums, m_up[0], v_up[0], m_down[0], v_down[0]
    )
    units = w_up.shape[2]
    tile_rows = tiles.shape[1]
    incoming = lax.all_to_all(
        tiles.reshape(16, 2, tile_rows, 2 * units), ("y", "x"), 0, 0, tiled=True
    )
    leaver = leaving[0]
    pair = lax.dynamic_index_in_dim(incoming, leaver // 2, 0, keepdims=False)
    own = lax.dynamic_index_in_dim(pair, half, 0, keepdims=False)
    other = lax.dynamic_index_in_dim(pair, 1 - half, 0, keepdims=False)
    mine = jnp.where(half == leaver % 2, own, lax.ppermute(other, ALL, across_pairs()))
    return (update_up[None], update_down[None], mine[None, :, :units], mine[None, :, units:])


def solution(mesh):
    wide = Mesh(mesh.devices.reshape(4, 2, 4, 4, 2), ALL)
    dp = ("zl", "co")
    expert = ("y", "x", "zh")
    row = P(dp + expert, None)
    up = P(expert, None, dp)
    down = P(expert, dp, None)
    return jax.shard_map(
        on_device,
        mesh=wide,
        in_specs=(row, row, row, row, up, down, up, up, down, down, P(), P()),
        out_specs=(up, down, up, up),
        check_vma=False,
    )
```

time: 403 us -> 317 us (0.79)
  the two profiles are of different devices: /device:TPU:33 before, /device:TPU:96 now
where the time goes in v1:
time: 317 us; the launch traced here: 313 us
  waiting for transfers between devices  164 us (52%)
  Pallas kernels  75.5 us (24%)
  starting transfers between devices  36.6 us (12%)
  blocking collectives  28.4 us (9%)
  local copies, waits for them, and re-layouts  4.55 us (1%)
    ppermute x12, waiting for transfers between devices, step(): return lax.ppermute(value, ALL, stream_pairs(places))  130 us
    pallas_call x5, Pallas kernels, absorb(): pl.pallas_call(body, out_shape=[shape, shape], in_specs=[SMEM] + [VMEM] *...  61.9 us
    all_to_all x1, waiting for transfers between devices, on_device(): lax.all_to_all(tiles.reshape(16, 2, tile_rows, 2 * units), ('y', 'x'), 0,...  29.1 us
    all_to_all x1, blocking collectives, on_device(): lax.all_to_all(sent.reshape(32, rows // 32, piece), ('co', 'y', 'x'), 0,...  28.4 us
    ppermute x12, starting transfers between devices, step(): return lax.ppermute(value, ALL, stream_pairs(places))  22 us
    pallas_call x1, Pallas kernels, finish(): pl.pallas_call(body, out_shape=[jax.ShapeDtypeStruct((width, hidden_units...  7.96 us
  transfers between devices with their start and end apart: 29, of which 13 were waited for; matrix products, arithmetic and copies ran while one was open for 1% of the time, Pallas kernels for 17%

profile of v1, /device:TPU:96, one launch (start us, length us, event | category | flops | bytes accessed | tf_op | source)
XLA Modules:
  0.0 312.6 jit_solution(13477671417687184825)
XLA Ops:
  0.6 5.6 %prepare.1 = (bf16[512,896]{1,0:T(8,128)(2,1)}, bf16[768,896]{1,0:T(8,128)(2,1)}) custom-call(s32[1]{0:T(128)} %bitcast.2.base_ref, bf16[128,3584]{1,0:T(8,128)(2,1)} %x_ref.1, bf16[128,3584]{1,0:T(8,128)(2,1)} %c_ref.1, f32[1,128]{1,0:T(1,128)} %bitcast.51, s32[1,128]{1,0:T(1,128)} %bitcast.52), custom_call_target="tpu_custom_call" | custom-call | tf_op jit(solution)/shard_map/prepare/pallas_call | solution.py:100
  6.3 28.4 %all_to_all.15 = bf16[32,24,896]{2,1,0:T(8,128)(2,1)S(1)} all-to-all(bf16[32,24,896]{2,1,0:T(8,128)(2,1)} %bitcast.45), channel_id=1, replica_groups=mesh['zl'=4,'co'=2,'y'=4,'x'=4,'zh'=2] {'co','y','x'}, dimensions={0} | all-to-all | bytes 2752512 | tf_op jit(solution)/shard_map/all_to_all | solution.py:287
  34.7 3.1 %collective-permute-start.8 = (bf16[768,896]{1,0:T(8,128)(2,1)S(1)}, bf16[768,896]{1,0:T(8,128)(2,1)S(1)}, u32[]{:S(2)}, u32[]{:S(2)}) collective-permute-start(bf16[768,896]{1,0:T(8,128)(2,1)S(1)} %bitcast.41), channel_id=1, source_target_pairs={{0,64},{2,66},{4,68},{6,70},{8,72},{10,74},{12,76},{14,78},{16,80}... | collective-permute-start | bytes 4128776 | tf_op jit(solution)/shard_map/ppermute | solution.py:279
  37.8 4.6 %all-to-all-start = ((bf16[32,16,896]{2,1,0:T(8,128)(2,1)}), bf16[32,16,896]{2,1,0:T(8,128)(2,1)}, u32[]{:S(2)}, u32[]{:S(2)}) async-start(bf16[32,16,896]{2,1,0:T(8,128)(2,1)} %bitcast.46), calls=%async_computation | async-start | bytes 1835008 | tf_op jit(solution)/shard_map/all_to_all | solution.py:287
  42.5 11.2 %collective-permute-done.8.refs_6_ = bf16[768,896]{1,0:T(8,128)(2,1)S(1)} collective-permute-done((bf16[768,896]{1,0:T(8,128)(2,1)S(1)}, bf16[768,896]{1,0:T(8,128)(2,1)S(1)}, u32[]{:S(2)}, u32[]{:S(2)}) %collective-permute-start.8) | collective-permute-done | bytes 1376288 | tf_op jit(solution)/shard_map/ppermute | solution.py:279
  53.6 1.3 broadcast_select_fusion.2
  55.0 3.7 %collective-permute-start.9 = (bf16[768,896]{1,0:T(8,128)(2,1)}, bf16[768,896]{1,0:T(8,128)(2,1)S(1)}, u32[]{:S(2)}, u32[]{:S(2)}) collective-permute-start(bf16[768,896]{1,0:T(8,128)(2,1)} %broadcast_select_fusion.2), channel_id=1, source_target_pairs={{0,64},{2,66},{4,68},{6,70},{8,72},{10,74},{12,76},{14,78},{16,80}... | collective-permute-start | bytes 4128776 | tf_op jit(solution)/shard_map/ppermute | solution.py:279
  58.7 0.1 all-to-all-done
  58.8 1.0 collective-permute-start.1
  59.8 24.8 %collective-permute-done.1.refs_2_ = bf16[512,896]{1,0:T(8,128)(2,1)S(1)} collective-permute-done((bf16[512,896]{1,0:T(8,128)(2,1)}, bf16[512,896]{1,0:T(8,128)(2,1)S(1)}, u32[]{:S(2)}, u32[]{:S(2)}) %collective-permute-start.1) | collective-permute-done | bytes 917536 | tf_op jit(solution)/shard_map/ppermute | solution.py:279
  84.8 0.8 copy-done.7
  85.6 3.6 %collective-permute-start.2 = (bf16[512,896]{1,0:T(8,128)(2,1)S(1)}, bf16[512,896]{1,0:T(8,128)(2,1)S(1)}, u32[]{:S(2)}, u32[]{:S(2)}) collective-permute-start(bf16[512,896]{1,0:T(8,128)(2,1)S(1)} %broadcast_select_fusion.5), channel_id=1, source_target_pairs={{0,64},{2,66},{4,68},{6,70},{8,72},{10,74},{12,76},{14,78},{16,80}... | collective-permute-start | bytes 2752520 | tf_op jit(solution)/shard_map/ppermute | solution.py:279
  89.2 0.1 broadcast_select_fusion.1
  89.4 1.3 collective-permute-start.10
  90.7 9.5 %collective-permute-done.2.refs_0_ = bf16[512,896]{1,0:T(8,128)(2,1)S(1)} collective-permute-done((bf16[512,896]{1,0:T(8,128)(2,1)S(1)}, bf16[512,896]{1,0:T(8,128)(2,1)S(1)}, u32[]{:S(2)}, u32[]{:S(2)}) %collective-permute-start.2) | collective-permute-done | bytes 917536 | tf_op jit(solution)/shard_map/ppermute | solution.py:279
  100.2 1.3 collective-permute-start.3
  101.6 0.5 collective-permute-start.24
  102.2 11.5 %collective-permute-done.10.refs_4_ = bf16[768,896]{1,0:T(8,128)(2,1)S(1)} collective-permute-done((bf16[768,896]{1,0:T(8,128)(2,1)S(1)}, bf16[768,896]{1,0:T(8,128)(2,1)S(1)}, u32[]{:S(2)}, u32[]{:S(2)}) %collective-permute-start.10) | collective-permute-done | bytes 1376288 | tf_op jit(solution)/shard_map/ppermute | solution.py:279
  113.8 0.2 broadcast_select_fusion
  114.0 1.3 collective-permute-start.11
  115.3 8.3 %collective-permute-done.3.refs_0_ = bf16[512,896]{1,0:T(8,128)(2,1)S(1)} collective-permute-done((bf16[512,896]{1,0:T(8,128)(2,1)S(1)}, bf16[512,896]{1,0:T(8,128)(2,1)S(1)}, u32[]{:S(2)}, u32[]{:S(2)}) %collective-permute-start.3) | collective-permute-done | bytes 917536 | tf_op jit(solution)/shard_map/ppermute | solution.py:279
  123.7 1.3 collective-permute-start.4
  125.2 0.6 collective-permute-start.23
  125.7 1.5 collective-permute-start.14
  127.3 20.9 %collective-permute-done.4.refs_2_ = bf16[512,896]{1,0:T(8,128)(2,1)S(1)} collective-permute-done((bf16[512,896]{1,0:T(8,128)(2,1)S(1)}, bf16[512,896]{1,0:T(8,128)(2,1)S(1)}, u32[]{:S(2)}, u32[]{:S(2)}) %collective-permute-start.4) | collective-permute-done | bytes 917536 | tf_op jit(solution)/shard_map/ppermute | solution.py:279
  148.2 1.3 collective-permute-start.16
  149.5 1.3 collective-permute-start.12
  150.9 0.8 copy-done.15
  151.7 6.4 %collective-permute-done.14.refs_0_ = bf16[512,896]{1,0:T(8,128)(2,1)} collective-permute-done((bf16[512,896]{1,0:T(8,128)(2,1)S(1)}, bf16[512,896]{1,0:T(8,128)(2,1)}, u32[]{:S(2)}, u32[]{:S(2)}) %collective-permute-start.14) | collective-permute-done | bytes 917536 | tf_op jit(solution)/shard_map/ppermute | solution.py:279
  158.1 1.3 collective-permute-start.5
  159.5 0.8 collective-permute-start.21
  160.2 12.6 %collective-permute-done.16.refs_2_ = bf16[768,896]{1,0:T(8,128)(2,1)} collective-permute-done((bf16[768,896]{1,0:T(8,128)(2,1)S(1)}, bf16[768,896]{1,0:T(8,128)(2,1)}, u32[]{:S(2)}, u32[]{:S(2)}) %collective-permute-start.16) | collective-permute-done | bytes 1376288 | tf_op jit(solution)/shard_map/ppermute | solution.py:279
  172.9 14.6 %collective-permute-done.12.refs_2_ = bf16[768,896]{1,0:T(8,128)(2,1)S(1)} collective-permute-done((bf16[768,896]{1,0:T(8,128)(2,1)}, bf16[768,896]{1,0:T(8,128)(2,1)S(1)}, u32[]{:S(2)}, u32[]{:S(2)}) %collective-permute-start.12) | collective-permute-done | bytes 1376288 | tf_op jit(solution)/shard_map/ppermute | solution.py:279
  187.5 9.9 %collective-permute-done.5.refs_0_ = bf16[512,896]{1,0:T(8,128)(2,1)} collective-permute-done((bf16[512,896]{1,0:T(8,128)(2,1)S(1)}, bf16[512,896]{1,0:T(8,128)(2,1)}, u32[]{:S(2)}, u32[]{:S(2)}) %collective-permute-start.5) | collective-permute-done | bytes 917536 | tf_op jit(solution)/shard_map/ppermute | solution.py:279
  197.5 1.1 copy-done.12
  198.6 0.5 collective-permute-start.6
  199.7 12.2 %absorb.5 = (f32[128,3584]{1,0:T(8,128)}, f32[128,3584]{1,0:T(8,128)}) custom-call(s32[1]{0:T(128)} %bitcast.1.place_ref, bf16[512,896]{1,0:T(8,128)(2,1)} %bitcast.6.refs_0_, bf16[512,896]{1,0:T(8,128)(2,1)} %copy-done.7, bf16[512,896]{1,0:T(8,128)(2,1)} %copy-done.3, bf16[512,896]{1,0:T(8,128)(2,1)} %copy-done.17, bf16[768,896]{1,0:T(8,128)(2,1)} %bitcast.43, ...), custom_call_target="tpu_custom_call" | custom-call | flops 1761607680 | bytes 27525120 | tf_op jit(solution)/shard_map/absorb/pallas_call | solution.py:202
  211.9 10.4 %absorb.6 = (f32[128,3584]{1,0:T(8,128)}, f32[128,3584]{1,0:T(8,128)}) custom-call(s32[1]{0:T(128)} %bitcast.1.place_ref, bf16[512,896]{1,0:T(8,128)(2,1)} %copy-done.2, bf16[512,896]{1,0:T(8,128)(2,1)} %copy-done.13, bf16[768,896]{1,0:T(8,128)(2,1)} %copy-done, bf16[768,896]{1,0:T(8,128)(2,1)} %copy-done.9, ...), custom_call_target="tpu_custom_call", output_to_operand_aliasing={{0}: (7, {}), {1}: (8, {})} | custom-call | flops 1174405120 | bytes 18350080 | tf_op jit(solution)/shard_map/absorb/pallas_call | solution.py:202
  222.3 22.7 %absorb.7 = (f32[128,3584]{1,0:T(8,128)}, f32[128,3584]{1,0:T(8,128)}) custom-call(s32[1]{0:T(128)} %bitcast.1.place_ref, bf16[512,896]{1,0:T(8,128)(2,1)} %copy-done.6, bf16[512,896]{1,0:T(8,128)(2,1)} %copy-done.15, bf16[512,896]{1,0:T(8,128)(2,1)} %copy-done.14, bf16[512,896]{1,0:T(8,128)(2,1)} %copy-done.16, ...), custom_call_target="tpu_custom_call", output_to_operand_aliasing={{0}: (11, {}), {1}: (12, {})} | custom-call | flops 1761607680 | bytes 27525120 | tf_op jit(solution)/shard_map/absorb/pallas_call | solution.py:202
  245.0 8.3 %absorb.8 = (f32[128,3584]{1,0:T(8,128)}, f32[128,3584]{1,0:T(8,128)}) custom-call(s32[1]{0:T(128)} %bitcast.1.place_ref, bf16[512,896]{1,0:T(8,128)(2,1)} %collective-permute-done.14.refs_0_, bf16[512,896]{1,0:T(8,128)(2,1)} %collective-permute-done.15.refs_1_, ...), custom_call_target="tpu_custom_call", output_to_operand_aliasing={{0}: (7, {}), {1}: (8, {})} | custom-call | flops 587202560 | bytes 9175040 | tf_op jit(solution)/shard_map/absorb/pallas_call | solution.py:202
  253.3 1.1 copy-done.10
  254.5 8.3 %absorb.9 = (f32[128,3584]{1,0:T(8,128)}, f32[128,3584]{1,0:T(8,128)}) custom-call(s32[1]{0:T(128)} %bitcast.1.place_ref, bf16[512,896]{1,0:T(8,128)(2,1)} %collective-permute-done.5.refs_0_, bf16[512,896]{1,0:T(8,128)(2,1)} %collective-permute-done.6.refs_1_, bf16[768,896]{1,0:T(8,128)(2,1)} %copy-done.8, ...), custom_call_target="tpu_custom_call", output_to_operand_aliasing={{0}: (7, {}), {1}: (8, {})} | custom-call | flops 587202560 | bytes 9175040 | tf_op jit(solution)/shard_map/absorb/pallas_call | solution.py:202
  262.8 8.0 %finish.1 = (bf16[3584,128]{1,0:T(8,128)(2,1)}, bf16[128,3584]{1,0:T(8,128)(2,1)}, bf16[32,112,256]{2,1,0:T(8,128)(2,1)}) custom-call(s32[1]{0:T(128)} %bitcast.me, s32[1]{0:T(128)} %copy.32.leave, s32[32]{0:T(128)} %owner.1, f32[128,3584]{1,0:T(8,128)} %get-tuple-element.29.gu, f32[128,3584]{1,0:T(8,128)} %get-tuple-element.30.gd, ...), custom_call_target="tpu_custom_call" | custom-call | tf_op jit(solution)/shard_map/finish/pallas_call | solution.py:241
  270.7 3.7 %all-to-all-start.2 = ((bf16[16,2,112,256]{3,2,1,0:T(8,128)(2,1)}), bf16[16,2,112,256]{3,2,1,0:T(8,128)(2,1)S(1)}, u32[]{:S(2)}, u32[]{:S(2)}) async-start(bf16[16,2,112,256]{3,2,1,0:T(8,128)(2,1)} %bitcast.44), calls=%async_computation.2 | async-start | bytes 3670016 | tf_op jit(solution)/shard_map/all_to_all | solution.py:334
  274.5 29.1 %all-to-all-done.2 = bf16[16,2,112,256]{3,2,1,0:T(8,128)(2,1)S(1)} async-done(((bf16[16,2,112,256]{3,2,1,0:T(8,128)(2,1)}), bf16[16,2,112,256]{3,2,1,0:T(8,128)(2,1)S(1)}, u32[]{:S(2)}, u32[]{:S(2)}) %all-to-all-start.2) | async-done | bytes 1835040 | tf_op jit(solution)/shard_map/all_to_all | solution.py:334
  303.6 3.5 %collective-permute-start.26 = (bf16[112,256]{1,0:T(8,128)(2,1)S(1)}, bf16[112,256]{1,0:T(8,128)(2,1)S(1)}, u32[]{:S(2)}, u32[]{:S(2)}) collective-permute-start(bf16[112,256]{1,0:T(8,128)(2,1)S(1)} %dynamic-slice_bitcast_fusion), channel_id=1, source_target_pairs={{0,1},{2,3},{4,5},{6,7},{8,9},{10,11},{12,13},{14,15},{16,17},{18,... | collective-permute-start | bytes 172040 | tf_op jit(solution)/shard_map/ppermute | solution.py:341
  307.2 4.6 %collective-permute-done.26 = bf16[112,256]{1,0:T(8,128)(2,1)S(1)} collective-permute-done((bf16[112,256]{1,0:T(8,128)(2,1)S(1)}, bf16[112,256]{1,0:T(8,128)(2,1)S(1)}, u32[]{:S(2)}, u32[]{:S(2)}) %collective-permute-start.26) | collective-permute-done | bytes 57376 | tf_op jit(solution)/shard_map/ppermute | solution.py:341
  311.7 0.6 slice_bitcast_fusion
  (63 shorter events, 0.8 us)
Async XLA Ops:
  34.7 19.0 %copy-start.4 = (bf16[32,24,896]{2,1,0:T(8,128)(2,1)}, bf16[32,24,896]{2,1,0:T(8,128)(2,1)S(1)}, u32[]{:S(2)}) copy-start(bf16[32,24,896]{2,1,0:T(8,128)(2,1)S(1)} %all_to_all.15) | copy-start | bytes 4128772
  34.7 19.0 %collective-permute-start.8 = (bf16[768,896]{1,0:T(8,128)(2,1)S(1)}, bf16[768,896]{1,0:T(8,128)(2,1)S(1)}, u32[]{:S(2)}, u32[]{:S(2)}) collective-permute-start(bf16[768,896]{1,0:T(8,128)(2,1)S(1)} %bitcast.41), channel_id=1, source_target_pairs={{0,64},{2,66},{4,68},{6,70},{8,72},{10,74},{12,76},{14,78},{16,80}... | collective-permute-start | bytes 4128776 | tf_op jit(solution)/shard_map/ppermute | solution.py:279
  37.8 15.8 %collective-permute-start.7 = (bf16[768,896]{1,0:T(8,128)(2,1)S(1)}, bf16[768,896]{1,0:T(8,128)(2,1)}, u32[]{:S(2)}, u32[]{:S(2)}) collective-permute-start(bf16[768,896]{1,0:T(8,128)(2,1)S(1)} %bitcast.42), channel_id=1, source_target_pairs={{0,32},{2,34},{4,36},{6,38},{8,40},{10,42},{12,44},{14,46},{16,48}... | collective-permute-start | bytes 4128776 | tf_op jit(solution)/shard_map/ppermute | solution.py:282
  37.8 21.0 %all-to-all-start = ((bf16[32,16,896]{2,1,0:T(8,128)(2,1)}), bf16[32,16,896]{2,1,0:T(8,128)(2,1)}, u32[]{:S(2)}, u32[]{:S(2)}) async-start(bf16[32,16,896]{2,1,0:T(8,128)(2,1)} %bitcast.46), calls=%async_computation | async-start | bytes 1835008 | tf_op jit(solution)/shard_map/all_to_all | solution.py:287
  53.6 47.9 %copy-start.1 = (bf16[768,896]{1,0:T(8,128)(2,1)}, bf16[768,896]{1,0:T(8,128)(2,1)S(1)}, u32[]{:S(2)}) copy-start(bf16[768,896]{1,0:T(8,128)(2,1)S(1)} %collective-permute-done.8.refs_6_) | copy-start | bytes 4128772
  55.0 34.2 %collective-permute-start.9 = (bf16[768,896]{1,0:T(8,128)(2,1)}, bf16[768,896]{1,0:T(8,128)(2,1)S(1)}, u32[]{:S(2)}, u32[]{:S(2)}) collective-permute-start(bf16[768,896]{1,0:T(8,128)(2,1)} %broadcast_select_fusion.2), channel_id=1, source_target_pairs={{0,64},{2,66},{4,68},{6,70},{8,72},{10,74},{12,76},{14,78},{16,80}... | collective-permute-start | bytes 4128776 | tf_op jit(solution)/shard_map/ppermute | solution.py:279
  58.8 25.9 %collective-permute-start.1 = (bf16[512,896]{1,0:T(8,128)(2,1)}, bf16[512,896]{1,0:T(8,128)(2,1)S(1)}, u32[]{:S(2)}, u32[]{:S(2)}) collective-permute-start(bf16[512,896]{1,0:T(8,128)(2,1)} %bitcast.6.refs_0_), channel_id=1, source_target_pairs={{0,64},{2,66},{4,68},{6,70},{8,72},{10,74},{12,76},{14,78},{16,80}... | collective-permute-start | bytes 2752520 | tf_op jit(solution)/shard_map/ppermute | solution.py:279
  59.8 24.9 %collective-permute-start = (bf16[512,896]{1,0:T(8,128)(2,1)}, bf16[512,896]{1,0:T(8,128)(2,1)S(1)}, u32[]{:S(2)}, u32[]{:S(2)}) collective-permute-start(bf16[512,896]{1,0:T(8,128)(2,1)} %bitcast.6.refs_0_), channel_id=1, source_target_pairs={{0,32},{2,34},{4,36},{6,38},{8,40},{10,42},{12,44},{14,46},{16,48}... | collective-permute-start | bytes 2752520 | tf_op jit(solution)/shard_map/ppermute | solution.py:282
  84.7 17.0 %copy-start.3 = (bf16[512,896]{1,0:T(8,128)(2,1)}, bf16[512,896]{1,0:T(8,128)(2,1)S(1)}, u32[]{:S(2)}) copy-start(bf16[512,896]{1,0:T(8,128)(2,1)S(1)} %collective-permute-done.1.refs_2_) | copy-start | bytes 2752516
  84.7 1.0 copy-start.7
  85.6 14.5 %collective-permute-start.2 = (bf16[512,896]{1,0:T(8,128)(2,1)S(1)}, bf16[512,896]{1,0:T(8,128)(2,1)S(1)}, u32[]{:S(2)}, u32[]{:S(2)}) collective-permute-start(bf16[512,896]{1,0:T(8,128)(2,1)S(1)} %broadcast_select_fusion.5), channel_id=1, source_target_pairs={{0,64},{2,66},{4,68},{6,70},{8,72},{10,74},{12,76},{14,78},{16,80}... | collective-permute-start | bytes 2752520 | tf_op jit(solution)/shard_map/ppermute | solution.py:279
  89.2 35.9 %copy-start = (bf16[768,896]{1,0:T(8,128)(2,1)}, bf16[768,896]{1,0:T(8,128)(2,1)S(1)}, u32[]{:S(2)}) copy-start(bf16[768,896]{1,0:T(8,128)(2,1)S(1)} %collective-permute-done.9.refs_2_) | copy-start | bytes 4128772
  89.4 24.4 %collective-permute-start.10 = (bf16[768,896]{1,0:T(8,128)(2,1)S(1)}, bf16[768,896]{1,0:T(8,128)(2,1)S(1)}, u32[]{:S(2)}, u32[]{:S(2)}) collective-permute-start(bf16[768,896]{1,0:T(8,128)(2,1)S(1)} %broadcast_select_fusion.1), channel_id=1, source_target_pairs={{0,64},{2,66},{4,68},{6,70},{8,72},{10,74},{12,76},{14,78},{16,80}... | collective-permute-start | bytes 4128776 | tf_op jit(solution)/shard_map/ppermute | solution.py:279
  100.1 23.5 %copy-start.2 = (bf16[512,896]{1,0:T(8,128)(2,1)}, bf16[512,896]{1,0:T(8,128)(2,1)S(1)}, u32[]{:S(2)}) copy-start(bf16[512,896]{1,0:T(8,128)(2,1)S(1)} %collective-permute-done.2.refs_0_) | copy-start | bytes 2752516
  100.2 23.4 %collective-permute-start.3 = (bf16[512,896]{1,0:T(8,128)(2,1)S(1)}, bf16[512,896]{1,0:T(8,128)(2,1)S(1)}, u32[]{:S(2)}, u32[]{:S(2)}) collective-permute-start(bf16[512,896]{1,0:T(8,128)(2,1)S(1)} %broadcast_select_fusion.4), channel_id=1, source_target_pairs={{0,64},{2,66},{4,68},{6,70},{8,72},{10,74},{12,76},{14,78},{16,80}... | collective-permute-start | bytes 2752520 | tf_op jit(solution)/shard_map/ppermute | solution.py:279
  101.5 24.2 %collective-permute-start.25 = (bf16[768,896]{1,0:T(8,128)(2,1)S(1)}, bf16[768,896]{1,0:T(8,128)(2,1)S(1)}, u32[]{:S(2)}, u32[]{:S(2)}) collective-permute-start(bf16[768,896]{1,0:T(8,128)(2,1)S(1)} %collective-permute-done.8.refs_6_), channel_id=1, source_target_pairs={{0,32},{2,34},{4,36},{6,38},{8,40},{10,42},{12,44},{14,46},{16,48}... | collective-permute-start | bytes 4128776 | tf_op jit(solution)/shard_map/ppermute | solution.py:282
  101.6 23.4 %collective-permute-start.24 = (bf16[512,896]{1,0:T(8,128)(2,1)S(1)}, bf16[512,896]{1,0:T(8,128)(2,1)S(1)}, u32[]{:S(2)}, u32[]{:S(2)}) collective-permute-start(bf16[512,896]{1,0:T(8,128)(2,1)S(1)} %collective-permute-done.1.refs_2_), channel_id=1, source_target_pairs={{0,32},{2,34},{4,36},{6,38},{8,40},{10,42},{12,44},{14,46},{16,48}... | collective-permute-start | bytes 2752520 | tf_op jit(solution)/shard_map/ppermute | solution.py:282
  102.1 23.0 %collective-permute-start.22 = (bf16[512,896]{1,0:T(8,128)(2,1)S(1)}, bf16[512,896]{1,0:T(8,128)(2,1)S(1)}, u32[]{:S(2)}, u32[]{:S(2)}) collective-permute-start(bf16[512,896]{1,0:T(8,128)(2,1)S(1)} %collective-permute-done.2.refs_0_), channel_id=1, source_target_pairs={{0,32},{2,34},{4,36},{6,38},{8,40},{10,42},{12,44},{14,46},{16,48}... | collective-permute-start | bytes 2752520 | tf_op jit(solution)/shard_map/ppermute | solution.py:282
  113.8 44.3 %copy-start.5 = (bf16[768,896]{1,0:T(8,128)(2,1)}, bf16[768,896]{1,0:T(8,128)(2,1)S(1)}, u32[]{:S(2)}) copy-start(bf16[768,896]{1,0:T(8,128)(2,1)S(1)} %collective-permute-done.10.refs_4_) | copy-start | bytes 4128772
  114.0 35.5 %collective-permute-start.11 = (bf16[768,896]{1,0:T(8,128)(2,1)S(1)}, bf16[768,896]{1,0:T(8,128)(2,1)}, u32[]{:S(2)}, u32[]{:S(2)}) collective-permute-start(bf16[768,896]{1,0:T(8,128)(2,1)S(1)} %broadcast_select_fusion), channel_id=1, source_target_pairs={{64,128},{66,130},{68,132},{70,134},{72,136},{74,138},{76,140},{78... | collective-permute-start | bytes 4128776 | tf_op jit(solution)/shard_map/ppermute | solution.py:279
  123.6 2.1 copy-start.6
  123.7 24.5 %collective-permute-start.4 = (bf16[512,896]{1,0:T(8,128)(2,1)S(1)}, bf16[512,896]{1,0:T(8,128)(2,1)S(1)}, u32[]{:S(2)}, u32[]{:S(2)}) collective-permute-start(bf16[512,896]{1,0:T(8,128)(2,1)S(1)} %broadcast_select_fusion.3), channel_id=1, source_target_pairs={{64,128},{66,130},{68,132},{70,134},{72,136},{74,138},{76,140},{78... | collective-permute-start | bytes 2752520 | tf_op jit(solution)/shard_map/ppermute | solution.py:279
  125.0 72.4 %copy-start.17 = (bf16[512,896]{1,0:T(8,128)(2,1)}, bf16[512,896]{1,0:T(8,128)(2,1)S(1)}, u32[]{:S(2)}) copy-start(bf16[512,896]{1,0:T(8,128)(2,1)S(1)} %collective-permute-done.24.refs_3_) | copy-start | bytes 2752516
  125.0 25.8 %collective-permute-start.18 = (bf16[512,896]{1,0:T(8,128)(2,1)S(1)}, bf16[512,896]{1,0:T(8,128)(2,1)S(1)}, u32[]{:S(2)}, u32[]{:S(2)}) collective-permute-start(bf16[512,896]{1,0:T(8,128)(2,1)S(1)} %collective-permute-done.3.refs_0_), channel_id=1, source_target_pairs={{0,32},{2,34},{4,36},{6,38},{8,40},{10,42},{12,44},{14,46},{16,48}... | collective-permute-start | bytes 2752520 | tf_op jit(solution)/shard_map/ppermute | solution.py:282
  125.1 72.3 %copy-start.13 = (bf16[512,896]{1,0:T(8,128)(2,1)}, bf16[512,896]{1,0:T(8,128)(2,1)S(1)}, u32[]{:S(2)}) copy-start(bf16[512,896]{1,0:T(8,128)(2,1)S(1)} %collective-permute-done.22.refs_1_) | copy-start | bytes 2752516
  125.2 33.0 %collective-permute-start.23 = (bf16[768,896]{1,0:T(8,128)(2,1)S(1)}, bf16[768,896]{1,0:T(8,128)(2,1)S(1)}, u32[]{:S(2)}, u32[]{:S(2)}) collective-permute-start(bf16[768,896]{1,0:T(8,128)(2,1)S(1)} %collective-permute-done.9.refs_2_), channel_id=1, source_target_pairs={{0,32},{2,34},{4,36},{6,38},{8,40},{10,42},{12,44},{14,46},{16,48}... | collective-permute-start | bytes 4128776 | tf_op jit(solution)/shard_map/ppermute | solution.py:282
  125.7 71.7 %copy-start.11 = (bf16[768,896]{1,0:T(8,128)(2,1)}, bf16[768,896]{1,0:T(8,128)(2,1)S(1)}, u32[]{:S(2)}) copy-start(bf16[768,896]{1,0:T(8,128)(2,1)S(1)} %collective-permute-done.25.refs_7_) | copy-start | bytes 4128772
  125.7 32.4 %collective-permute-start.14 = (bf16[512,896]{1,0:T(8,128)(2,1)S(1)}, bf16[512,896]{1,0:T(8,128)(2,1)}, u32[]{:S(2)}, u32[]{:S(2)}) collective-permute-start(bf16[512,896]{1,0:T(8,128)(2,1)S(1)} %collective-permute-done.3.refs_0_), channel_id=1, source_target_pairs={{96,32},{98,34},{100,36},{102,38},{104,40},{106,42},{108,44},{110,... | collective-permute-start | bytes 2752520 | tf_op jit(solution)/shard_map/ppermute | solution.py:279
  148.2 49.3 %copy-start.14 = (bf16[512,896]{1,0:T(8,128)(2,1)}, bf16[512,896]{1,0:T(8,128)(2,1)S(1)}, u32[]{:S(2)}) copy-start(bf16[512,896]{1,0:T(8,128)(2,1)S(1)} %collective-permute-done.4.refs_2_) | copy-start | bytes 2752516
  148.2 24.7 %collective-permute-start.16 = (bf16[768,896]{1,0:T(8,128)(2,1)S(1)}, bf16[768,896]{1,0:T(8,128)(2,1)}, u32[]{:S(2)}, u32[]{:S(2)}) collective-permute-start(bf16[768,896]{1,0:T(8,128)(2,1)S(1)} %collective-permute-done.10.refs_4_), channel_id=1, source_target_pairs={{96,32},{98,34},{100,36},{102,38},{104,40},{106,42},{108,44},{110,... | collective-permute-start | bytes 4128776 | tf_op jit(solution)/shard_map/ppermute | solution.py:279
  149.5 38.0 %collective-permute-start.12 = (bf16[768,896]{1,0:T(8,128)(2,1)}, bf16[768,896]{1,0:T(8,128)(2,1)S(1)}, u32[]{:S(2)}, u32[]{:S(2)}) collective-permute-start(bf16[768,896]{1,0:T(8,128)(2,1)} %collective-permute-done.11.refs_6_), channel_id=1, source_target_pairs={{96,32},{98,34},{100,36},{102,38},{104,40},{106,42},{108,44},{110,... | collective-permute-start | bytes 4128776 | tf_op jit(solution)/shard_map/ppermute | solution.py:279
  150.8 0.9 copy-start.15
  150.8 8.6 %collective-permute-start.19 = (bf16[512,896]{1,0:T(8,128)(2,1)S(1)}, bf16[512,896]{1,0:T(8,128)(2,1)S(1)}, u32[]{:S(2)}, u32[]{:S(2)}) collective-permute-start(bf16[512,896]{1,0:T(8,128)(2,1)S(1)} %collective-permute-done.4.refs_2_), channel_id=1, source_target_pairs={{0,32},{2,34},{4,36},{6,38},{8,40},{10,42},{12,44},{14,46},{16,48}... | collective-permute-start | bytes 2752520 | tf_op jit(solution)/shard_map/ppermute | solution.py:282
  158.1 39.3 %collective-permute-start.20 = (bf16[768,896]{1,0:T(8,128)(2,1)S(1)}, bf16[768,896]{1,0:T(8,128)(2,1)S(1)}, u32[]{:S(2)}, u32[]{:S(2)}) collective-permute-start(bf16[768,896]{1,0:T(8,128)(2,1)S(1)} %collective-permute-done.10.refs_4_), channel_id=1, source_target_pairs={{0,32},{2,34},{4,36},{6,38},{8,40},{10,42},{12,44},{14,46},{16,48}... | collective-permute-start | bytes 4128776 | tf_op jit(solution)/shard_map/ppermute | solution.py:282
  158.1 39.4 %copy-start.9 = (bf16[768,896]{1,0:T(8,128)(2,1)}, bf16[768,896]{1,0:T(8,128)(2,1)S(1)}, u32[]{:S(2)}) copy-start(bf16[768,896]{1,0:T(8,128)(2,1)S(1)} %collective-permute-done.23.refs_3_) | copy-start | bytes 4128772
  158.1 39.3 %collective-permute-start.5 = (bf16[512,896]{1,0:T(8,128)(2,1)S(1)}, bf16[512,896]{1,0:T(8,128)(2,1)}, u32[]{:S(2)}, u32[]{:S(2)}) collective-permute-start(bf16[512,896]{1,0:T(8,128)(2,1)S(1)} %collective-permute-done.4.refs_2_), channel_id=1, source_target_pairs={{96,32},{98,34},{100,36},{102,38},{104,40},{106,42},{108,44},{110,... | collective-permute-start | bytes 2752520 | tf_op jit(solution)/shard_map/ppermute | solution.py:279
  159.4 38.0 %copy-start.16 = (bf16[512,896]{1,0:T(8,128)(2,1)}, bf16[512,896]{1,0:T(8,128)(2,1)S(1)}, u32[]{:S(2)}) copy-start(bf16[512,896]{1,0:T(8,128)(2,1)S(1)} %collective-permute-done.19.refs_3_) | copy-start | bytes 2752516
  159.5 62.9 %collective-permute-start.21 = (bf16[768,896]{1,0:T(8,128)(2,1)}, bf16[768,896]{1,0:T(8,128)(2,1)}, u32[]{:S(2)}, u32[]{:S(2)}) collective-permute-start(bf16[768,896]{1,0:T(8,128)(2,1)} %collective-permute-done.11.refs_6_), channel_id=1, source_target_pairs={{0,32},{2,34},{4,36},{6,38},{8,40},{10,42},{12,44},{14,46},{16,48}... | collective-permute-start | bytes 4128776 | tf_op jit(solution)/shard_map/ppermute | solution.py:282
  172.9 72.1 %collective-permute-start.17 = (bf16[768,896]{1,0:T(8,128)(2,1)}, bf16[768,896]{1,0:T(8,128)(2,1)}, u32[]{:S(2)}, u32[]{:S(2)}) collective-permute-start(bf16[768,896]{1,0:T(8,128)(2,1)} %collective-permute-done.16.refs_2_), channel_id=1, source_target_pairs={{0,32},{2,34},{4,36},{6,38},{8,40},{10,42},{12,44},{14,46},{16,48}... | collective-permute-start | bytes 4128776 | tf_op jit(solution)/shard_map/ppermute | solution.py:282
  187.5 24.4 %copy-start.8 = (bf16[768,896]{1,0:T(8,128)(2,1)}, bf16[768,896]{1,0:T(8,128)(2,1)S(1)}, u32[]{:S(2)}) copy-start(bf16[768,896]{1,0:T(8,128)(2,1)S(1)} %collective-permute-done.12.refs_2_) | copy-start | bytes 4128772
  187.5 65.8 %collective-permute-start.13 = (bf16[768,896]{1,0:T(8,128)(2,1)S(1)}, bf16[768,896]{1,0:T(8,128)(2,1)S(1)}, u32[]{:S(2)}, u32[]{:S(2)}) collective-permute-start(bf16[768,896]{1,0:T(8,128)(2,1)S(1)} %collective-permute-done.12.refs_2_), channel_id=1, source_target_pairs={{0,32},{2,34},{4,36},{6,38},{8,40},{10,42},{12,44},{14,46},{16,48}... | collective-permute-start | bytes 4128776 | tf_op jit(solution)/shard_map/ppermute | solution.py:282
  197.4 47.6 %collective-permute-start.15 = (bf16[512,896]{1,0:T(8,128)(2,1)}, bf16[512,896]{1,0:T(8,128)(2,1)}, u32[]{:S(2)}, u32[]{:S(2)}) collective-permute-start(bf16[512,896]{1,0:T(8,128)(2,1)} %collective-permute-done.14.refs_0_), channel_id=1, source_target_pairs={{0,32},{2,34},{4,36},{6,38},{8,40},{10,42},{12,44},{14,46},{16,48}... | collective-permute-start | bytes 2752520 | tf_op jit(solution)/shard_map/ppermute | solution.py:282
  197.5 1.1 copy-start.12
  198.6 54.7 %collective-permute-start.6 = (bf16[512,896]{1,0:T(8,128)(2,1)}, bf16[512,896]{1,0:T(8,128)(2,1)}, u32[]{:S(2)}, u32[]{:S(2)}) collective-permute-start(bf16[512,896]{1,0:T(8,128)(2,1)} %collective-permute-done.5.refs_0_), channel_id=1, source_target_pairs={{0,32},{2,34},{4,36},{6,38},{8,40},{10,42},{12,44},{14,46},{16,48}... | collective-permute-start | bytes 2752520 | tf_op jit(solution)/shard_map/ppermute | solution.py:282
  253.3 1.1 copy-start.10
  270.7 32.9 %all-to-all-start.2 = ((bf16[16,2,112,256]{3,2,1,0:T(8,128)(2,1)}), bf16[16,2,112,256]{3,2,1,0:T(8,128)(2,1)S(1)}, u32[]{:S(2)}, u32[]{:S(2)}) async-start(bf16[16,2,112,256]{3,2,1,0:T(8,128)(2,1)} %bitcast.44), calls=%async_computation.2 | async-start | bytes 3670016 | tf_op jit(solution)/shard_map/all_to_all | solution.py:334
  303.6 8.1 %collective-permute-start.26 = (bf16[112,256]{1,0:T(8,128)(2,1)S(1)}, bf16[112,256]{1,0:T(8,128)(2,1)S(1)}, u32[]{:S(2)}, u32[]{:S(2)}) collective-permute-start(bf16[112,256]{1,0:T(8,128)(2,1)S(1)} %dynamic-slice_bitcast_fusion), channel_id=1, source_target_pairs={{0,1},{2,3},{4,5},{6,7},{8,9},{10,11},{12,13},{14,15},{16,17},{18,... | collective-permute-start | bytes 172040 | tf_op jit(solution)/shard_map/ppermute | solution.py:341

commit v2 on v1

v2 whole, which is shorter than its diff:
```python
import jax
import jax.numpy as jnp
from jax import lax
from jax.experimental import pallas as pl
from jax.experimental.pallas import tpu as pltpu
from jax.sharding import Mesh
from jax.sharding import PartitionSpec as P


BETA_ONE = 0.9
BETA_TWO = 0.95
EPSILON = 1e-08

ALL = ("zl", "co", "y", "x", "zh")
SLOT_GROUPS = ((0, 2), (2, 3))
TAGS = ("a", "b")
SUMS = ("ao1p2q3r", "a45 bo1p", "b2q", "b3r4 a6", "b5")
LAST = "b6"
PIECES = 4
VMEM = pl.BlockSpec(memory_space=pltpu.VMEM)
SMEM = pl.BlockSpec(memory_space=pltpu.SMEM)
LIMIT = 60 * 1024 * 1024


def device_id(z, core, y, x):
    return (((z % 4) * 2 + core) * 4 + y) * 8 + x * 2 + z // 4


def every():
    for z in range(8):
        for core in range(2):
            for y in range(4):
                for x in range(4):
                    yield z, core, y, x


def stream_pairs(places):
    pairs = []
    for z, core, y, x in every():
        place = z % 4 if core == 0 else 3 - z % 4
        if place in places:
            there = (z + (1 if core == 0 else -1)) % 8
            pairs.append((device_id(z, core, y, x), device_id(there, core, y, x)))
    return pairs


def swap_pairs():
    return [(device_id(z, c, y, x), device_id(z, 1 - c, y, x)) for z, c, y, x in every()]


def across_pairs():
    return [(device_id(z, c, y, x), device_id((z + 4) % 8, c, y, x)) for z, c, y, x in every()]


def over(value, divisor):
    if divisor & (divisor - 1) == 0:
        return value >> (divisor.bit_length() - 1)
    return (value * (-(-(1 << 18) // divisor))) >> 18


def prepare(base, tokens, cotangent, gates_row, routes_row, outs_slots):
    tok_count, width = tokens.shape
    piece = width // PIECES
    parts = 2 * PIECES

    def body(base_ref, x_ref, c_ref, g_ref, r_ref, *rest):
        outs, (held,) = rest[:-1], rest[-1:]
        routes = jnp.broadcast_to(r_ref[...], (tok_count, tok_count))
        routes_down = routes.T
        gate_down = jnp.broadcast_to(g_ref[...], (tok_count, tok_count)).T
        at_row = lax.broadcasted_iota(jnp.int32, (tok_count, tok_count), 0)
        at_col = lax.broadcasted_iota(jnp.int32, (tok_count, tok_count), 1)
        before = jnp.where((routes_down == routes) & (at_row < at_col), 1, 0)
        rank = jnp.sum(before, axis=0, keepdims=True)
        code = r_ref[...] * 8 + rank
        for q in range(PIECES):
            held[q * tok_count : (q + 1) * tok_count, :] = x_ref[:, q * piece : (q + 1) * piece]
            for j in range(piece // 128):
                cols = c_ref[:, q * piece + j * 128 : q * piece + (j + 1) * 128]
                held[
                    (PIECES + q) * tok_count : (PIECES + q + 1) * tok_count,
                    j * 128 : (j + 1) * 128,
                ] = (gate_down * cols.astype(jnp.float32)).astype(jnp.bfloat16)
        for out, (first, slots) in zip(outs, outs_slots):
            rows = 32 * parts * slots
            row = lax.broadcasted_iota(jnp.int32, (rows, tok_count), 0)
            group = over(row, slots)
            slot = row - group * slots
            part = group & (parts - 1)
            dest = group >> 3
            expert = ((dest & 15) << 1) | (base_ref[0] ^ (dest >> 4))
            hit = (expert * 8 + (slot + first)) == code
            picker = jnp.concatenate(
                [
                    jnp.where(hit & (part == q), 1.0, 0.0).astype(jnp.bfloat16)
                    for q in range(parts)
                ],
                axis=1,
            )
            out[...] = jnp.dot(
                picker, held[...], preferred_element_type=jnp.float32
            ).astype(jnp.bfloat16)

    return pl.pallas_call(
        body,
        out_shape=[
            jax.ShapeDtypeStruct((32 * parts * slots, piece), jnp.bfloat16)
            for _, slots in outs_slots
        ],
        in_specs=[SMEM, VMEM, VMEM, VMEM, VMEM],
        out_specs=[VMEM] * len(outs_slots),
        scratch_shapes=[pltpu.VMEM((parts * tok_count, piece), jnp.bfloat16)],
        compiler_params=pltpu.CompilerParams(vmem_limit_bytes=LIMIT),
        name="prepare",
    )(base, tokens, cotangent, gates_row, routes_row)


def sorter(slots):
    rows = 16 * 8 * slots
    row = lax.broadcasted_iota(jnp.int32, (rows, rows), 0)
    col = lax.broadcasted_iota(jnp.int32, (rows, rows), 1)
    part = over(row, 16 * slots)
    rest = row - part * (16 * slots)
    sender = over(rest, slots)
    slot = rest - sender * slots
    return jnp.where(col == sender * (8 * slots) + part * slots + slot, 1.0, 0.0).astype(
        jnp.bfloat16
    )


def arrange(received, slots):
    _, piece = received.shape
    count = 16 * slots

    def body(in_ref, out_ref):
        order = sorter(slots)
        for half in range(2):
            block = in_ref[half * 8 * count : (half + 1) * 8 * count, :]
            ordered = jnp.dot(order, block, preferred_element_type=jnp.float32)
            ordered = ordered.astype(jnp.bfloat16)
            for q in range(2 * PIECES):
                out_ref[q, half * count : (half + 1) * count, :] = ordered[
                    q * count : (q + 1) * count, :
                ]

    return pl.pallas_call(
        body,
        out_shape=jax.ShapeDtypeStruct((2 * PIECES, 2 * count, piece), jnp.bfloat16),
        in_specs=[VMEM],
        out_specs=VMEM,
        compiler_params=pltpu.CompilerParams(vmem_limit_bytes=LIMIT),
        name="arrange",
    )(received)


def flatten(blocks):
    arrays = []
    for _, first, second in blocks:
        arrays.append(first)
        if second is not None:
            arrays.append(second)
    return arrays


def gather_rows(at, blocks, refs, held_x, held_c):
    refs = list(refs)
    piece = refs[0].shape[2]
    offset = 0
    for test, _, second in blocks:
        first_ref = refs.pop(0)
        second_ref = refs.pop(0) if second is not None else None
        count = first_ref.shape[1]
        for q in range(2 * PIECES):
            part = first_ref[q]
            if second_ref is not None:
                part = jnp.where(test(at), part, second_ref[q])
            elif test is not None and q >= PIECES:
                part = jnp.where(test(at), part, jnp.zeros_like(part))
            held = held_x if q < PIECES else held_c
            left = (q % PIECES) * piece
            held[offset : offset + count, left : left + piece] = part
        offset += count


def row_terms(up_ref, down_ref, held_x, held_c, held_pre, held_hid, tile):
    def rows_of(i, carry):
        span = pl.ds(pl.multiple_of(i * tile, tile), tile)
        preact = jnp.dot(held_x[span, :], up_ref[...], preferred_element_type=jnp.float32)
        back_grad = lax.dot_general(
            held_c[span, :],
            down_ref[...],
            (((1,), (1,)), ((), ())),
            preferred_element_type=jnp.float32,
        )
        squash = jax.nn.sigmoid(preact)
        held_hid[span, :] = (preact * squash).astype(jnp.bfloat16)
        slope = squash * (1.0 + preact * (1.0 - squash))
        held_pre[span, :] = (back_grad * slope).astype(jnp.bfloat16)
        return carry

    lax.fori_loop(0, held_x.shape[0] // tile, rows_of, 0)


def column_sums(left, right):
    return lax.dot_general(left, right, (((0,), (0,)), ((), ())), preferred_element_type=jnp.float32)


def absorb(place, blocks, w_up, w_down, sums):
    arrays = flatten(blocks)
    width, hidden_units = w_up.shape
    total = sum(first.shape[1] for _, first, _ in blocks)
    have = sums is not None
    step = width // 7
    tile = total // 2 if total > 128 else total

    def body(place_ref, *refs):
        ins, refs = refs[: len(arrays)], refs[len(arrays) :]
        up_ref, down_ref = refs[:2]
        refs = refs[2:]
        if have:
            old_up, old_down = refs[:2]
            refs = refs[2:]
        out_up, out_down, held_x, held_c, held_pre, held_hid = refs
        gather_rows(place_ref[0], blocks, ins, held_x, held_c)
        row_terms(up_ref, down_ref, held_x, held_c, held_pre, held_hid, tile)

        def columns(j, carry):
            span = pl.ds(pl.multiple_of(j * step, step), step)
            part_up = column_sums(held_pre[...], held_x[:, span])
            part_down = column_sums(held_hid[...], held_c[:, span])
            out_up[:, span] = part_up + old_up[:, span] if have else part_up
            out_down[:, span] = part_down + old_down[:, span] if have else part_down
            return carry

        lax.fori_loop(0, 7, columns, 0)

    shape = jax.ShapeDtypeStruct((hidden_units, width), jnp.float32)
    args = [place, *arrays, w_up, w_down] + (list(sums) if have else [])
    return pl.pallas_call(
        body,
        out_shape=[shape, shape],
        in_specs=[SMEM] + [VMEM] * (len(args) - 1),
        out_specs=[VMEM, VMEM],
        scratch_shapes=[
            pltpu.VMEM((total, width), jnp.bfloat16),
            pltpu.VMEM((total, width), jnp.bfloat16),
            pltpu.VMEM((total, hidden_units), jnp.bfloat16),
            pltpu.VMEM((total, hidden_units), jnp.bfloat16),
        ],
        input_output_aliases={len(args) - 2: 0, len(args) - 1: 1} if have else {},
        compiler_params=pltpu.CompilerParams(vmem_limit_bytes=LIMIT),
        cost_estimate=pl.CostEstimate(
            flops=8 * total * width * hidden_units,
            transcendentals=0,
            bytes_accessed=4 * total * width,
        ),
        name="absorb",
    )(*args)


def adam_step(gradient, moment_one, moment_two):
    new_one = BETA_ONE * moment_one.astype(jnp.float32) + (1.0 - BETA_ONE) * gradient
    new_two = BETA_TWO * moment_two.astype(jnp.float32) + (1.0 - BETA_TWO) * gradient * gradient
    return new_one / (jnp.sqrt(new_two) + EPSILON)


def finish_down(place, my_index, leaving, tile_owner, blocks, w_up, w_down, old, m_down, v_down):
    arrays = flatten(blocks)
    width, hidden_units = w_up.shape
    tiles = tile_owner.shape[0]
    tile_rows = width // tiles
    total = sum(first.shape[1] for _, first, _ in blocks)
    step = 256

    def body(place_ref, me, leave, owner, *refs):
        ins, refs = refs[: len(arrays)], refs[len(arrays) :]
        up_ref, down_ref, old_down, md, vd = refs[:5]
        out_down, out_tiles, out_x, out_pre, both, held_c, held_hid = refs[5:]
        keep = me[0] != leave[0]
        gather_rows(place_ref[0], blocks, ins, out_x, held_c)
        row_terms(up_ref, down_ref, out_x, held_c, out_pre, held_hid, total)

        def columns(j, carry):
            span = pl.ds(pl.multiple_of(j * step, step), step)
            grad = old_down[:, span] + column_sums(held_hid[...], held_c[:, span])
            step_down = adam_step(grad, md[:, span], vd[:, span])
            both[span, :] = step_down.T.astype(jnp.bfloat16)
            out_down[:, span] = jnp.where(keep, step_down, 0.0).astype(jnp.bfloat16)
            return carry

        lax.fori_loop(0, width // step, columns, 0)
        for t in range(tiles):
            out_tiles[owner[t]] = both[t * tile_rows : (t + 1) * tile_rows, :]

    return pl.pallas_call(
        body,
        out_shape=[
            jax.ShapeDtypeStruct((hidden_units, width), jnp.bfloat16),
            jax.ShapeDtypeStruct((tiles, tile_rows, hidden_units), jnp.bfloat16),
            jax.ShapeDtypeStruct((total, width), jnp.bfloat16),
            jax.ShapeDtypeStruct((total, hidden_units), jnp.bfloat16),
        ],
        in_specs=[SMEM] * 4 + [VMEM] * (len(arrays) + 5),
        out_specs=[VMEM] * 4,
        scratch_shapes=[
            pltpu.VMEM((width, hidden_units), jnp.bfloat16),
            pltpu.VMEM((total, width), jnp.bfloat16),
            pltpu.VMEM((total, hidden_units), jnp.bfloat16),
        ],
        compiler_params=pltpu.CompilerParams(vmem_limit_bytes=LIMIT),
        name="finish_down",
    )(place, my_index, leaving, tile_owner, *arrays, w_up, w_down, old, m_down, v_down)


def finish_up(my_index, leaving, tile_owner, rows_x, pre_grad, old, m_up, v_up):
    width, hidden_units = m_up.shape
    tiles = tile_owner.shape[0]
    tile_rows = width // tiles
    step = 256

    def body(me, leave, owner, x_ref, pre_ref, old_up, mu, vu, out_up, out_tiles, both):
        keep = me[0] != leave[0]

        def columns(j, carry):
            span = pl.ds(pl.multiple_of(j * step, step), step)
            grad = old_up[:, span] + column_sums(pre_ref[...], x_ref[:, span])
            step_up = adam_step(grad.T, mu[span, :], vu[span, :])
            both[span, :] = step_up.astype(jnp.bfloat16)
            out_up[span, :] = jnp.where(keep, step_up, 0.0).astype(jnp.bfloat16)
            return carry

        lax.fori_loop(0, width // step, columns, 0)
        for t in range(tiles):
            out_tiles[owner[t]] = both[t * tile_rows : (t + 1) * tile_rows, :]

    return pl.pallas_call(
        body,
        out_shape=[
            jax.ShapeDtypeStruct((width, hidden_units), jnp.bfloat16),
            jax.ShapeDtypeStruct((tiles, tile_rows, hidden_units), jnp.bfloat16),
        ],
        in_specs=[SMEM] * 3 + [VMEM] * 5,
        out_specs=[VMEM] * 2,
        scratch_shapes=[pltpu.VMEM((width, hidden_units), jnp.bfloat16)],
        compiler_params=pltpu.CompilerParams(vmem_limit_bytes=LIMIT),
        cost_estimate=pl.CostEstimate(
            flops=8 * 160 * width * hidden_units,
            transcendentals=0,
            bytes_accessed=12 * width * hidden_units,
        ),
        name="finish_up",
    )(my_index, leaving, tile_owner, rows_x, pre_grad, old, m_up, v_up)


def on_device(
    tokens, cotangent, gates, routes, w_up, w_down, m_up, v_up, m_down, v_down, leaving, tile_owner
):
    tok_count, width = tokens.shape
    piece = width // PIECES
    core = lax.axis_index("co")
    low = lax.axis_index("zl")
    half = lax.axis_index("zh")
    column = lax.axis_index(("y", "x"))
    place = jnp.where(core == 0, low, 3 - low)
    base = jnp.where(low <= 1, half, 1 - half)
    place_ref = place.reshape(1)

    outgoing = prepare(
        base.reshape(1),
        tokens,
        cotangent,
        gates.reshape(1, tok_count),
        routes.reshape(1, tok_count),
        SLOT_GROUPS,
    )

    def step(value, places):
        return lax.ppermute(value, ALL, stream_pairs(places))

    def swap(value):
        return lax.ppermute(value, ALL, swap_pairs())

    chunks = []
    previous = None
    for tag, (_, slots), sent in zip(TAGS, SLOT_GROUPS, outgoing):
        rows = sent.shape[0]
        if previous is not None:
            previous, sent = lax.optimization_barrier((previous, sent))
            chunks[-1][0] = previous
        previous = lax.all_to_all(
            sent.reshape(32, rows // 32, piece), ("co", "y", "x"), 0, 0, tiled=True
        ).reshape(rows, piece)
        chunks.append({"tag": tag, "slots": slots, 0: previous})
    everyone = (0, 1, 2, 3)
    for ch in chunks:
        tag = ch["tag"]
        ch[0] = arrange(ch[0], ch["slots"])
        ch[1] = step(ch[0], everyone)
        ch["s0"] = swap(ch[0])
        ch[2] = step(jnp.where(place == 2, ch["s0"], ch[1]), everyone)
        ch["s1"] = swap(ch[1])
        ch[3] = step(jnp.where(place == 2, ch[1], ch[2]), (0, 1, 2))
        ch["s2"] = swap(ch[2])
        ch[4] = step(jnp.where(place == 2, ch[2], ch[3]), (1, 2))
        ch["s3"] = swap(ch[3])
        ch[5] = step(ch[3], (2,))
        ch["s4"] = swap(ch[4])
        ch[6] = step(ch[4], (2,))
        ch["s5"] = swap(ch[5])
        ch["s6"] = swap(ch[6])

    rules = {
        "o": (lambda at: at <= 1, 0, "s0"),
        "1": (lambda at: at < 3, 1, None),
        "p": (lambda at: at > 0, "s1", None),
        "2": (None, 2, None),
        "q": (None, "s2", None),
        "3": (None, 3, None),
        "r": (None, "s3", None),
        "4": (lambda at: at >= 2, 4, "s4"),
        "5": (lambda at: at == 3, 5, "s5"),
        "6": (lambda at: at == 3, 6, "s6"),
    }

    def blocks_of(words):
        blocks = []
        for word in words.split():
            ch = chunks[TAGS.index(word[0])]
            for letter in word[1:]:
                test, one, two = rules[letter]
                blocks.append((test, ch[one], None if two is None else ch[two]))
        return blocks

    sums = None
    for words in SUMS:
        sums = absorb(place_ref, blocks_of(words), w_up[0], w_down[0], sums)
    my_index = (column * 2 + half).reshape(1)
    leaver = leaving[0]

    def adopt(tiles):
        _, rows, units = tiles.shape
        incoming = lax.all_to_all(tiles.reshape(16, 2, rows, units), ("y", "x"), 0, 0, tiled=True)
        pair = lax.dynamic_index_in_dim(incoming, leaver // 2, 0, keepdims=False)
        own = lax.dynamic_index_in_dim(pair, half, 0, keepdims=False)
        other = lax.dynamic_index_in_dim(pair, 1 - half, 0, keepdims=False)
        crossed = lax.ppermute(other, ALL, across_pairs())
        return jnp.where(half == leaver % 2, own, crossed)[None]

    update_down, tiles_down, rows_x, pre_grad = finish_down(
        place_ref,
        my_index,
        leaving,
        tile_owner,
        blocks_of(LAST),
        w_up[0],
        w_down[0],
        sums[1],
        m_down[0],
        v_down[0],
    )
    adopted_down = adopt(tiles_down)
    update_up, tiles_up = finish_up(
        my_index, leaving, tile_owner, rows_x, pre_grad, sums[0], m_up[0], v_up[0]
    )
    adopted_up = adopt(tiles_up)
    return (update_up[None], update_down[None], adopted_up, adopted_down)


def solution(mesh):
    wide = Mesh(mesh.devices.reshape(4, 2, 4, 4, 2), ALL)
    dp = ("zl", "co")
    expert = ("y", "x", "zh")
    row = P(dp + expert, None)
    up = P(expert, None, dp)
    down = P(expert, dp, None)
    return jax.shard_map(
        on_device,
        mesh=wide,
        in_specs=(row, row, row, row, up, down, up, up, down, down, P(), P()),
        out_specs=(up, down, up, up),
        check_vma=False,
    )
```

time: 317 us -> 327 us (1.032)
  the two profiles are of different devices: /device:TPU:96 before, /device:TPU:224 now
where the time goes in v2:
time: 327 us; the launch traced here: 326 us
  waiting for transfers between devices  161 us (49%)
  Pallas kernels  78.7 us (24%)
  blocking collectives  48.7 us (15%)
  starting transfers between devices  28.1 us (9%)
  other arithmetic  4.64 us (1%)
  local copies, waits for them, and re-layouts  3.58 us (1%)
    ppermute x12, waiting for transfers between devices, step(): return lax.ppermute(value, ALL, stream_pairs(places))  130 us
    pallas_call x5, Pallas kernels, absorb(): pl.pallas_call(body, out_shape=[shape, shape], in_specs=[SMEM] + [VMEM] *...  48.8 us
    all_to_all x2, blocking collectives, on_device(): lax.all_to_all(sent.reshape(32, rows // 32, piece), ('co', 'y', 'x'), 0,...  48.7 us
    all_to_all x2, waiting for transfers between devices, adopt(): lax.all_to_all(tiles.reshape(16, 2, rows, units), ('y', 'x'), 0, 0, tiled...  22.3 us
    ppermute x12, starting transfers between devices, step(): return lax.ppermute(value, ALL, stream_pairs(places))  15 us
    pallas_call x1, Pallas kernels, finish_down(): pl.pallas_call(body, out_shape=[jax.ShapeDtypeStruct((hidden_units, width...  10.3 us
    pallas_call x1, Pallas kernels, finish_up(): pl.pallas_call(body, out_shape=[jax.ShapeDtypeStruct((width, hidden_units...  8.16 us
    all_to_all x2, starting transfers between devices, adopt(): lax.all_to_all(tiles.reshape(16, 2, rows, units), ('y', 'x'), 0, 0, tiled...  7.27 us
  transfers between devices with their start and end apart: 30, of which 13 were waited for; matrix products, arithmetic and copies ran while one was open for 1% of the time, Pallas kernels for 18%

profile of v2, /device:TPU:224, one launch (start us, length us, event | category | flops | bytes accessed | tf_op | source)
XLA Modules:
  0.0 326.3 jit_solution(14731297492759175185)
XLA Ops:
  0.6 5.6 %prepare.1 = (bf16[512,896]{1,0:T(8,128)(2,1)}, bf16[768,896]{1,0:T(8,128)(2,1)}) custom-call(s32[1]{0:T(128)} %bitcast.2.base_ref, bf16[128,3584]{1,0:T(8,128)(2,1)} %x_ref.1, bf16[128,3584]{1,0:T(8,128)(2,1)} %c_ref.1, f32[1,128]{1,0:T(1,128)} %bitcast.62, s32[1,128]{1,0:T(1,128)} %bitcast.63), custom_call_target="tpu_custom_call" | custom-call | tf_op jit(solution)/shard_map/prepare/pallas_call | solution.py:104
  6.3 23.9 %all_to_all.20 = bf16[32,16,896]{2,1,0:T(8,128)(2,1)} all-to-all(bf16[32,16,896]{2,1,0:T(8,128)(2,1)} %bitcast.61), channel_id=1, replica_groups=mesh['zl'=4,'co'=2,'y'=4,'x'=4,'zh'=2] {'co','y','x'}, dimensions={0} | all-to-all | bytes 1835008 | tf_op jit(solution)/shard_map/all_to_all | solution.py:390
  30.2 24.8 %all_to_all.21 = bf16[32,24,896]{2,1,0:T(8,128)(2,1)} all-to-all(bf16[32,24,896]{2,1,0:T(8,128)(2,1)S(1)} %bitcast.54), channel_id=1, replica_groups=mesh['zl'=4,'co'=2,'y'=4,'x'=4,'zh'=2] {'co','y','x'}, dimensions={0} | all-to-all | bytes 2752512 | tf_op jit(solution)/shard_map/all_to_all | solution.py:390
  54.9 3.4 %arrange.2.refs_4_ = bf16[8,96,896]{2,1,0:T(8,128)(2,1)} custom-call(bf16[768,896]{1,0:T(8,128)(2,1)} %bitcast.52), custom_call_target="tpu_custom_call" | custom-call | tf_op jit(solution)/shard_map/arrange/pallas_call | solution.py:146
  58.3 2.5 arrange.3.refs_0_
  60.9 2.2 collective-permute-start.12
  63.1 13.7 %collective-permute-done.1.refs_6_ = bf16[8,96,896]{2,1,0:T(8,128)(2,1)S(1)} collective-permute-done((bf16[8,96,896]{2,1,0:T(8,128)(2,1)}, bf16[8,96,896]{2,1,0:T(8,128)(2,1)S(1)}, u32[]{:S(2)}, u32[]{:S(2)}) %collective-permute-start.1) | collective-permute-done | bytes 1376288 | tf_op jit(solution)/shard_map/ppermute | solution.py:378
  77.0 0.9 copy-done.3
  77.9 1.2 collective-permute-start.2
  79.1 7.6 %collective-permute-done.12.refs_2_ = bf16[8,64,896]{2,1,0:T(8,128)(2,1)} collective-permute-done((bf16[8,64,896]{2,1,0:T(8,128)(2,1)}, bf16[8,64,896]{2,1,0:T(8,128)(2,1)}, u32[]{:S(2)}, u32[]{:S(2)}) %collective-permute-start.12) | collective-permute-done | bytes 917536 | tf_op jit(solution)/shard_map/ppermute | solution.py:378
  86.8 1.3 broadcast_select_fusion.5
  88.1 1.3 collective-permute-start.13
  89.3 12.1 %collective-permute-done.2.refs_0_ = bf16[8,96,896]{2,1,0:T(8,128)(2,1)S(1)} collective-permute-done((bf16[8,96,896]{2,1,0:T(8,128)(2,1)S(1)}, bf16[8,96,896]{2,1,0:T(8,128)(2,1)S(1)}, u32[]{:S(2)}, u32[]{:S(2)}) %collective-permute-start.2) | collective-permute-done | bytes 1376288 | tf_op jit(solution)/shard_map/ppermute | solution.py:378
  101.6 1.3 collective-permute-start.3
  102.9 8.3 %collective-permute-done.13.refs_4_ = bf16[8,64,896]{2,1,0:T(8,128)(2,1)S(1)} collective-permute-done((bf16[8,64,896]{2,1,0:T(8,128)(2,1)S(1)}, bf16[8,64,896]{2,1,0:T(8,128)(2,1)S(1)}, u32[]{:S(2)}, u32[]{:S(2)}) %collective-permute-start.13) | collective-permute-done | bytes 917536 | tf_op jit(solution)/shard_map/ppermute | solution.py:378
  111.4 1.3 collective-permute-start.14
  113.3 22.5 %collective-permute-done.14.refs_6_ = bf16[8,64,896]{2,1,0:T(8,128)(2,1)S(1)} collective-permute-done((bf16[8,64,896]{2,1,0:T(8,128)(2,1)S(1)}, bf16[8,64,896]{2,1,0:T(8,128)(2,1)S(1)}, u32[]{:S(2)}, u32[]{:S(2)}) %collective-permute-start.14) | collective-permute-done | bytes 917536 | tf_op jit(solution)/shard_map/ppermute | solution.py:378
  135.9 1.3 collective-permute-start.15
  137.2 1.5 broadcast_select_fusion
  138.8 1.3 collective-permute-start.4
  140.7 1.3 collective-permute-start.20
  142.0 9.2 %collective-permute-done.15.refs_0_ = bf16[8,64,896]{2,1,0:T(8,128)(2,1)S(1)} collective-permute-done((bf16[8,64,896]{2,1,0:T(8,128)(2,1)S(1)}, bf16[8,64,896]{2,1,0:T(8,128)(2,1)S(1)}, u32[]{:S(2)}, u32[]{:S(2)}) %collective-permute-start.15) | collective-permute-done | bytes 917536 | tf_op jit(solution)/shard_map/ppermute | solution.py:378
  151.2 1.3 collective-permute-start.7
  152.5 13.5 %collective-permute-done.4.refs_2_ = bf16[8,96,896]{2,1,0:T(8,128)(2,1)} collective-permute-done((bf16[8,96,896]{2,1,0:T(8,128)(2,1)S(1)}, bf16[8,96,896]{2,1,0:T(8,128)(2,1)}, u32[]{:S(2)}, u32[]{:S(2)}) %collective-permute-start.4) | collective-permute-done | bytes 1376288 | tf_op jit(solution)/shard_map/ppermute | solution.py:378
  166.1 1.3 collective-permute-start.5
  167.4 8.4 %collective-permute-done.20.refs_2_ = bf16[8,64,896]{2,1,0:T(8,128)(2,1)S(1)} collective-permute-done((bf16[8,64,896]{2,1,0:T(8,128)(2,1)S(1)}, bf16[8,64,896]{2,1,0:T(8,128)(2,1)S(1)}, u32[]{:S(2)}, u32[]{:S(2)}) %collective-permute-start.20) | collective-permute-done | bytes 917536 | tf_op jit(solution)/shard_map/ppermute | solution.py:378
  176.3 1.3 collective-permute-start.16
  177.6 2.6 collective-permute-done.21.refs_3_
  180.4 34.8 %collective-permute-done.16.refs_4_ = bf16[8,64,896]{2,1,0:T(8,128)(2,1)} collective-permute-done((bf16[8,64,896]{2,1,0:T(8,128)(2,1)S(1)}, bf16[8,64,896]{2,1,0:T(8,128)(2,1)}, u32[]{:S(2)}, u32[]{:S(2)}) %collective-permute-start.16) | collective-permute-done | bytes 917536 | tf_op jit(solution)/shard_map/ppermute | solution.py:378
  215.2 0.5 collective-permute-start.8
  215.9 1.1 copy-done.9
  218.0 10.1 %absorb.5 = (f32[128,3584]{1,0:T(8,128)}, f32[128,3584]{1,0:T(8,128)}) custom-call(s32[1]{0:T(128)} %bitcast.1.place_ref, bf16[8,64,896]{2,1,0:T(8,128)(2,1)} %arrange.3.refs_0_, bf16[8,64,896]{2,1,0:T(8,128)(2,1)} %collective-permute-done.11.refs_1_, bf16[8,64,896]{2,1,0:T(8,128)(2,1)} %collective-permute-done.12.refs_2_, bf16[8,64,896]{2,1,0:T(8,128)(2,1)} %copy-done.10, ...), custom_call_target="tpu_custom_call" | custom-call | flops 1644167168 | bytes 6422528 | tf_op jit(solution)/shard_map/absorb/pallas_call | solution.py:239
  228.2 11.7 %absorb.6 = (f32[128,3584]{1,0:T(8,128)}, f32[128,3584]{1,0:T(8,128)}) custom-call(s32[1]{0:T(128)} %bitcast.1.place_ref, bf16[8,64,896]{2,1,0:T(8,128)(2,1)} %copy-done.12, bf16[8,64,896]{2,1,0:T(8,128)(2,1)} %copy-done.15, bf16[8,64,896]{2,1,0:T(8,128)(2,1)} %copy-done.13, ...), custom_call_target="tpu_custom_call", output_to_operand_aliasing={{0}: (11, {}), {1}: (12, {})} | custom-call | flops 1526726656 | bytes 5963776 | tf_op jit(solution)/shard_map/absorb/pallas_call | solution.py:239
  239.9 8.4 %absorb.7 = (f32[128,3584]{1,0:T(8,128)}, f32[128,3584]{1,0:T(8,128)}) custom-call(s32[1]{0:T(128)} %bitcast.1.place_ref, bf16[8,96,896]{2,1,0:T(8,128)(2,1)} %copy-done.1, bf16[8,96,896]{2,1,0:T(8,128)(2,1)} %copy-done.9, bf16[3584,128]{1,0:T(8,128)(2,1)} %bitcast.42, bf16[128,3584]{1,0:T(8,128)(2,1)} %bitcast.48, ...), custom_call_target="tpu_custom_call", output_to_operand_aliasing={{0}: (5, {}), {1}: (6, {})} | custom-call | flops 704643072 | bytes 2752512 | tf_op jit(solution)/shard_map/absorb/pallas_call | solution.py:239
  248.4 1.1 copy-done.5
  249.9 10.8 %absorb.8 = (f32[128,3584]{1,0:T(8,128)}, f32[128,3584]{1,0:T(8,128)}) custom-call(s32[1]{0:T(128)} %bitcast.1.place_ref, bf16[8,96,896]{2,1,0:T(8,128)(2,1)} %collective-permute-done.3.refs_0_, bf16[8,96,896]{2,1,0:T(8,128)(2,1)} %copy-done.5, bf16[8,96,896]{2,1,0:T(8,128)(2,1)} %collective-permute-done.4.refs_2_, ...), custom_call_target="tpu_custom_call", output_to_operand_aliasing={{0}: (9, {}), {1}: (10, {})} | custom-call | flops 1291845632 | bytes 5046272 | tf_op jit(solution)/shard_map/absorb/pallas_call | solution.py:239
  260.7 7.6 %absorb.9 = (f32[128,3584]{1,0:T(8,128)}, f32[128,3584]{1,0:T(8,128)}) custom-call(s32[1]{0:T(128)} %bitcast.1.place_ref, bf16[8,96,896]{2,1,0:T(8,128)(2,1)} %collective-permute-done.7.refs_0_, bf16[8,96,896]{2,1,0:T(8,128)(2,1)} %collective-permute-done.8.refs_1_, bf16[3584,128]{1,0:T(8,128)(2,1)} %bitcast.44, ...), custom_call_target="tpu_custom_call", output_to_operand_aliasing={{0}: (5, {}), {1}: (6, {})} | custom-call | flops 352321536 | bytes 1376256 | tf_op jit(solution)/shard_map/absorb/pallas_call | solution.py:239
  268.3 10.3 %finish_down.1 = (bf16[128,3584]{1,0:T(8,128)(2,1)}, bf16[32,112,128]{2,1,0:T(8,128)(2,1)}, bf16[96,3584]{1,0:T(8,128)(2,1)}, bf16[96,128]{1,0:T(8,128)(2,1)}) custom-call(s32[1]{0:T(128)} %bitcast.1.place_ref, s32[1]{0:T(128)} %bitcast.me, s32[1]{0:T(128)} %copy.32.leave, s32[32]{0:T(128)} %owner.3, bf16[8,96,896]{2,1,0:T(8,128)(2,1)} %collective-permute-done.5.refs_0_, ...), custom_call_target="tpu_custom_call" | custom-call | tf_op jit(solution)/shard_map/finish_down/pallas_call | solution.py:295
  278.6 3.6 %all-to-all-start.3 = ((bf16[16,2,112,128]{3,2,1,0:T(8,128)(2,1)}), bf16[16,2,112,128]{3,2,1,0:T(8,128)(2,1)S(1)}, u32[]{:S(2)}, u32[]{:S(2)}) async-start(bf16[16,2,112,128]{3,2,1,0:T(8,128)(2,1)} %bitcast.60), calls=%async_computation.3 | async-start | bytes 1835008 | tf_op jit(solution)/shard_map/all_to_all | solution.py:442
  282.3 8.2 %finish_up.1 = (bf16[3584,128]{1,0:T(8,128)(2,1)}, bf16[32,112,128]{2,1,0:T(8,128)(2,1)}) custom-call(s32[1]{0:T(128)} %bitcast.me, s32[1]{0:T(128)} %copy.32.leave, s32[32]{0:T(128)} %owner.3, bf16[96,3584]{1,0:T(8,128)(2,1)} %get-tuple-element.37.x_ref, bf16[96,128]{1,0:T(8,128)(2,1)} %get-tuple-element.38.pre_ref, f32[128,3584]{1,0:T(8,128)} %get-tuple-element.39.old_up, ...), custom_call_target="tpu_custom_call" | custom-call | flops 587202560 | bytes 5505024 | tf_op jit(solution)/shard_map/finish_up/pallas_call | solution.py:336
  290.4 8.2 %all-to-all-done.3 = bf16[16,2,112,128]{3,2,1,0:T(8,128)(2,1)S(1)} async-done(((bf16[16,2,112,128]{3,2,1,0:T(8,128)(2,1)}), bf16[16,2,112,128]{3,2,1,0:T(8,128)(2,1)S(1)}, u32[]{:S(2)}, u32[]{:S(2)}) %all-to-all-start.3) | async-done | bytes 917536 | tf_op jit(solution)/shard_map/all_to_all | solution.py:442
  298.6 3.6 %all-to-all-start.2 = ((bf16[16,2,112,128]{3,2,1,0:T(8,128)(2,1)}), bf16[16,2,112,128]{3,2,1,0:T(8,128)(2,1)S(1)}, u32[]{:S(2)}, u32[]{:S(2)}) async-start(bf16[16,2,112,128]{3,2,1,0:T(8,128)(2,1)} %bitcast.59), calls=%async_computation.2 | async-start | bytes 1835008 | tf_op jit(solution)/shard_map/all_to_all | solution.py:442
  302.4 1.5 collective-permute-start.27
  303.8 14.1 %all-to-all-done.2 = bf16[16,2,112,128]{3,2,1,0:T(8,128)(2,1)S(1)} async-done(((bf16[16,2,112,128]{3,2,1,0:T(8,128)(2,1)}), bf16[16,2,112,128]{3,2,1,0:T(8,128)(2,1)S(1)}, u32[]{:S(2)}, u32[]{:S(2)}) %all-to-all-start.2) | async-done | bytes 917536 | tf_op jit(solution)/shard_map/all_to_all | solution.py:442
  317.9 1.4 collective-permute-start.26
  319.4 0.6 fusion
  320.0 5.7 %collective-permute-done.26 = bf16[112,128]{1,0:T(8,128)(2,1)S(1)} collective-permute-done((bf16[112,128]{1,0:T(8,128)(2,1)S(1)}, bf16[112,128]{1,0:T(8,128)(2,1)S(1)}, u32[]{:S(2)}, u32[]{:S(2)}) %collective-permute-start.26) | collective-permute-done | bytes 28704 | tf_op jit(solution)/shard_map/ppermute | solution.py:446
  325.7 0.6 fusion.1
  (68 shorter events, 3.4 us)
Async XLA Ops:
  6.3 23.9 %copy-start.7 = (bf16[768,896]{1,0:T(8,128)(2,1)S(1)}, bf16[768,896]{1,0:T(8,128)(2,1)}, u32[]{:S(2)}) copy-start(bf16[768,896]{1,0:T(8,128)(2,1)} %get-tuple-element.26) | copy-start | bytes 4128772
  58.3 18.5 %collective-permute-start.1 = (bf16[8,96,896]{2,1,0:T(8,128)(2,1)}, bf16[8,96,896]{2,1,0:T(8,128)(2,1)S(1)}, u32[]{:S(2)}, u32[]{:S(2)}) collective-permute-start(bf16[8,96,896]{2,1,0:T(8,128)(2,1)} %arrange.2.refs_4_), channel_id=1, source_target_pairs={{0,64},{2,66},{4,68},{6,70},{8,72},{10,74},{12,76},{14,78},{16,80}... | collective-permute-start | bytes 4128776 | tf_op jit(solution)/shard_map/ppermute | solution.py:378
  58.3 18.5 %collective-permute-start = (bf16[8,96,896]{2,1,0:T(8,128)(2,1)}, bf16[8,96,896]{2,1,0:T(8,128)(2,1)S(1)}, u32[]{:S(2)}, u32[]{:S(2)}) collective-permute-start(bf16[8,96,896]{2,1,0:T(8,128)(2,1)} %arrange.2.refs_4_), channel_id=1, source_target_pairs={{0,32},{2,34},{4,36},{6,38},{8,40},{10,42},{12,44},{14,46},{16,48}... | collective-permute-start | bytes 4128776 | tf_op jit(solution)/shard_map/ppermute | solution.py:381
  60.9 25.9 %collective-permute-start.12 = (bf16[8,64,896]{2,1,0:T(8,128)(2,1)}, bf16[8,64,896]{2,1,0:T(8,128)(2,1)}, u32[]{:S(2)}, u32[]{:S(2)}) collective-permute-start(bf16[8,64,896]{2,1,0:T(8,128)(2,1)} %arrange.3.refs_0_), channel_id=1, source_target_pairs={{0,64},{2,66},{4,68},{6,70},{8,72},{10,74},{12,76},{14,78},{16,80}... | collective-permute-start | bytes 2752520 | tf_op jit(solution)/shard_map/ppermute | solution.py:378
  63.1 23.7 %collective-permute-start.11 = (bf16[8,64,896]{2,1,0:T(8,128)(2,1)}, bf16[8,64,896]{2,1,0:T(8,128)(2,1)}, u32[]{:S(2)}, u32[]{:S(2)}) collective-permute-start(bf16[8,64,896]{2,1,0:T(8,128)(2,1)} %arrange.3.refs_0_), channel_id=1, source_target_pairs={{0,32},{2,34},{4,36},{6,38},{8,40},{10,42},{12,44},{14,46},{16,48}... | collective-permute-start | bytes 2752520 | tf_op jit(solution)/shard_map/ppermute | solution.py:381
  76.8 63.3 %copy-start = (bf16[8,96,896]{2,1,0:T(8,128)(2,1)}, bf16[8,96,896]{2,1,0:T(8,128)(2,1)S(1)}, u32[]{:S(2)}) copy-start(bf16[8,96,896]{2,1,0:T(8,128)(2,1)S(1)} %collective-permute-done.1.refs_6_) | copy-start | bytes 4128772
  76.8 1.1 copy-start.3
  77.9 23.5 %collective-permute-start.2 = (bf16[8,96,896]{2,1,0:T(8,128)(2,1)S(1)}, bf16[8,96,896]{2,1,0:T(8,128)(2,1)S(1)}, u32[]{:S(2)}, u32[]{:S(2)}) collective-permute-start(bf16[8,96,896]{2,1,0:T(8,128)(2,1)S(1)} %broadcast_select_fusion.2), channel_id=1, source_target_pairs={{0,64},{2,66},{4,68},{6,70},{8,72},{10,74},{12,76},{14,78},{16,80}... | collective-permute-start | bytes 4128776 | tf_op jit(solution)/shard_map/ppermute | solution.py:378
  88.1 23.2 %collective-permute-start.13 = (bf16[8,64,896]{2,1,0:T(8,128)(2,1)S(1)}, bf16[8,64,896]{2,1,0:T(8,128)(2,1)S(1)}, u32[]{:S(2)}, u32[]{:S(2)}) collective-permute-start(bf16[8,64,896]{2,1,0:T(8,128)(2,1)S(1)} %broadcast_select_fusion.5), channel_id=1, source_target_pairs={{0,64},{2,66},{4,68},{6,70},{8,72},{10,74},{12,76},{14,78},{16,80}... | collective-permute-start | bytes 2752520 | tf_op jit(solution)/shard_map/ppermute | solution.py:378
  101.4 74.4 %copy-start.1 = (bf16[8,96,896]{2,1,0:T(8,128)(2,1)}, bf16[8,96,896]{2,1,0:T(8,128)(2,1)S(1)}, u32[]{:S(2)}) copy-start(bf16[8,96,896]{2,1,0:T(8,128)(2,1)S(1)} %collective-permute-done.2.refs_0_) | copy-start | bytes 4128772
  101.6 35.6 %collective-permute-start.3 = (bf16[8,96,896]{2,1,0:T(8,128)(2,1)S(1)}, bf16[8,96,896]{2,1,0:T(8,128)(2,1)}, u32[]{:S(2)}, u32[]{:S(2)}) collective-permute-start(bf16[8,96,896]{2,1,0:T(8,128)(2,1)S(1)} %broadcast_select_fusion.1), channel_id=1, source_target_pairs={{0,64},{2,66},{4,68},{6,70},{8,72},{10,74},{12,76},{14,78},{16,80}... | collective-permute-start | bytes 4128776 | tf_op jit(solution)/shard_map/ppermute | solution.py:378
  111.2 24.6 %copy-start.2 = (bf16[8,64,896]{2,1,0:T(8,128)(2,1)}, bf16[8,64,896]{2,1,0:T(8,128)(2,1)S(1)}, u32[]{:S(2)}) copy-start(bf16[8,64,896]{2,1,0:T(8,128)(2,1)S(1)} %collective-permute-done.13.refs_4_) | copy-start | bytes 2752516
  111.4 24.4 %collective-permute-start.14 = (bf16[8,64,896]{2,1,0:T(8,128)(2,1)S(1)}, bf16[8,64,896]{2,1,0:T(8,128)(2,1)S(1)}, u32[]{:S(2)}, u32[]{:S(2)}) collective-permute-start(bf16[8,64,896]{2,1,0:T(8,128)(2,1)S(1)} %broadcast_select_fusion.4), channel_id=1, source_target_pairs={{0,64},{2,66},{4,68},{6,70},{8,72},{10,74},{12,76},{14,78},{16,80}... | collective-permute-start | bytes 2752520 | tf_op jit(solution)/shard_map/ppermute | solution.py:378
  112.7 27.5 %collective-permute-start.23 = (bf16[8,64,896]{2,1,0:T(8,128)(2,1)}, bf16[8,64,896]{2,1,0:T(8,128)(2,1)S(1)}, u32[]{:S(2)}, u32[]{:S(2)}) collective-permute-start(bf16[8,64,896]{2,1,0:T(8,128)(2,1)} %collective-permute-done.12.refs_2_), channel_id=1, source_target_pairs={{0,32},{2,34},{4,36},{6,38},{8,40},{10,42},{12,44},{14,46},{16,48}... | collective-permute-start | bytes 2752520 | tf_op jit(solution)/shard_map/ppermute | solution.py:381
  112.8 27.9 %collective-permute-start.24 = (bf16[8,64,896]{2,1,0:T(8,128)(2,1)S(1)}, bf16[8,64,896]{2,1,0:T(8,128)(2,1)S(1)}, u32[]{:S(2)}, u32[]{:S(2)}) collective-permute-start(bf16[8,64,896]{2,1,0:T(8,128)(2,1)S(1)} %collective-permute-done.13.refs_4_), channel_id=1, source_target_pairs={{0,32},{2,34},{4,36},{6,38},{8,40},{10,42},{12,44},{14,46},{16,48}... | collective-permute-start | bytes 2752520 | tf_op jit(solution)/shard_map/ppermute | solution.py:381
  135.8 4.9 %copy-start.4 = (bf16[8,64,896]{2,1,0:T(8,128)(2,1)}, bf16[8,64,896]{2,1,0:T(8,128)(2,1)S(1)}, u32[]{:S(2)}) copy-start(bf16[8,64,896]{2,1,0:T(8,128)(2,1)S(1)} %collective-permute-done.14.refs_6_) | copy-start | bytes 2752516
  135.9 15.3 %collective-permute-start.15 = (bf16[8,64,896]{2,1,0:T(8,128)(2,1)S(1)}, bf16[8,64,896]{2,1,0:T(8,128)(2,1)S(1)}, u32[]{:S(2)}, u32[]{:S(2)}) collective-permute-start(bf16[8,64,896]{2,1,0:T(8,128)(2,1)S(1)} %broadcast_select_fusion.3), channel_id=1, source_target_pairs={{64,128},{66,130},{68,132},{70,134},{72,136},{74,138},{76,140},{78... | collective-permute-start | bytes 2752520 | tf_op jit(solution)/shard_map/ppermute | solution.py:378
  138.8 27.3 %collective-permute-start.4 = (bf16[8,96,896]{2,1,0:T(8,128)(2,1)S(1)}, bf16[8,96,896]{2,1,0:T(8,128)(2,1)}, u32[]{:S(2)}, u32[]{:S(2)}) collective-permute-start(bf16[8,96,896]{2,1,0:T(8,128)(2,1)S(1)} %broadcast_select_fusion), channel_id=1, source_target_pairs={{64,128},{66,130},{68,132},{70,134},{72,136},{74,138},{76,140},{78... | collective-permute-start | bytes 4128776 | tf_op jit(solution)/shard_map/ppermute | solution.py:378
  140.1 35.7 %collective-permute-start.22 = (bf16[8,96,896]{2,1,0:T(8,128)(2,1)S(1)}, bf16[8,96,896]{2,1,0:T(8,128)(2,1)S(1)}, u32[]{:S(2)}, u32[]{:S(2)}) collective-permute-start(bf16[8,96,896]{2,1,0:T(8,128)(2,1)S(1)} %collective-permute-done.1.refs_6_), channel_id=1, source_target_pairs={{0,32},{2,34},{4,36},{6,38},{8,40},{10,42},{12,44},{14,46},{16,48}... | collective-permute-start | bytes 4128776 | tf_op jit(solution)/shard_map/ppermute | solution.py:381
  140.2 75.6 %copy-start.10 = (bf16[8,64,896]{2,1,0:T(8,128)(2,1)}, bf16[8,64,896]{2,1,0:T(8,128)(2,1)S(1)}, u32[]{:S(2)}) copy-start(bf16[8,64,896]{2,1,0:T(8,128)(2,1)S(1)} %collective-permute-done.23.refs_3_) | copy-start | bytes 2752516
  140.2 11.0 %collective-permute-start.25 = (bf16[8,64,896]{2,1,0:T(8,128)(2,1)S(1)}, bf16[8,64,896]{2,1,0:T(8,128)(2,1)S(1)}, u32[]{:S(2)}, u32[]{:S(2)}) collective-permute-start(bf16[8,64,896]{2,1,0:T(8,128)(2,1)S(1)} %collective-permute-done.14.refs_6_), channel_id=1, source_target_pairs={{0,32},{2,34},{4,36},{6,38},{8,40},{10,42},{12,44},{14,46},{16,48}... | collective-permute-start | bytes 2752520 | tf_op jit(solution)/shard_map/ppermute | solution.py:381
  140.7 75.1 %copy-start.11 = (bf16[8,64,896]{2,1,0:T(8,128)(2,1)}, bf16[8,64,896]{2,1,0:T(8,128)(2,1)S(1)}, u32[]{:S(2)}) copy-start(bf16[8,64,896]{2,1,0:T(8,128)(2,1)S(1)} %collective-permute-done.24.refs_5_) | copy-start | bytes 2752516
  140.7 35.1 %collective-permute-start.20 = (bf16[8,64,896]{2,1,0:T(8,128)(2,1)S(1)}, bf16[8,64,896]{2,1,0:T(8,128)(2,1)S(1)}, u32[]{:S(2)}, u32[]{:S(2)}) collective-permute-start(bf16[8,64,896]{2,1,0:T(8,128)(2,1)S(1)} %collective-permute-done.14.refs_6_), channel_id=1, source_target_pairs={{96,32},{98,34},{100,36},{102,38},{104,40},{106,42},{108,44},{110,... | collective-permute-start | bytes 2752520 | tf_op jit(solution)/shard_map/ppermute | solution.py:378
  151.2 64.6 %copy-start.12 = (bf16[8,64,896]{2,1,0:T(8,128)(2,1)}, bf16[8,64,896]{2,1,0:T(8,128)(2,1)S(1)}, u32[]{:S(2)}) copy-start(bf16[8,64,896]{2,1,0:T(8,128)(2,1)S(1)} %collective-permute-done.15.refs_0_) | copy-start | bytes 2752516
  151.2 25.1 %collective-permute-start.19 = (bf16[8,64,896]{2,1,0:T(8,128)(2,1)S(1)}, bf16[8,64,896]{2,1,0:T(8,128)(2,1)S(1)}, u32[]{:S(2)}, u32[]{:S(2)}) collective-permute-start(bf16[8,64,896]{2,1,0:T(8,128)(2,1)S(1)} %collective-permute-done.15.refs_0_), channel_id=1, source_target_pairs={{0,32},{2,34},{4,36},{6,38},{8,40},{10,42},{12,44},{14,46},{16,48}... | collective-permute-start | bytes 2752520 | tf_op jit(solution)/shard_map/ppermute | solution.py:381
  151.2 16.1 %copy-start.14 = (bf16[8,64,896]{2,1,0:T(8,128)(2,1)}, bf16[8,64,896]{2,1,0:T(8,128)(2,1)S(1)}, u32[]{:S(2)}) copy-start(bf16[8,64,896]{2,1,0:T(8,128)(2,1)S(1)} %collective-permute-done.25.refs_7_) | copy-start | bytes 2752516
  151.2 64.0 %collective-permute-start.7 = (bf16[8,96,896]{2,1,0:T(8,128)(2,1)}, bf16[8,96,896]{2,1,0:T(8,128)(2,1)}, u32[]{:S(2)}, u32[]{:S(2)}) collective-permute-start(bf16[8,96,896]{2,1,0:T(8,128)(2,1)} %collective-permute-done.3.refs_0_), channel_id=1, source_target_pairs={{96,32},{98,34},{100,36},{102,38},{104,40},{106,42},{108,44},{110,... | collective-permute-start | bytes 4128776 | tf_op jit(solution)/shard_map/ppermute | solution.py:378
  166.1 49.7 %collective-permute-start.5 = (bf16[8,96,896]{2,1,0:T(8,128)(2,1)}, bf16[8,96,896]{2,1,0:T(8,128)(2,1)}, u32[]{:S(2)}, u32[]{:S(2)}) collective-permute-start(bf16[8,96,896]{2,1,0:T(8,128)(2,1)} %collective-permute-done.4.refs_2_), channel_id=1, source_target_pairs={{96,32},{98,34},{100,36},{102,38},{104,40},{106,42},{108,44},{110,... | collective-permute-start | bytes 4128776 | tf_op jit(solution)/shard_map/ppermute | solution.py:378
  175.8 40.1 %copy-start.13 = (bf16[8,64,896]{2,1,0:T(8,128)(2,1)}, bf16[8,64,896]{2,1,0:T(8,128)(2,1)S(1)}, u32[]{:S(2)}) copy-start(bf16[8,64,896]{2,1,0:T(8,128)(2,1)S(1)} %collective-permute-done.20.refs_2_) | copy-start | bytes 2752516
  175.8 40.0 %collective-permute-start.18 = (bf16[8,96,896]{2,1,0:T(8,128)(2,1)S(1)}, bf16[8,96,896]{2,1,0:T(8,128)(2,1)S(1)}, u32[]{:S(2)}, u32[]{:S(2)}) collective-permute-start(bf16[8,96,896]{2,1,0:T(8,128)(2,1)S(1)} %collective-permute-done.2.refs_0_), channel_id=1, source_target_pairs={{0,32},{2,34},{4,36},{6,38},{8,40},{10,42},{12,44},{14,46},{16,48}... | collective-permute-start | bytes 4128776 | tf_op jit(solution)/shard_map/ppermute | solution.py:381
  175.8 40.1 %copy-start.8 = (bf16[8,96,896]{2,1,0:T(8,128)(2,1)}, bf16[8,96,896]{2,1,0:T(8,128)(2,1)S(1)}, u32[]{:S(2)}) copy-start(bf16[8,96,896]{2,1,0:T(8,128)(2,1)S(1)} %collective-permute-done.22.refs_7_) | copy-start | bytes 4128772
  175.8 4.4 %collective-permute-start.21 = (bf16[8,64,896]{2,1,0:T(8,128)(2,1)S(1)}, bf16[8,64,896]{2,1,0:T(8,128)(2,1)S(1)}, u32[]{:S(2)}, u32[]{:S(2)}) collective-permute-start(bf16[8,64,896]{2,1,0:T(8,128)(2,1)S(1)} %collective-permute-done.20.refs_2_), channel_id=1, source_target_pairs={{0,32},{2,34},{4,36},{6,38},{8,40},{10,42},{12,44},{14,46},{16,48}... | collective-permute-start | bytes 2752520 | tf_op jit(solution)/shard_map/ppermute | solution.py:381
  176.3 39.6 %copy-start.15 = (bf16[8,64,896]{2,1,0:T(8,128)(2,1)}, bf16[8,64,896]{2,1,0:T(8,128)(2,1)S(1)}, u32[]{:S(2)}) copy-start(bf16[8,64,896]{2,1,0:T(8,128)(2,1)S(1)} %collective-permute-done.19.refs_1_) | copy-start | bytes 2752516
  176.3 38.9 %collective-permute-start.16 = (bf16[8,64,896]{2,1,0:T(8,128)(2,1)S(1)}, bf16[8,64,896]{2,1,0:T(8,128)(2,1)}, u32[]{:S(2)}, u32[]{:S(2)}) collective-permute-start(bf16[8,64,896]{2,1,0:T(8,128)(2,1)S(1)} %collective-permute-done.15.refs_0_), channel_id=1, source_target_pairs={{96,32},{98,34},{100,36},{102,38},{104,40},{106,42},{108,44},{110,... | collective-permute-start | bytes 2752520 | tf_op jit(solution)/shard_map/ppermute | solution.py:378
  180.2 35.6 %copy-start.16 = (bf16[8,64,896]{2,1,0:T(8,128)(2,1)}, bf16[8,64,896]{2,1,0:T(8,128)(2,1)S(1)}, u32[]{:S(2)}) copy-start(bf16[8,64,896]{2,1,0:T(8,128)(2,1)S(1)} %collective-permute-done.21.refs_3_) | copy-start | bytes 2752516
  180.2 68.1 %collective-permute-start.9 = (bf16[8,96,896]{2,1,0:T(8,128)(2,1)}, bf16[8,96,896]{2,1,0:T(8,128)(2,1)S(1)}, u32[]{:S(2)}, u32[]{:S(2)}) collective-permute-start(bf16[8,96,896]{2,1,0:T(8,128)(2,1)} %collective-permute-done.3.refs_0_), channel_id=1, source_target_pairs={{0,32},{2,34},{4,36},{6,38},{8,40},{10,42},{12,44},{14,46},{16,48}... | collective-permute-start | bytes 4128776 | tf_op jit(solution)/shard_map/ppermute | solution.py:381
  215.2 33.1 %collective-permute-start.10 = (bf16[8,96,896]{2,1,0:T(8,128)(2,1)}, bf16[8,96,896]{2,1,0:T(8,128)(2,1)S(1)}, u32[]{:S(2)}, u32[]{:S(2)}) collective-permute-start(bf16[8,96,896]{2,1,0:T(8,128)(2,1)} %collective-permute-done.4.refs_2_), channel_id=1, source_target_pairs={{0,32},{2,34},{4,36},{6,38},{8,40},{10,42},{12,44},{14,46},{16,48}... | collective-permute-start | bytes 4128776 | tf_op jit(solution)/shard_map/ppermute | solution.py:381
  215.2 45.5 %collective-permute-start.8 = (bf16[8,96,896]{2,1,0:T(8,128)(2,1)}, bf16[8,96,896]{2,1,0:T(8,128)(2,1)}, u32[]{:S(2)}, u32[]{:S(2)}) collective-permute-start(bf16[8,96,896]{2,1,0:T(8,128)(2,1)} %collective-permute-done.7.refs_0_), channel_id=1, source_target_pairs={{0,32},{2,34},{4,36},{6,38},{8,40},{10,42},{12,44},{14,46},{16,48}... | collective-permute-start | bytes 4128776 | tf_op jit(solution)/shard_map/ppermute | solution.py:381
  215.7 52.6 %collective-permute-start.6 = (bf16[8,96,896]{2,1,0:T(8,128)(2,1)}, bf16[8,96,896]{2,1,0:T(8,128)(2,1)}, u32[]{:S(2)}, u32[]{:S(2)}) collective-permute-start(bf16[8,96,896]{2,1,0:T(8,128)(2,1)} %collective-permute-done.5.refs_0_), channel_id=1, source_target_pairs={{0,32},{2,34},{4,36},{6,38},{8,40},{10,42},{12,44},{14,46},{16,48}... | collective-permute-start | bytes 4128776 | tf_op jit(solution)/shard_map/ppermute | solution.py:381
  215.9 1.1 copy-start.9
  217.0 31.4 %collective-permute-start.17 = (bf16[8,64,896]{2,1,0:T(8,128)(2,1)}, bf16[8,64,896]{2,1,0:T(8,128)(2,1)}, u32[]{:S(2)}, u32[]{:S(2)}) collective-permute-start(bf16[8,64,896]{2,1,0:T(8,128)(2,1)} %collective-permute-done.16.refs_4_), channel_id=1, source_target_pairs={{0,32},{2,34},{4,36},{6,38},{8,40},{10,42},{12,44},{14,46},{16,48}... | collective-permute-start | bytes 2752520 | tf_op jit(solution)/shard_map/ppermute | solution.py:381
  248.4 1.1 copy-start.5
  248.4 1.5 copy-start.6
  278.6 20.0 %all-to-all-start.3 = ((bf16[16,2,112,128]{3,2,1,0:T(8,128)(2,1)}), bf16[16,2,112,128]{3,2,1,0:T(8,128)(2,1)S(1)}, u32[]{:S(2)}, u32[]{:S(2)}) async-start(bf16[16,2,112,128]{3,2,1,0:T(8,128)(2,1)} %bitcast.60), calls=%async_computation.3 | async-start | bytes 1835008 | tf_op jit(solution)/shard_map/all_to_all | solution.py:442
  298.6 19.3 %all-to-all-start.2 = ((bf16[16,2,112,128]{3,2,1,0:T(8,128)(2,1)}), bf16[16,2,112,128]{3,2,1,0:T(8,128)(2,1)S(1)}, u32[]{:S(2)}, u32[]{:S(2)}) async-start(bf16[16,2,112,128]{3,2,1,0:T(8,128)(2,1)} %bitcast.59), calls=%async_computation.2 | async-start | bytes 1835008 | tf_op jit(solution)/shard_map/all_to_all | solution.py:442
  302.4 17.0 %collective-permute-start.27 = (bf16[112,128]{1,0:T(8,128)(2,1)S(1)}, bf16[112,128]{1,0:T(8,128)(2,1)S(1)}, u32[]{:S(2)}, u32[]{:S(2)}) collective-permute-start(bf16[112,128]{1,0:T(8,128)(2,1)S(1)} %dynamic-slice_bitcast_fusion), channel_id=1, source_target_pairs={{0,1},{2,3},{4,5},{6,7},{8,9},{10,11},{12,13},{14,15},{16,17},{18,... | collective-permute-start | bytes 86024 | tf_op jit(solution)/shard_map/ppermute | solution.py:446
  317.9 7.8 %collective-permute-start.26 = (bf16[112,128]{1,0:T(8,128)(2,1)S(1)}, bf16[112,128]{1,0:T(8,128)(2,1)S(1)}, u32[]{:S(2)}, u32[]{:S(2)}) collective-permute-start(bf16[112,128]{1,0:T(8,128)(2,1)S(1)} %dynamic-slice_bitcast_fusion.1), channel_id=1, source_target_pairs={{0,1},{2,3},{4,5},{6,7},{8,9},{10,11},{12,13},{14,15},{16,17},{18,... | collective-permute-start | bytes 86024 | tf_op jit(solution)/shard_map/ppermute | solution.py:446

commit v3 on v2

--- a/solution.py
+++ b/solution.py
@@ -14,11 +14,12 @@
 ALL = ("zl", "co", "y", "x", "zh")
 SLOT_GROUPS = ((0, 2), (2, 3))
 TAGS = ("a", "b")
-SUMS = ("ao1p2q3r", "a45 bo1p", "b2q", "b3r4 a6", "b5")
+SUMS = ("ao1p2q3r", "a4 bo1p", "a5 b2q", "a6 b3r", "b45")
 LAST = "b6"
 PIECES = 4
 VMEM = pl.BlockSpec(memory_space=pltpu.VMEM)
 SMEM = pl.BlockSpec(memory_space=pltpu.SMEM)
+HBM = pl.BlockSpec(memory_space=pltpu.MemorySpace.HBM)
 LIMIT = 60 * 1024 * 1024
 
 
@@ -210,42 +211,77 @@
     width, hidden_units = w_up.shape
     total = sum(first.shape[1] for _, first, _ in blocks)
     have = sums is not None
-    step = width // 7
+    steps = 7
+    step = width // steps
     tile = total // 2 if total > 128 else total
+    count = len(arrays)
 
     def body(place_ref, *refs):
-        ins, refs = refs[: len(arrays)], refs[len(arrays) :]
-        up_ref, down_ref = refs[:2]
-        refs = refs[2:]
+        hbm_in, refs = refs[: count + 2], refs[count + 2 :]
         if have:
-            old_up, old_down = refs[:2]
-            refs = refs[2:]
-        out_up, out_down, held_x, held_c, held_pre, held_hid = refs
-        gather_rows(place_ref[0], blocks, ins, held_x, held_c)
-        row_terms(up_ref, down_ref, held_x, held_c, held_pre, held_hid, tile)
+            hbm_in, refs = hbm_in + refs[:2], refs[2:]
+        outs, refs = refs[:2], refs[2:]
+        vmem_in, refs = list(refs[: count + 2]), refs[count + 2 :]
+        acc_up, acc_down, held_x, held_c, held_pre, held_hid, in_sems, out_sems = refs
+        if have:
+            vmem_in += [acc_up, acc_down]
+        copies = [
+            pltpu.make_async_copy(source, target, in_sems.at[i])
+            for i, (source, target) in enumerate(zip(hbm_in, vmem_in))
+        ]
+        for copy in copies:
+            copy.start()
+        for copy in copies[:count]:
+            copy.wait()
+        gather_rows(place_ref[0], blocks, vmem_in[:count], held_x, held_c)
+        for copy in copies[count : count + 2]:
+            copy.wait()
+        row_terms(vmem_in[count], vmem_in[count + 1], held_x, held_c, held_pre, held_hid, tile)
+        for copy in copies[count + 2 :]:
+            copy.wait()
+
+        def leave(j):
+            span = pl.ds(pl.multiple_of(j * step, step), step)
+            return [
+                pltpu.make_async_copy(acc.at[:, span], out.at[:, span], out_sems.at[k, j])
+                for k, (acc, out) in enumerate(zip((acc_up, acc_down), outs))
+            ]
 
         def columns(j, carry):
             span = pl.ds(pl.multiple_of(j * step, step), step)
             part_up = column_sums(held_pre[...], held_x[:, span])
+            acc_up[:, span] = part_up + acc_up[:, span] if have else part_up
             part_down = column_sums(held_hid[...], held_c[:, span])
-            out_up[:, span] = part_up + old_up[:, span] if have else part_up
-            out_down[:, span] = part_down + old_down[:, span] if have else part_down
+            acc_down[:, span] = part_down + acc_down[:, span] if have else part_down
+            for copy in leave(j):
+                copy.start()
             return carry
 
-        lax.fori_loop(0, 7, columns, 0)
+        def drain(j, carry):
+            for copy in leave(j):
+                copy.wait()
+            return carry
+
+        lax.fori_loop(0, steps, columns, 0)
+        lax.fori_loop(0, steps, drain, 0)
 
     shape = jax.ShapeDtypeStruct((hidden_units, width), jnp.float32)
     args = [place, *arrays, w_up, w_down] + (list(sums) if have else [])
     return pl.pallas_call(
         body,
         out_shape=[shape, shape],
-        in_specs=[SMEM] + [VMEM] * (len(args) - 1),
-        out_specs=[VMEM, VMEM],
-        scratch_shapes=[
+        in_specs=[SMEM] + [HBM] * (len(args) - 1),
+        out_specs=[HBM, HBM],
+        scratch_shapes=[pltpu.VMEM(a.shape, a.dtype) for a in (*arrays, w_up, w_down)]
+        + [
+            pltpu.VMEM((hidden_units, width), jnp.float32),
+            pltpu.VMEM((hidden_units, width), jnp.float32),
             pltpu.VMEM((total, width), jnp.bfloat16),
             pltpu.VMEM((total, width), jnp.bfloat16),
             pltpu.VMEM((total, hidden_units), jnp.bfloat16),
             pltpu.VMEM((total, hidden_units), jnp.bfloat16),
+            pltpu.SemaphoreType.DMA((len(args) - 1,)),
+            pltpu.SemaphoreType.DMA((2, steps)),
         ],
         input_output_aliases={len(args) - 2: 0, len(args) - 1: 1} if have else {},
         compiler_params=pltpu.CompilerParams(vmem_limit_bytes=LIMIT),
@@ -270,15 +306,31 @@
     tiles = tile_owner.shape[0]
     tile_rows = width // tiles
     total = sum(first.shape[1] for _, first, _ in blocks)
-    step = 256
+    step = width // PIECES
+
+    count = len(arrays)
 
     def body(place_ref, me, leave, owner, *refs):
-        ins, refs = refs[: len(arrays)], refs[len(arrays) :]
-        up_ref, down_ref, old_down, md, vd = refs[:5]
-        out_down, out_tiles, out_x, out_pre, both, held_c, held_hid = refs[5:]
+        hbm_in, refs = refs[: count + 5], refs[count + 5 :]
+        out_down, out_tiles, out_x, out_pre = refs[:4]
+        vmem_in, refs = refs[4 : count + 9], refs[count + 9 :]
+        both, held_c, held_hid, sems = refs
+        copies = [
+            pltpu.make_async_copy(source, target, sems.at[i])
+            for i, (source, target) in enumerate(zip(hbm_in, vmem_in))
+        ]
+        for copy in copies:
+            copy.start()
         keep = me[0] != leave[0]
-        gather_rows(place_ref[0], blocks, ins, out_x, held_c)
+        for copy in copies[:count]:
+            copy.wait()
+        gather_rows(place_ref[0], blocks, vmem_in[:count], out_x, held_c)
+        up_ref, down_ref, old_down, md, vd = vmem_in[count:]
+        for copy in copies[count : count + 2]:
+            copy.wait()
         row_terms(up_ref, down_ref, out_x, held_c, out_pre, held_hid, total)
+        for copy in copies[count + 2 :]:
+            copy.wait()
 
         def columns(j, carry):
             span = pl.ds(pl.multiple_of(j * step, step), step)
@@ -292,6 +344,7 @@
         for t in range(tiles):
             out_tiles[owner[t]] = both[t * tile_rows : (t + 1) * tile_rows, :]
 
+    args = (*arrays, w_up, w_down, old, m_down, v_down)
     return pl.pallas_call(
         body,
         out_shape=[
@@ -300,23 +353,25 @@
             jax.ShapeDtypeStruct((total, width), jnp.bfloat16),
             jax.ShapeDtypeStruct((total, hidden_units), jnp.bfloat16),
         ],
-        in_specs=[SMEM] * 4 + [VMEM] * (len(arrays) + 5),
+        in_specs=[SMEM] * 4 + [HBM] * len(args),
         out_specs=[VMEM] * 4,
-        scratch_shapes=[
+        scratch_shapes=[pltpu.VMEM(a.shape, a.dtype) for a in args]
+        + [
             pltpu.VMEM((width, hidden_units), jnp.bfloat16),
             pltpu.VMEM((total, width), jnp.bfloat16),
             pltpu.VMEM((total, hidden_units), jnp.bfloat16),
+            pltpu.SemaphoreType.DMA((len(args),)),
         ],
         compiler_params=pltpu.CompilerParams(vmem_limit_bytes=LIMIT),
         name="finish_down",
-    )(place, my_index, leaving, tile_owner, *arrays, w_up, w_down, old, m_down, v_down)
+    )(place, my_index, leaving, tile_owner, *args)
 
 
 def finish_up(my_index, leaving, tile_owner, rows_x, pre_grad, old, m_up, v_up):
     width, hidden_units = m_up.shape
     tiles = tile_owner.shape[0]
     tile_rows = width // tiles
-    step = 256
+    step = width // PIECES
 
     def body(me, leave, owner, x_ref, pre_ref, old_up, mu, vu, out_up, out_tiles, both):
         keep = me[0] != leave[0]
@@ -365,14 +420,16 @@
     base = jnp.where(low <= 1, half, 1 - half)
     place_ref = place.reshape(1)
 
-    outgoing = prepare(
-        base.reshape(1),
-        tokens,
-        cotangent,
-        gates.reshape(1, tok_count),
-        routes.reshape(1, tok_count),
-        SLOT_GROUPS,
-    )
+    outgoing = []
+    for tag, group in zip(TAGS, SLOT_GROUPS):
+        outgoing += prepare(
+            base.reshape(1),
+            tokens,
+            cotangent,
+            gates.reshape(1, tok_count),
+            routes.reshape(1, tok_count),
+            (group,),
+        )
 
     def step(value, places):
         return lax.ppermute(value, ALL, stream_pairs(places))
@@ -391,21 +448,30 @@
             sent.reshape(32, rows // 32, piece), ("co", "y", "x"), 0, 0, tiled=True
         ).reshape(rows, piece)
         chunks.append({"tag": tag, "slots": slots, 0: previous})
-    everyone = (0, 1, 2, 3)
+
+    def joined(first, second):
+        return jnp.where(place == 3, first, second)
+
     for ch in chunks:
         tag = ch["tag"]
         ch[0] = arrange(ch[0], ch["slots"])
-        ch[1] = step(ch[0], everyone)
+        ch[1] = step(ch[0], (0, 1, 2, 3))
         ch["s0"] = swap(ch[0])
-        ch[2] = step(jnp.where(place == 2, ch["s0"], ch[1]), everyone)
+        x2 = step(ch["s0"], (2,))
+        y2 = step(ch[1], (0, 1, 3))
         ch["s1"] = swap(ch[1])
-        ch[3] = step(jnp.where(place == 2, ch[1], ch[2]), (0, 1, 2))
+        x3 = step(ch[1], (2,))
+        y3 = step(y2, (0, 1))
+        ch[2] = joined(x2, y2)
         ch["s2"] = swap(ch[2])
-        ch[4] = step(jnp.where(place == 2, ch[2], ch[3]), (1, 2))
+        x4 = step(y2, (2,))
+        y4 = step(y3, (1,))
+        ch[3] = joined(x3, y3)
         ch["s3"] = swap(ch[3])
-        ch[5] = step(ch[3], (2,))
+        ch[5] = step(y3, (2,))
+        ch[4] = joined(x4, y4)
         ch["s4"] = swap(ch[4])
-        ch[6] = step(ch[4], (2,))
+        ch[6] = step(y4, (2,))
         ch["s5"] = swap(ch[5])
         ch["s6"] = swap(ch[6])
 

time: 327 us -> 336 us (1.028)
  the two profiles are of different devices: /device:TPU:224 before, /device:TPU:96 now
where the time goes in v3:
time: 336 us; the launch traced here: 335 us
  waiting for transfers between devices  177 us (53%)
  Pallas kernels  66.4 us (20%)
  starting transfers between devices  58.2 us (17%)
  blocking collectives  25.7 us (8%)
  other arithmetic  5.51 us (2%)
    ppermute x18, waiting for transfers between devices, step(): return lax.ppermute(value, ALL, stream_pairs(places))  140 us
    pallas_call x5, Pallas kernels, absorb(): pl.pallas_call(body, out_shape=[shape, shape], in_specs=[SMEM] + [HBM] *...  38.4 us
    ppermute x18, starting transfers between devices, step(): return lax.ppermute(value, ALL, stream_pairs(places))  29.8 us
    all_to_all x1, blocking collectives, on_device(): lax.all_to_all(sent.reshape(32, rows // 32, piece), ('co', 'y', 'x'), 0,...  25.7 us
    all_to_all x2, waiting for transfers between devices, adopt(): lax.all_to_all(tiles.reshape(16, 2, rows, units), ('y', 'x'), 0, 0, tiled...  22.2 us
    all_to_all x1, waiting for transfers between devices, on_device(): lax.all_to_all(sent.reshape(32, rows // 32, piece), ('co', 'y', 'x'), 0,...  11.8 us
    ppermute x2, starting transfers between devices, adopt(): crossed = lax.ppermute(other, ALL, across_pairs())  8.85 us
    pallas_call x2, Pallas kernels, prepare(): pl.pallas_call(body, out_shape=[jax.ShapeDtypeStruct((32 * parts * slots,...  8.27 us
  transfers between devices with their start and end apart: 37, of which 13 were waited for; matrix products, arithmetic and copies ran while one was open for 1% of the time, Pallas kernels for 15%

profile of v3, /device:TPU:96, one launch (start us, length us, event | category | flops | bytes accessed | tf_op | source)
XLA Modules:
  0.0 335.5 jit_solution(9460631733431753458)
XLA Ops:
  0.6 3.7 %prepare.2 = bf16[512,896]{1,0:T(8,128)(2,1)} custom-call(s32[1]{0:T(128)} %bitcast.2.base_ref, bf16[128,3584]{1,0:T(8,128)(2,1)} %x_ref.3, bf16[128,3584]{1,0:T(8,128)(2,1)} %c_ref.3, f32[1,128]{1,0:T(1,128)} %bitcast.62, s32[1,128]{1,0:T(1,128)} %bitcast.64), custom_call_target="tpu_custom_call" | custom-call | tf_op jit(solution)/shard_map/prepare/pallas_call | solution.py:105
  4.4 7.3 %all-to-all-start = ((bf16[32,16,896]{2,1,0:T(8,128)(2,1)}), bf16[32,16,896]{2,1,0:T(8,128)(2,1)S(1)}, u32[]{:S(2)}, u32[]{:S(2)}) async-start(bf16[32,16,896]{2,1,0:T(8,128)(2,1)} %bitcast.55), calls=%async_computation | async-start | bytes 1835008 | tf_op jit(solution)/shard_map/all_to_all | solution.py:447
  11.7 4.5 %prepare.3 = bf16[768,896]{1,0:T(8,128)(2,1)} custom-call(s32[1]{0:T(128)} %bitcast.2.base_ref, bf16[128,3584]{1,0:T(8,128)(2,1)} %x_ref.3, bf16[128,3584]{1,0:T(8,128)(2,1)} %c_ref.3, f32[1,128]{1,0:T(1,128)} %bitcast.63, s32[1,128]{1,0:T(1,128)} %bitcast.65), custom_call_target="tpu_custom_call" | custom-call | tf_op jit(solution)/shard_map/prepare/pallas_call | solution.py:105
  16.2 11.8 %all-to-all-done = bf16[32,16,896]{2,1,0:T(8,128)(2,1)S(1)} async-done(((bf16[32,16,896]{2,1,0:T(8,128)(2,1)}), bf16[32,16,896]{2,1,0:T(8,128)(2,1)S(1)}, u32[]{:S(2)}, u32[]{:S(2)}) %all-to-all-start) | async-done | bytes 917536 | tf_op jit(solution)/shard_map/all_to_all | solution.py:447
  28.1 25.7 %all_to_all.20 = bf16[32,24,896]{2,1,0:T(8,128)(2,1)} all-to-all(bf16[32,24,896]{2,1,0:T(8,128)(2,1)} %bitcast.52), channel_id=1, replica_groups=mesh['zl'=4,'co'=2,'y'=4,'x'=4,'zh'=2] {'co','y','x'}, dimensions={0} | all-to-all | bytes 2752512 | tf_op jit(solution)/shard_map/all_to_all | solution.py:447
  53.8 3.4 %arrange.2.refs_2_ = bf16[8,96,896]{2,1,0:T(8,128)(2,1)} custom-call(bf16[768,896]{1,0:T(8,128)(2,1)} %bitcast.53), custom_call_target="tpu_custom_call" | custom-call | tf_op jit(solution)/shard_map/arrange/pallas_call | solution.py:147
  57.3 3.1 collective-permute-start
  60.4 2.5 arrange.3.refs_0_
  63.9 22.4 %collective-permute-done.10.refs_2_ = bf16[8,64,896]{2,1,0:T(8,128)(2,1)} collective-permute-done((bf16[8,64,896]{2,1,0:T(8,128)(2,1)}, bf16[8,64,896]{2,1,0:T(8,128)(2,1)}, u32[]{:S(2)}, u32[]{:S(2)}) %collective-permute-start.10) | collective-permute-done | bytes 917536 | tf_op jit(solution)/shard_map/ppermute | solution.py:435
  86.4 6.5 %collective-permute-start.11 = (bf16[8,64,896]{2,1,0:T(8,128)(2,1)}, bf16[8,64,896]{2,1,0:T(8,128)(2,1)}, u32[]{:S(2)}, u32[]{:S(2)}) collective-permute-start(bf16[8,64,896]{2,1,0:T(8,128)(2,1)} %collective-permute-done.10.refs_2_), channel_id=1, source_target_pairs={{0,64},{2,66},{4,68},{6,70},{8,72},{10,74},{12,76},{14,78},{16,80}... | collective-permute-start | bytes 2752520 | tf_op jit(solution)/shard_map/ppermute | solution.py:435
  92.9 1.3 collective-permute-start.28
  94.2 2.5 collective-permute-start.1
  96.7 1.3 collective-permute-start.30
  98.1 5.1 %collective-permute-done.11 = bf16[8,64,896]{2,1,0:T(8,128)(2,1)} collective-permute-done((bf16[8,64,896]{2,1,0:T(8,128)(2,1)}, bf16[8,64,896]{2,1,0:T(8,128)(2,1)}, u32[]{:S(2)}, u32[]{:S(2)}) %collective-permute-start.11) | collective-permute-done | bytes 917536 | tf_op jit(solution)/shard_map/ppermute | solution.py:435
  103.2 1.6 collective-permute-start.12
  104.8 3.4 %collective-permute-done.28 = bf16[8,64,896]{2,1,0:T(8,128)(2,1)S(1)} collective-permute-done((bf16[8,64,896]{2,1,0:T(8,128)(2,1)S(1)}, bf16[8,64,896]{2,1,0:T(8,128)(2,1)S(1)}, u32[]{:S(2)}, u32[]{:S(2)}) %collective-permute-start.28) | collective-permute-done | bytes 917536 | tf_op jit(solution)/shard_map/ppermute | solution.py:435
  109.1 1.3 broadcast_select_fusion.4.refs_4_
  110.4 7.7 %collective-permute-done.30 = bf16[8,64,896]{2,1,0:T(8,128)(2,1)} collective-permute-done((bf16[8,64,896]{2,1,0:T(8,128)(2,1)}, bf16[8,64,896]{2,1,0:T(8,128)(2,1)}, u32[]{:S(2)}, u32[]{:S(2)}) %collective-permute-start.30) | collective-permute-done | bytes 917536 | tf_op jit(solution)/shard_map/ppermute | solution.py:435
  118.9 1.3 collective-permute-start.23
  120.2 1.3 broadcast_select_fusion.3.refs_6_
  121.5 3.1 collective-permute-start.31
  125.4 14.5 %collective-permute-done.23 = bf16[8,64,896]{2,1,0:T(8,128)(2,1)S(1)} collective-permute-done((bf16[8,64,896]{2,1,0:T(8,128)(2,1)}, bf16[8,64,896]{2,1,0:T(8,128)(2,1)S(1)}, u32[]{:S(2)}, u32[]{:S(2)}) %collective-permute-start.23) | collective-permute-done | bytes 917536 | tf_op jit(solution)/shard_map/ppermute | solution.py:435
  139.9 1.3 collective-permute-start.21
  141.2 1.3 collective-permute-start.18
  142.5 1.3 collective-permute-start.16
  144.7 25.4 %collective-permute-done.18.refs_0_ = bf16[8,64,896]{2,1,0:T(8,128)(2,1)S(1)} collective-permute-done((bf16[8,64,896]{2,1,0:T(8,128)(2,1)}, bf16[8,64,896]{2,1,0:T(8,128)(2,1)S(1)}, u32[]{:S(2)}, u32[]{:S(2)}) %collective-permute-start.18) | collective-permute-done | bytes 917536 | tf_op jit(solution)/shard_map/ppermute | solution.py:435
  170.6 1.3 collective-permute-start.6
  171.9 12.9 %collective-permute-done.16 = bf16[8,96,896]{2,1,0:T(8,128)(2,1)S(1)} collective-permute-done((bf16[8,96,896]{2,1,0:T(8,128)(2,1)S(1)}, bf16[8,96,896]{2,1,0:T(8,128)(2,1)S(1)}, u32[]{:S(2)}, u32[]{:S(2)}) %collective-permute-start.16) | collective-permute-done | bytes 1376288 | tf_op jit(solution)/shard_map/ppermute | solution.py:435
  184.9 1.3 collective-permute-start.8
  186.2 1.3 collective-permute-start.4
  187.8 1.3 collective-permute-start.14
  189.4 10.2 %collective-permute-done.6 = bf16[8,96,896]{2,1,0:T(8,128)(2,1)S(1)} collective-permute-done((bf16[8,96,896]{2,1,0:T(8,128)(2,1)}, bf16[8,96,896]{2,1,0:T(8,128)(2,1)S(1)}, u32[]{:S(2)}, u32[]{:S(2)}) %collective-permute-start.6) | collective-permute-done | bytes 1376288 | tf_op jit(solution)/shard_map/ppermute | solution.py:435
  199.6 1.2 broadcast_select_fusion.2.refs_0_
  200.8 38.2 %collective-permute-done.14.refs_0_ = bf16[8,64,896]{2,1,0:T(8,128)(2,1)} collective-permute-done((bf16[8,64,896]{2,1,0:T(8,128)(2,1)S(1)}, bf16[8,64,896]{2,1,0:T(8,128)(2,1)}, u32[]{:S(2)}, u32[]{:S(2)}) %collective-permute-start.14) | collective-permute-done | bytes 917536 | tf_op jit(solution)/shard_map/ppermute | solution.py:435
  240.8 8.9 %absorb.5 = (f32[128,3584]{1,0:T(8,128)}, f32[128,3584]{1,0:T(8,128)}) custom-call(s32[1]{0:T(128)} %bitcast.1.place_ref, bf16[8,64,896]{2,1,0:T(8,128)(2,1)} %arrange.3.refs_0_, bf16[8,64,896]{2,1,0:T(8,128)(2,1)} %copy-done.10, bf16[8,64,896]{2,1,0:T(8,128)(2,1)} %collective-permute-done.10.refs_2_, bf16[8,64,896]{2,1,0:T(8,128)(2,1)} %collective-permute-done.27.refs_3_, ...), custom_call_target="tpu_custom_call" | custom-call | flops 1644167168 | bytes 6422528 | tf_op jit(solution)/shard_map/absorb/pallas_call | solution.py:270
  249.7 8.5 %absorb.6 = (f32[128,3584]{1,0:T(8,128)}, f32[128,3584]{1,0:T(8,128)}) custom-call(s32[1]{0:T(128)} %bitcast.1.place_ref, bf16[8,64,896]{2,1,0:T(8,128)(2,1)} %copy-done.5, bf16[8,64,896]{2,1,0:T(8,128)(2,1)} %copy-done.14, bf16[8,96,896]{2,1,0:T(8,128)(2,1)} %arrange.2.refs_2_, ...), custom_call_target="tpu_custom_call", output_to_operand_aliasing={{0}: (9, {}), {1}: (10, {})} | custom-call | flops 1291845632 | bytes 5046272 | tf_op jit(solution)/shard_map/absorb/pallas_call | solution.py:270
  258.2 6.9 %absorb.7 = (f32[128,3584]{1,0:T(8,128)}, f32[128,3584]{1,0:T(8,128)}) custom-call(s32[1]{0:T(128)} %bitcast.1.place_ref, bf16[8,64,896]{2,1,0:T(8,128)(2,1)} %copy-done.12, bf16[8,64,896]{2,1,0:T(8,128)(2,1)} %copy-done.13, bf16[8,96,896]{2,1,0:T(8,128)(2,1)} %copy-done.1, ...), custom_call_target="tpu_custom_call", output_to_operand_aliasing={{0}: (7, {}), {1}: (8, {})} | custom-call | flops 939524096 | bytes 3670016 | tf_op jit(solution)/shard_map/absorb/pallas_call | solution.py:270
  265.2 6.9 %absorb.8 = (f32[128,3584]{1,0:T(8,128)}, f32[128,3584]{1,0:T(8,128)}) custom-call(s32[1]{0:T(128)} %bitcast.1.place_ref, bf16[8,64,896]{2,1,0:T(8,128)(2,1)} %collective-permute-done.14.refs_0_, bf16[8,64,896]{2,1,0:T(8,128)(2,1)} %collective-permute-done.15.refs_1_, bf16[8,96,896]{2,1,0:T(8,128)(2,1)} %copy-done.2, ...), custom_call_target="tpu_custom_call", output_to_operand_aliasing={{0}: (7, {}), {1}: (8, {})} | custom-call | flops 939524096 | bytes 3670016 | tf_op jit(solution)/shard_map/absorb/pallas_call | solution.py:270
  272.1 7.1 %absorb.9 = (f32[128,3584]{1,0:T(8,128)}, f32[128,3584]{1,0:T(8,128)}) custom-call(s32[1]{0:T(128)} %bitcast.1.place_ref, bf16[8,96,896]{2,1,0:T(8,128)(2,1)} %broadcast_select_fusion.2.refs_0_, bf16[8,96,896]{2,1,0:T(8,128)(2,1)} %collective-permute-done.7.refs_1_, ...), custom_call_target="tpu_custom_call", output_to_operand_aliasing={{0}: (7, {}), {1}: (8, {})} | custom-call | flops 704643072 | bytes 2752512 | tf_op jit(solution)/shard_map/absorb/pallas_call | solution.py:270
  279.2 8.0 %finish_down.1 = (bf16[128,3584]{1,0:T(8,128)(2,1)}, bf16[32,112,128]{2,1,0:T(8,128)(2,1)}, bf16[96,3584]{1,0:T(8,128)(2,1)}, bf16[96,128]{1,0:T(8,128)(2,1)}) custom-call(s32[1]{0:T(128)} %bitcast.1.place_ref, s32[1]{0:T(128)} %bitcast.me, s32[1]{0:T(128)} %copy.32.leave, s32[32]{0:T(128)} %owner.3, bf16[8,96,896]{2,1,0:T(8,128)(2,1)} %collective-permute-done.4.refs_0_, ...), custom_call_target="tpu_custom_call" | custom-call | tf_op jit(solution)/shard_map/finish_down/pallas_call | solution.py:348
  287.2 3.6 %all-to-all-start.3 = ((bf16[16,2,112,128]{3,2,1,0:T(8,128)(2,1)}), bf16[16,2,112,128]{3,2,1,0:T(8,128)(2,1)S(1)}, u32[]{:S(2)}, u32[]{:S(2)}) async-start(bf16[16,2,112,128]{3,2,1,0:T(8,128)(2,1)} %bitcast.61), calls=%async_computation.3 | async-start | bytes 1835008 | tf_op jit(solution)/shard_map/all_to_all | solution.py:508
  290.9 5.8 %finish_up.1 = (bf16[3584,128]{1,0:T(8,128)(2,1)}, bf16[32,112,128]{2,1,0:T(8,128)(2,1)}) custom-call(s32[1]{0:T(128)} %bitcast.me, s32[1]{0:T(128)} %copy.32.leave, s32[32]{0:T(128)} %owner.3, bf16[96,3584]{1,0:T(8,128)(2,1)} %get-tuple-element.33.x_ref, bf16[96,128]{1,0:T(8,128)(2,1)} %get-tuple-element.34.pre_ref, f32[128,3584]{1,0:T(8,128)} %get-tuple-element.35.old_up, ...), custom_call_target="tpu_custom_call" | custom-call | flops 587202560 | bytes 5505024 | tf_op jit(solution)/shard_map/finish_up/pallas_call | solution.py:391
  296.7 11.0 %all-to-all-done.3 = bf16[16,2,112,128]{3,2,1,0:T(8,128)(2,1)S(1)} async-done(((bf16[16,2,112,128]{3,2,1,0:T(8,128)(2,1)}), bf16[16,2,112,128]{3,2,1,0:T(8,128)(2,1)S(1)}, u32[]{:S(2)}, u32[]{:S(2)}) %all-to-all-start.3) | async-done | bytes 917536 | tf_op jit(solution)/shard_map/all_to_all | solution.py:508
  307.7 3.6 %all-to-all-start.2 = ((bf16[16,2,112,128]{3,2,1,0:T(8,128)(2,1)}), bf16[16,2,112,128]{3,2,1,0:T(8,128)(2,1)S(1)}, u32[]{:S(2)}, u32[]{:S(2)}) async-start(bf16[16,2,112,128]{3,2,1,0:T(8,128)(2,1)} %bitcast.60), calls=%async_computation.2 | async-start | bytes 1835008 | tf_op jit(solution)/shard_map/all_to_all | solution.py:508
  311.4 4.5 %collective-permute-start.33 = (bf16[112,128]{1,0:T(8,128)(2,1)S(1)}, bf16[112,128]{1,0:T(8,128)(2,1)S(1)}, u32[]{:S(2)}, u32[]{:S(2)}) collective-permute-start(bf16[112,128]{1,0:T(8,128)(2,1)S(1)} %dynamic-slice_bitcast_fusion), channel_id=1, source_target_pairs={{0,1},{2,3},{4,5},{6,7},{8,9},{10,11},{12,13},{14,15},{16,17},{18,... | collective-permute-start | bytes 86024 | tf_op jit(solution)/shard_map/ppermute | solution.py:512
  315.9 11.2 %all-to-all-done.2 = bf16[16,2,112,128]{3,2,1,0:T(8,128)(2,1)S(1)} async-done(((bf16[16,2,112,128]{3,2,1,0:T(8,128)(2,1)}), bf16[16,2,112,128]{3,2,1,0:T(8,128)(2,1)S(1)}, u32[]{:S(2)}, u32[]{:S(2)}) %all-to-all-start.2) | async-done | bytes 917536 | tf_op jit(solution)/shard_map/all_to_all | solution.py:508
  327.1 4.4 %collective-permute-start.32 = (bf16[112,128]{1,0:T(8,128)(2,1)S(1)}, bf16[112,128]{1,0:T(8,128)(2,1)S(1)}, u32[]{:S(2)}, u32[]{:S(2)}) collective-permute-start(bf16[112,128]{1,0:T(8,128)(2,1)S(1)} %dynamic-slice_bitcast_fusion.1), channel_id=1, source_target_pairs={{0,1},{2,3},{4,5},{6,7},{8,9},{10,11},{12,13},{14,15},{16,17},{18,... | collective-permute-start | bytes 86024 | tf_op jit(solution)/shard_map/ppermute | solution.py:512
  332.1 2.8 collective-permute-done.32
  (80 shorter events, 7.9 us)
Async XLA Ops:
  4.4 23.7 %all-to-all-start = ((bf16[32,16,896]{2,1,0:T(8,128)(2,1)}), bf16[32,16,896]{2,1,0:T(8,128)(2,1)S(1)}, u32[]{:S(2)}, u32[]{:S(2)}) async-start(bf16[32,16,896]{2,1,0:T(8,128)(2,1)} %bitcast.55), calls=%async_computation | async-start | bytes 1835008 | tf_op jit(solution)/shard_map/all_to_all | solution.py:447
  28.1 25.7 %copy-start.6 = (bf16[32,16,896]{2,1,0:T(8,128)(2,1)}, bf16[32,16,896]{2,1,0:T(8,128)(2,1)S(1)}, u32[]{:S(2)}) copy-start(bf16[32,16,896]{2,1,0:T(8,128)(2,1)S(1)} %all-to-all-done) | copy-start | bytes 2752516
  57.3 40.7 %copy-start = (bf16[8,96,896]{2,1,0:T(8,128)(2,1)S(1)}, bf16[8,96,896]{2,1,0:T(8,128)(2,1)}, u32[]{:S(2)}) copy-start(bf16[8,96,896]{2,1,0:T(8,128)(2,1)} %arrange.2.refs_2_) | copy-start | bytes 4128772
  57.3 36.9 %collective-permute-start = (bf16[8,96,896]{2,1,0:T(8,128)(2,1)}, bf16[8,96,896]{2,1,0:T(8,128)(2,1)S(1)}, u32[]{:S(2)}, u32[]{:S(2)}) collective-permute-start(bf16[8,96,896]{2,1,0:T(8,128)(2,1)} %arrange.2.refs_2_), channel_id=1, source_target_pairs={{0,64},{2,66},{4,68},{6,70},{8,72},{10,74},{12,76},{14,78},{16,80}... | collective-permute-start | bytes 4128776 | tf_op jit(solution)/shard_map/ppermute | solution.py:435
  62.9 23.4 %collective-permute-start.10 = (bf16[8,64,896]{2,1,0:T(8,128)(2,1)}, bf16[8,64,896]{2,1,0:T(8,128)(2,1)}, u32[]{:S(2)}, u32[]{:S(2)}) collective-permute-start(bf16[8,64,896]{2,1,0:T(8,128)(2,1)} %arrange.3.refs_0_), channel_id=1, source_target_pairs={{0,64},{2,66},{4,68},{6,70},{8,72},{10,74},{12,76},{14,78},{16,80}... | collective-permute-start | bytes 2752520 | tf_op jit(solution)/shard_map/ppermute | solution.py:435
  63.9 28.9 %collective-permute-start.26 = (bf16[8,64,896]{2,1,0:T(8,128)(2,1)}, bf16[8,64,896]{2,1,0:T(8,128)(2,1)S(1)}, u32[]{:S(2)}, u32[]{:S(2)}) collective-permute-start(bf16[8,64,896]{2,1,0:T(8,128)(2,1)} %arrange.3.refs_0_), channel_id=1, source_target_pairs={{0,32},{2,34},{4,36},{6,38},{8,40},{10,42},{12,44},{14,46},{16,48}... | collective-permute-start | bytes 2752520 | tf_op jit(solution)/shard_map/ppermute | solution.py:438
  86.4 16.8 %collective-permute-start.11 = (bf16[8,64,896]{2,1,0:T(8,128)(2,1)}, bf16[8,64,896]{2,1,0:T(8,128)(2,1)}, u32[]{:S(2)}, u32[]{:S(2)}) collective-permute-start(bf16[8,64,896]{2,1,0:T(8,128)(2,1)} %collective-permute-done.10.refs_2_), channel_id=1, source_target_pairs={{0,64},{2,66},{4,68},{6,70},{8,72},{10,74},{12,76},{14,78},{16,80}... | collective-permute-start | bytes 2752520 | tf_op jit(solution)/shard_map/ppermute | solution.py:435
  92.9 5.2 %copy-start.10 = (bf16[8,64,896]{2,1,0:T(8,128)(2,1)}, bf16[8,64,896]{2,1,0:T(8,128)(2,1)S(1)}, u32[]{:S(2)}) copy-start(bf16[8,64,896]{2,1,0:T(8,128)(2,1)S(1)} %collective-permute-done.26.refs_1_) | copy-start | bytes 2752516
  92.9 15.3 %collective-permute-start.28 = (bf16[8,64,896]{2,1,0:T(8,128)(2,1)S(1)}, bf16[8,64,896]{2,1,0:T(8,128)(2,1)S(1)}, u32[]{:S(2)}, u32[]{:S(2)}) collective-permute-start(bf16[8,64,896]{2,1,0:T(8,128)(2,1)S(1)} %collective-permute-done.26.refs_1_), channel_id=1, source_target_pairs={{96,32},{98,34},{100,36},{102,38},{104,40},{106,42},{108,44},{110,... | collective-permute-start | bytes 2752520 | tf_op jit(solution)/shard_map/ppermute | solution.py:435
  94.2 48.3 %copy-start.7 = (bf16[8,96,896]{2,1,0:T(8,128)(2,1)}, bf16[8,96,896]{2,1,0:T(8,128)(2,1)S(1)}, u32[]{:S(2)}) copy-start(bf16[8,96,896]{2,1,0:T(8,128)(2,1)S(1)} %collective-permute-done.refs_4_) | copy-start | bytes 4128772
  94.2 23.9 %collective-permute-start.1 = (bf16[8,96,896]{2,1,0:T(8,128)(2,1)S(1)}, bf16[8,96,896]{2,1,0:T(8,128)(2,1)}, u32[]{:S(2)}, u32[]{:S(2)}) collective-permute-start(bf16[8,96,896]{2,1,0:T(8,128)(2,1)S(1)} %collective-permute-done.refs_4_), channel_id=1, source_target_pairs={{0,64},{2,66},{4,68},{6,70},{8,72},{10,74},{12,76},{14,78},{16,80}... | collective-permute-start | bytes 4128776 | tf_op jit(solution)/shard_map/ppermute | solution.py:435
  96.7 21.4 %collective-permute-start.30 = (bf16[8,64,896]{2,1,0:T(8,128)(2,1)}, bf16[8,64,896]{2,1,0:T(8,128)(2,1)}, u32[]{:S(2)}, u32[]{:S(2)}) collective-permute-start(bf16[8,64,896]{2,1,0:T(8,128)(2,1)} %collective-permute-done.10.refs_2_), channel_id=1, source_target_pairs={{96,32},{98,34},{100,36},{102,38},{104,40},{106,42},{108,44},{110,... | collective-permute-start | bytes 2752520 | tf_op jit(solution)/shard_map/ppermute | solution.py:435
  98.0 26.6 %collective-permute-start.20 = (bf16[8,96,896]{2,1,0:T(8,128)(2,1)S(1)}, bf16[8,96,896]{2,1,0:T(8,128)(2,1)}, u32[]{:S(2)}, u32[]{:S(2)}) collective-permute-start(bf16[8,96,896]{2,1,0:T(8,128)(2,1)S(1)} %copy-done), channel_id=1, source_target_pairs={{0,32},{2,34},{4,36},{6,38},{8,40},{10,42},{12,44},{14,46},{16,48}... | collective-permute-start | bytes 4128776 | tf_op jit(solution)/shard_map/ppermute | solution.py:438
  103.2 15.7 %collective-permute-start.12 = (bf16[8,64,896]{2,1,0:T(8,128)(2,1)}, bf16[8,64,896]{2,1,0:T(8,128)(2,1)}, u32[]{:S(2)}, u32[]{:S(2)}) collective-permute-start(bf16[8,64,896]{2,1,0:T(8,128)(2,1)} %collective-permute-done.11), channel_id=1, source_target_pairs={{0,64},{2,66},{4,68},{6,70},{8,72},{10,74},{12,76},{14,78},{16,80}... | collective-permute-start | bytes 2752520 | tf_op jit(solution)/shard_map/ppermute | solution.py:435
  109.1 12.4 %collective-permute-start.27 = (bf16[8,64,896]{2,1,0:T(8,128)(2,1)}, bf16[8,64,896]{2,1,0:T(8,128)(2,1)}, u32[]{:S(2)}, u32[]{:S(2)}) collective-permute-start(bf16[8,64,896]{2,1,0:T(8,128)(2,1)} %collective-permute-done.10.refs_2_), channel_id=1, source_target_pairs={{0,32},{2,34},{4,36},{6,38},{8,40},{10,42},{12,44},{14,46},{16,48}... | collective-permute-start | bytes 2752520 | tf_op jit(solution)/shard_map/ppermute | solution.py:438
  110.4 11.1 %copy-start.3 = (bf16[8,64,896]{2,1,0:T(8,128)(2,1)}, bf16[8,64,896]{2,1,0:T(8,128)(2,1)S(1)}, u32[]{:S(2)}) copy-start(bf16[8,64,896]{2,1,0:T(8,128)(2,1)S(1)} %broadcast_select_fusion.4.refs_4_) | copy-start | bytes 2752516
  118.1 7.2 %collective-permute-start.29 = (bf16[8,64,896]{2,1,0:T(8,128)(2,1)S(1)}, bf16[8,64,896]{2,1,0:T(8,128)(2,1)}, u32[]{:S(2)}, u32[]{:S(2)}) collective-permute-start(bf16[8,64,896]{2,1,0:T(8,128)(2,1)S(1)} %broadcast_select_fusion.4.refs_4_), channel_id=1, source_target_pairs={{0,32},{2,34},{4,36},{6,38},{8,40},{10,42},{12,44},{14,46},{16,48}... | collective-permute-start | bytes 2752520 | tf_op jit(solution)/shard_map/ppermute | solution.py:438
  118.1 25.7 %collective-permute-start.2 = (bf16[8,96,896]{2,1,0:T(8,128)(2,1)}, bf16[8,96,896]{2,1,0:T(8,128)(2,1)S(1)}, u32[]{:S(2)}, u32[]{:S(2)}) collective-permute-start(bf16[8,96,896]{2,1,0:T(8,128)(2,1)} %collective-permute-done.1), channel_id=1, source_target_pairs={{0,64},{2,66},{4,68},{6,70},{8,72},{10,74},{12,76},{14,78},{16,80}... | collective-permute-start | bytes 4128776 | tf_op jit(solution)/shard_map/ppermute | solution.py:435
  118.9 21.0 %collective-permute-start.23 = (bf16[8,64,896]{2,1,0:T(8,128)(2,1)}, bf16[8,64,896]{2,1,0:T(8,128)(2,1)S(1)}, u32[]{:S(2)}, u32[]{:S(2)}) collective-permute-start(bf16[8,64,896]{2,1,0:T(8,128)(2,1)} %collective-permute-done.11), channel_id=1, source_target_pairs={{96,32},{98,34},{100,36},{102,38},{104,40},{106,42},{108,44},{110,... | collective-permute-start | bytes 2752520 | tf_op jit(solution)/shard_map/ppermute | solution.py:435
  121.5 23.2 %copy-start.4 = (bf16[8,64,896]{2,1,0:T(8,128)(2,1)}, bf16[8,64,896]{2,1,0:T(8,128)(2,1)S(1)}, u32[]{:S(2)}) copy-start(bf16[8,64,896]{2,1,0:T(8,128)(2,1)S(1)} %broadcast_select_fusion.3.refs_6_) | copy-start | bytes 2752516
  121.5 19.7 %collective-permute-start.31 = (bf16[8,64,896]{2,1,0:T(8,128)(2,1)S(1)}, bf16[8,64,896]{2,1,0:T(8,128)(2,1)S(1)}, u32[]{:S(2)}, u32[]{:S(2)}) collective-permute-start(bf16[8,64,896]{2,1,0:T(8,128)(2,1)S(1)} %broadcast_select_fusion.3.refs_6_), channel_id=1, source_target_pairs={{0,32},{2,34},{4,36},{6,38},{8,40},{10,42},{12,44},{14,46},{16,48}... | collective-permute-start | bytes 2752520 | tf_op jit(solution)/shard_map/ppermute | solution.py:438
  124.5 17.9 %collective-permute-start.13 = (bf16[8,64,896]{2,1,0:T(8,128)(2,1)}, bf16[8,64,896]{2,1,0:T(8,128)(2,1)S(1)}, u32[]{:S(2)}, u32[]{:S(2)}) collective-permute-start(bf16[8,64,896]{2,1,0:T(8,128)(2,1)} %collective-permute-done.12), channel_id=1, source_target_pairs={{64,128},{66,130},{68,132},{70,134},{72,136},{74,138},{76,140},{78... | collective-permute-start | bytes 2752520 | tf_op jit(solution)/shard_map/ppermute | solution.py:435
  125.3 44.9 %collective-permute-start.25 = (bf16[8,96,896]{2,1,0:T(8,128)(2,1)S(1)}, bf16[8,96,896]{2,1,0:T(8,128)(2,1)S(1)}, u32[]{:S(2)}, u32[]{:S(2)}) collective-permute-start(bf16[8,96,896]{2,1,0:T(8,128)(2,1)S(1)} %collective-permute-done.refs_4_), channel_id=1, source_target_pairs={{0,32},{2,34},{4,36},{6,38},{8,40},{10,42},{12,44},{14,46},{16,48}... | collective-permute-start | bytes 4128776 | tf_op jit(solution)/shard_map/ppermute | solution.py:438
  139.9 30.8 %collective-permute-start.21 = (bf16[8,96,896]{2,1,0:T(8,128)(2,1)}, bf16[8,96,896]{2,1,0:T(8,128)(2,1)S(1)}, u32[]{:S(2)}, u32[]{:S(2)}) collective-permute-start(bf16[8,96,896]{2,1,0:T(8,128)(2,1)} %collective-permute-done.20.refs_3_), channel_id=1, source_target_pairs={{96,32},{98,34},{100,36},{102,38},{104,40},{106,42},{108,44},{110,... | collective-permute-start | bytes 4128776 | tf_op jit(solution)/shard_map/ppermute | solution.py:435
  141.2 28.9 %collective-permute-start.18 = (bf16[8,64,896]{2,1,0:T(8,128)(2,1)}, bf16[8,64,896]{2,1,0:T(8,128)(2,1)S(1)}, u32[]{:S(2)}, u32[]{:S(2)}) collective-permute-start(bf16[8,64,896]{2,1,0:T(8,128)(2,1)} %collective-permute-done.12), channel_id=1, source_target_pairs={{96,32},{98,34},{100,36},{102,38},{104,40},{106,42},{108,44},{110,... | collective-permute-start | bytes 2752520 | tf_op jit(solution)/shard_map/ppermute | solution.py:435
  142.5 42.4 %collective-permute-start.16 = (bf16[8,96,896]{2,1,0:T(8,128)(2,1)S(1)}, bf16[8,96,896]{2,1,0:T(8,128)(2,1)S(1)}, u32[]{:S(2)}, u32[]{:S(2)}) collective-permute-start(bf16[8,96,896]{2,1,0:T(8,128)(2,1)S(1)} %collective-permute-done.refs_4_), channel_id=1, source_target_pairs={{96,32},{98,34},{100,36},{102,38},{104,40},{106,42},{108,44},{110,... | collective-permute-start | bytes 4128776 | tf_op jit(solution)/shard_map/ppermute | solution.py:435
  143.8 42.3 %collective-permute-start.3 = (bf16[8,96,896]{2,1,0:T(8,128)(2,1)S(1)}, bf16[8,96,896]{2,1,0:T(8,128)(2,1)S(1)}, u32[]{:S(2)}, u32[]{:S(2)}) collective-permute-start(bf16[8,96,896]{2,1,0:T(8,128)(2,1)S(1)} %collective-permute-done.2), channel_id=1, source_target_pairs={{64,128},{66,130},{68,132},{70,134},{72,136},{74,138},{76,140},{78... | collective-permute-start | bytes 4128776 | tf_op jit(solution)/shard_map/ppermute | solution.py:435
  144.7 43.0 %copy-start.5 = (bf16[8,64,896]{2,1,0:T(8,128)(2,1)}, bf16[8,64,896]{2,1,0:T(8,128)(2,1)S(1)}, u32[]{:S(2)}) copy-start(bf16[8,64,896]{2,1,0:T(8,128)(2,1)S(1)} %broadcast_select_fusion.5.refs_0_) | copy-start | bytes 2752516
  170.1 19.2 %copy-start.12 = (bf16[8,64,896]{2,1,0:T(8,128)(2,1)}, bf16[8,64,896]{2,1,0:T(8,128)(2,1)S(1)}, u32[]{:S(2)}) copy-start(bf16[8,64,896]{2,1,0:T(8,128)(2,1)S(1)} %collective-permute-done.18.refs_0_) | copy-start | bytes 2752516
  170.1 17.6 %collective-permute-start.24 = (bf16[8,64,896]{2,1,0:T(8,128)(2,1)S(1)}, bf16[8,64,896]{2,1,0:T(8,128)(2,1)S(1)}, u32[]{:S(2)}, u32[]{:S(2)}) collective-permute-start(bf16[8,64,896]{2,1,0:T(8,128)(2,1)S(1)} %broadcast_select_fusion.5.refs_0_), channel_id=1, source_target_pairs={{0,32},{2,34},{4,36},{6,38},{8,40},{10,42},{12,44},{14,46},{16,48}... | collective-permute-start | bytes 2752520 | tf_op jit(solution)/shard_map/ppermute | solution.py:438
  170.1 16.0 %copy-start.8 = (bf16[8,96,896]{2,1,0:T(8,128)(2,1)}, bf16[8,96,896]{2,1,0:T(8,128)(2,1)S(1)}, u32[]{:S(2)}) copy-start(bf16[8,96,896]{2,1,0:T(8,128)(2,1)S(1)} %collective-permute-done.25.refs_5_) | copy-start | bytes 4128772
  170.1 17.7 %collective-permute-start.19 = (bf16[8,64,896]{2,1,0:T(8,128)(2,1)S(1)}, bf16[8,64,896]{2,1,0:T(8,128)(2,1)S(1)}, u32[]{:S(2)}, u32[]{:S(2)}) collective-permute-start(bf16[8,64,896]{2,1,0:T(8,128)(2,1)S(1)} %collective-permute-done.18.refs_0_), channel_id=1, source_target_pairs={{0,32},{2,34},{4,36},{6,38},{8,40},{10,42},{12,44},{14,46},{16,48}... | collective-permute-start | bytes 2752520 | tf_op jit(solution)/shard_map/ppermute | solution.py:438
  170.6 29.0 %collective-permute-start.6 = (bf16[8,96,896]{2,1,0:T(8,128)(2,1)}, bf16[8,96,896]{2,1,0:T(8,128)(2,1)S(1)}, u32[]{:S(2)}, u32[]{:S(2)}) collective-permute-start(bf16[8,96,896]{2,1,0:T(8,128)(2,1)} %collective-permute-done.1), channel_id=1, source_target_pairs={{96,32},{98,34},{100,36},{102,38},{104,40},{106,42},{108,44},{110,... | collective-permute-start | bytes 4128776 | tf_op jit(solution)/shard_map/ppermute | solution.py:435
  184.9 54.2 %collective-permute-start.8 = (bf16[8,96,896]{2,1,0:T(8,128)(2,1)S(1)}, bf16[8,96,896]{2,1,0:T(8,128)(2,1)}, u32[]{:S(2)}, u32[]{:S(2)}) collective-permute-start(bf16[8,96,896]{2,1,0:T(8,128)(2,1)S(1)} %collective-permute-done.2), channel_id=1, source_target_pairs={{96,32},{98,34},{100,36},{102,38},{104,40},{106,42},{108,44},{110,... | collective-permute-start | bytes 4128776 | tf_op jit(solution)/shard_map/ppermute | solution.py:435
  186.2 53.4 %collective-permute-start.4 = (bf16[8,96,896]{2,1,0:T(8,128)(2,1)S(1)}, bf16[8,96,896]{2,1,0:T(8,128)(2,1)}, u32[]{:S(2)}, u32[]{:S(2)}) collective-permute-start(bf16[8,96,896]{2,1,0:T(8,128)(2,1)S(1)} %collective-permute-done.3), channel_id=1, source_target_pairs={{96,32},{98,34},{100,36},{102,38},{104,40},{106,42},{108,44},{110,... | collective-permute-start | bytes 4128776 | tf_op jit(solution)/shard_map/ppermute | solution.py:435
  187.7 51.9 %collective-permute-start.22 = (bf16[8,96,896]{2,1,0:T(8,128)(2,1)S(1)}, bf16[8,96,896]{2,1,0:T(8,128)(2,1)S(1)}, u32[]{:S(2)}, u32[]{:S(2)}) collective-permute-start(bf16[8,96,896]{2,1,0:T(8,128)(2,1)S(1)} %broadcast_select_fusion.refs_2_), channel_id=1, source_target_pairs={{0,32},{2,34},{4,36},{6,38},{8,40},{10,42},{12,44},{14,46},{16,48}... | collective-permute-start | bytes 4128776 | tf_op jit(solution)/shard_map/ppermute | solution.py:438
  187.8 51.2 %collective-permute-start.14 = (bf16[8,64,896]{2,1,0:T(8,128)(2,1)S(1)}, bf16[8,64,896]{2,1,0:T(8,128)(2,1)}, u32[]{:S(2)}, u32[]{:S(2)}) collective-permute-start(bf16[8,64,896]{2,1,0:T(8,128)(2,1)S(1)} %collective-permute-done.13), channel_id=1, source_target_pairs={{96,32},{98,34},{100,36},{102,38},{104,40},{106,42},{108,44},{110,... | collective-permute-start | bytes 2752520 | tf_op jit(solution)/shard_map/ppermute | solution.py:435
  189.4 11.5 %copy-start.2 = (bf16[8,96,896]{2,1,0:T(8,128)(2,1)}, bf16[8,96,896]{2,1,0:T(8,128)(2,1)S(1)}, u32[]{:S(2)}) copy-start(bf16[8,96,896]{2,1,0:T(8,128)(2,1)S(1)} %broadcast_select_fusion.1.refs_2_) | copy-start | bytes 4128772
  199.6 65.5 %collective-permute-start.17 = (bf16[8,96,896]{2,1,0:T(8,128)(2,1)S(1)}, bf16[8,96,896]{2,1,0:T(8,128)(2,1)}, u32[]{:S(2)}, u32[]{:S(2)}) collective-permute-start(bf16[8,96,896]{2,1,0:T(8,128)(2,1)S(1)} %broadcast_select_fusion.1.refs_2_), channel_id=1, source_target_pairs={{0,32},{2,34},{4,36},{6,38},{8,40},{10,42},{12,44},{14,46},{16,48}... | collective-permute-start | bytes 4128776 | tf_op jit(solution)/shard_map/ppermute | solution.py:438
  239.0 33.0 %collective-permute-start.7 = (bf16[8,96,896]{2,1,0:T(8,128)(2,1)}, bf16[8,96,896]{2,1,0:T(8,128)(2,1)}, u32[]{:S(2)}, u32[]{:S(2)}) collective-permute-start(bf16[8,96,896]{2,1,0:T(8,128)(2,1)} %broadcast_select_fusion.2.refs_0_), channel_id=1, source_target_pairs={{0,32},{2,34},{4,36},{6,38},{8,40},{10,42},{12,44},{14,46},{16,48}... | collective-permute-start | bytes 4128776 | tf_op jit(solution)/shard_map/ppermute | solution.py:438
  239.0 33.0 %collective-permute-start.9 = (bf16[8,96,896]{2,1,0:T(8,128)(2,1)}, bf16[8,96,896]{2,1,0:T(8,128)(2,1)}, u32[]{:S(2)}, u32[]{:S(2)}) collective-permute-start(bf16[8,96,896]{2,1,0:T(8,128)(2,1)} %collective-permute-done.8.refs_2_), channel_id=1, source_target_pairs={{0,32},{2,34},{4,36},{6,38},{8,40},{10,42},{12,44},{14,46},{16,48}... | collective-permute-start | bytes 4128776 | tf_op jit(solution)/shard_map/ppermute | solution.py:438
  239.5 39.7 %collective-permute-start.5 = (bf16[8,96,896]{2,1,0:T(8,128)(2,1)}, bf16[8,96,896]{2,1,0:T(8,128)(2,1)}, u32[]{:S(2)}, u32[]{:S(2)}) collective-permute-start(bf16[8,96,896]{2,1,0:T(8,128)(2,1)} %collective-permute-done.4.refs_0_), channel_id=1, source_target_pairs={{0,32},{2,34},{4,36},{6,38},{8,40},{10,42},{12,44},{14,46},{16,48}... | collective-permute-start | bytes 4128776 | tf_op jit(solution)/shard_map/ppermute | solution.py:438
  239.6 10.0 %copy-start.9 = (bf16[8,96,896]{2,1,0:T(8,128)(2,1)}, bf16[8,96,896]{2,1,0:T(8,128)(2,1)S(1)}, u32[]{:S(2)}) copy-start(bf16[8,96,896]{2,1,0:T(8,128)(2,1)S(1)} %collective-permute-done.22.refs_3_) | copy-start | bytes 4128772
  239.6 25.5 %collective-permute-start.15 = (bf16[8,64,896]{2,1,0:T(8,128)(2,1)}, bf16[8,64,896]{2,1,0:T(8,128)(2,1)}, u32[]{:S(2)}, u32[]{:S(2)}) collective-permute-start(bf16[8,64,896]{2,1,0:T(8,128)(2,1)} %collective-permute-done.14.refs_0_), channel_id=1, source_target_pairs={{0,32},{2,34},{4,36},{6,38},{8,40},{10,42},{12,44},{14,46},{16,48}... | collective-permute-start | bytes 2752520 | tf_op jit(solution)/shard_map/ppermute | solution.py:438
  287.2 20.5 %all-to-all-start.3 = ((bf16[16,2,112,128]{3,2,1,0:T(8,128)(2,1)}), bf16[16,2,112,128]{3,2,1,0:T(8,128)(2,1)S(1)}, u32[]{:S(2)}, u32[]{:S(2)}) async-start(bf16[16,2,112,128]{3,2,1,0:T(8,128)(2,1)} %bitcast.61), calls=%async_computation.3 | async-start | bytes 1835008 | tf_op jit(solution)/shard_map/all_to_all | solution.py:508
  307.7 19.4 %all-to-all-start.2 = ((bf16[16,2,112,128]{3,2,1,0:T(8,128)(2,1)}), bf16[16,2,112,128]{3,2,1,0:T(8,128)(2,1)S(1)}, u32[]{:S(2)}, u32[]{:S(2)}) async-start(bf16[16,2,112,128]{3,2,1,0:T(8,128)(2,1)} %bitcast.60), calls=%async_computation.2 | async-start | bytes 1835008 | tf_op jit(solution)/shard_map/all_to_all | solution.py:508
  311.4 20.0 %collective-permute-start.33 = (bf16[112,128]{1,0:T(8,128)(2,1)S(1)}, bf16[112,128]{1,0:T(8,128)(2,1)S(1)}, u32[]{:S(2)}, u32[]{:S(2)}) collective-permute-start(bf16[112,128]{1,0:T(8,128)(2,1)S(1)} %dynamic-slice_bitcast_fusion), channel_id=1, source_target_pairs={{0,1},{2,3},{4,5},{6,7},{8,9},{10,11},{12,13},{14,15},{16,17},{18,... | collective-permute-start | bytes 86024 | tf_op jit(solution)/shard_map/ppermute | solution.py:512
  327.1 7.8 %collective-permute-start.32 = (bf16[112,128]{1,0:T(8,128)(2,1)S(1)}, bf16[112,128]{1,0:T(8,128)(2,1)S(1)}, u32[]{:S(2)}, u32[]{:S(2)}) collective-permute-start(bf16[112,128]{1,0:T(8,128)(2,1)S(1)} %dynamic-slice_bitcast_fusion.1), channel_id=1, source_target_pairs={{0,1},{2,3},{4,5},{6,7},{8,9},{10,11},{12,13},{14,15},{16,17},{18,... | collective-permute-start | bytes 86024 | tf_op jit(solution)/shard_map/ppermute | solution.py:512
  (5 other events, 8.4 us)

commit v4 on v3

--- a/solution.py
+++ b/solution.py
@@ -14,8 +14,8 @@
 ALL = ("zl", "co", "y", "x", "zh")
 SLOT_GROUPS = ((0, 2), (2, 3))
 TAGS = ("a", "b")
-SUMS = ("ao1p2q3r", "a4 bo1p", "a5 b2q", "a6 b3r", "b45")
-LAST = "b6"
+SUMS = ("ao1p2q3r", "a4 bo1p", "a5 b2q", "a6 b3r4")
+LAST = "b56"
 PIECES = 4
 VMEM = pl.BlockSpec(memory_space=pltpu.VMEM)
 SMEM = pl.BlockSpec(memory_space=pltpu.SMEM)
@@ -297,114 +297,150 @@
 def adam_step(gradient, moment_one, moment_two):
     new_one = BETA_ONE * moment_one.astype(jnp.float32) + (1.0 - BETA_ONE) * gradient
     new_two = BETA_TWO * moment_two.astype(jnp.float32) + (1.0 - BETA_TWO) * gradient * gradient
-    return new_one / (jnp.sqrt(new_two) + EPSILON)
-
-
-def finish_down(place, my_index, leaving, tile_owner, blocks, w_up, w_down, old, m_down, v_down):
+    return new_one / (new_two * lax.rsqrt(new_two) + EPSILON)
+
+
+def pick_copies(at, blocks, refs, targets, sems):
+    starts, waits, refs = [], [], list(refs)
+    for i, (test, _, second) in enumerate(blocks):
+        first_ref = refs.pop(0)
+        here = pltpu.make_async_copy(first_ref, targets[i], sems.at[i])
+        waits.append(here)
+        if second is None:
+            starts.append(here.start)
+            continue
+        there = pltpu.make_async_copy(refs.pop(0), targets[i], sems.at[i])
+
+        def start(here=here, there=there, test=test):
+            pl.when(test(at))(here.start)
+            pl.when(jnp.logical_not(test(at)))(there.start)
+
+        starts.append(start)
+    return starts, waits
+
+
+def lay_rows(blocks_vmem, held, first_part):
+    piece = blocks_vmem[0].shape[2]
+    offset = 0
+    for ref in blocks_vmem:
+        count = ref.shape[1]
+        for q in range(PIECES):
+            held[offset : offset + count, q * piece : (q + 1) * piece] = ref[first_part + q]
+        offset += count
+
+
+def finish(place, half, my_index, leaving, tile_owner, blocks, w_up, w_down, sums, moments):
     arrays = flatten(blocks)
     width, hidden_units = w_up.shape
     tiles = tile_owner.shape[0]
     tile_rows = width // tiles
     total = sum(first.shape[1] for _, first, _ in blocks)
     step = width // PIECES
-
-    count = len(arrays)
-
-    def body(place_ref, me, leave, owner, *refs):
-        hbm_in, refs = refs[: count + 5], refs[count + 5 :]
-        out_down, out_tiles, out_x, out_pre = refs[:4]
-        vmem_in, refs = refs[4 : count + 9], refs[count + 9 :]
-        both, held_c, held_hid, sems = refs
-        copies = [
-            pltpu.make_async_copy(source, target, sems.at[i])
-            for i, (source, target) in enumerate(zip(hbm_in, vmem_in))
+    each = tiles // PIECES
+    count = len(blocks)
+    rest = (w_up, w_down, sums[1], moments[2], moments[3], sums[0], moments[0], moments[1])
+
+    def body(place_ref, half_ref, me, leave, owner, *refs):
+        rows_in, refs = refs[: len(arrays)], refs[len(arrays) :]
+        rest_in, refs = refs[: len(rest)], refs[len(rest) :]
+        out_up, out_down, out_near, out_far = refs[:4]
+        refs = refs[4:]
+        rows_vmem, refs = refs[:count], refs[count:]
+        rest_vmem, refs = refs[: len(rest)], refs[len(rest) :]
+        up_ref, down_ref, old_down, md, vd, old_up, mu, vu = rest_vmem
+        moved_up, moved_down, both, held_x, held_c, held_pre, held_hid = refs[:7]
+        sems, up_sems, down_sems, tile_sems = refs[7:]
+        starts, waits = pick_copies(place_ref[0], blocks, rows_in, rows_vmem, sems)
+        others = [
+            pltpu.make_async_copy(source, target, sems.at[count + i])
+            for i, (source, target) in enumerate(zip(rest_in, rest_vmem))
         ]
-        for copy in copies:
+        for start in starts:
+            start()
+        for copy in others:
             copy.start()
         keep = me[0] != leave[0]
-        for copy in copies[:count]:
+        for copy in waits:
             copy.wait()
-        gather_rows(place_ref[0], blocks, vmem_in[:count], out_x, held_c)
-        up_ref, down_ref, old_down, md, vd = vmem_in[count:]
-        for copy in copies[count : count + 2]:
+        lay_rows(rows_vmem, held_x, 0)
+        lay_rows(rows_vmem, held_c, PIECES)
+        for copy in others[:2]:
             copy.wait()
-        row_terms(up_ref, down_ref, out_x, held_c, out_pre, held_hid, total)
-        for copy in copies[count + 2 :]:
+        row_terms(up_ref, down_ref, held_x, held_c, held_pre, held_hid, total)
+        for copy in others[2:]:
             copy.wait()
+
+        def leave_steps(j):
+            span = pl.ds(pl.multiple_of(j * step, step), step)
+            return (
+                pltpu.make_async_copy(moved_up.at[span, :], out_up.at[span, :], up_sems.at[j]),
+                pltpu.make_async_copy(moved_down.at[:, span], out_down.at[:, span], down_sems.at[j]),
+            )
+
+        def tile_copy(t, out):
+            span = pl.ds(pl.multiple_of(t * tile_rows, tile_rows), tile_rows)
+            return pltpu.make_async_copy(
+                both.at[span, :], out.at[owner[t] >> 1], tile_sems.at[t]
+            )
 
         def columns(j, carry):
             span = pl.ds(pl.multiple_of(j * step, step), step)
             grad = old_down[:, span] + column_sums(held_hid[...], held_c[:, span])
             step_down = adam_step(grad, md[:, span], vd[:, span])
-            both[span, :] = step_down.T.astype(jnp.bfloat16)
-            out_down[:, span] = jnp.where(keep, step_down, 0.0).astype(jnp.bfloat16)
+            both[span, hidden_units:] = step_down.T.astype(jnp.bfloat16)
+            moved_down[:, span] = jnp.where(keep, step_down, 0.0).astype(jnp.bfloat16)
+            grad = old_up[:, span] + column_sums(held_pre[...], held_x[:, span])
+            step_up = adam_step(grad.T, mu[span, :], vu[span, :])
+            both[span, :hidden_units] = step_up.astype(jnp.bfloat16)
+            moved_up[span, :] = jnp.where(keep, step_up, 0.0).astype(jnp.bfloat16)
+            for k in range(each):
+                t = j * each + k
+                near = (owner[t] & 1) == half_ref[0]
+                pl.when(near)(tile_copy(t, out_near).start)
+                pl.when(jnp.logical_not(near))(tile_copy(t, out_far).start)
+            for copy in leave_steps(j):
+                copy.start()
             return carry
 
-        lax.fori_loop(0, width // step, columns, 0)
-        for t in range(tiles):
-            out_tiles[owner[t]] = both[t * tile_rows : (t + 1) * tile_rows, :]
-
-    args = (*arrays, w_up, w_down, old, m_down, v_down)
-    return pl.pallas_call(
-        body,
-        out_shape=[
-            jax.ShapeDtypeStruct((hidden_units, width), jnp.bfloat16),
-            jax.ShapeDtypeStruct((tiles, tile_rows, hidden_units), jnp.bfloat16),
-            jax.ShapeDtypeStruct((total, width), jnp.bfloat16),
-            jax.ShapeDtypeStruct((total, hidden_units), jnp.bfloat16),
-        ],
-        in_specs=[SMEM] * 4 + [HBM] * len(args),
-        out_specs=[VMEM] * 4,
-        scratch_shapes=[pltpu.VMEM(a.shape, a.dtype) for a in args]
-        + [
-            pltpu.VMEM((width, hidden_units), jnp.bfloat16),
-            pltpu.VMEM((total, width), jnp.bfloat16),
-            pltpu.VMEM((total, hidden_units), jnp.bfloat16),
-            pltpu.SemaphoreType.DMA((len(args),)),
-        ],
-        compiler_params=pltpu.CompilerParams(vmem_limit_bytes=LIMIT),
-        name="finish_down",
-    )(place, my_index, leaving, tile_owner, *args)
-
-
-def finish_up(my_index, leaving, tile_owner, rows_x, pre_grad, old, m_up, v_up):
-    width, hidden_units = m_up.shape
-    tiles = tile_owner.shape[0]
-    tile_rows = width // tiles
-    step = width // PIECES
-
-    def body(me, leave, owner, x_ref, pre_ref, old_up, mu, vu, out_up, out_tiles, both):
-        keep = me[0] != leave[0]
-
-        def columns(j, carry):
-            span = pl.ds(pl.multiple_of(j * step, step), step)
-            grad = old_up[:, span] + column_sums(pre_ref[...], x_ref[:, span])
-            step_up = adam_step(grad.T, mu[span, :], vu[span, :])
-            both[span, :] = step_up.astype(jnp.bfloat16)
-            out_up[span, :] = jnp.where(keep, step_up, 0.0).astype(jnp.bfloat16)
+        def drain(j, carry):
+            for copy in leave_steps(j):
+                copy.wait()
+            for k in range(each):
+                tile_copy(j * each + k, out_near).wait()
             return carry
 
-        lax.fori_loop(0, width // step, columns, 0)
-        for t in range(tiles):
-            out_tiles[owner[t]] = both[t * tile_rows : (t + 1) * tile_rows, :]
-
+        lax.fori_loop(0, PIECES, columns, 0)
+        lax.fori_loop(0, PIECES, drain, 0)
+
+    tile_shape = jax.ShapeDtypeStruct((tiles // 2, tile_rows, 2 * hidden_units), jnp.bfloat16)
     return pl.pallas_call(
         body,
         out_shape=[
             jax.ShapeDtypeStruct((width, hidden_units), jnp.bfloat16),
-            jax.ShapeDtypeStruct((tiles, tile_rows, hidden_units), jnp.bfloat16),
+            jax.ShapeDtypeStruct((hidden_units, width), jnp.bfloat16),
+            tile_shape,
+            tile_shape,
         ],
-        in_specs=[SMEM] * 3 + [VMEM] * 5,
-        out_specs=[VMEM] * 2,
-        scratch_shapes=[pltpu.VMEM((width, hidden_units), jnp.bfloat16)],
+        in_specs=[SMEM] * 5 + [HBM] * (len(arrays) + len(rest)),
+        out_specs=[HBM] * 4,
+        scratch_shapes=[pltpu.VMEM(first.shape, first.dtype) for _, first, _ in blocks]
+        + [pltpu.VMEM(a.shape, a.dtype) for a in rest]
+        + [
+            pltpu.VMEM((width, hidden_units), jnp.bfloat16),
+            pltpu.VMEM((hidden_units, width), jnp.bfloat16),
+            pltpu.VMEM((width, 2 * hidden_units), jnp.bfloat16),
+            pltpu.VMEM((total, width), jnp.bfloat16),
+            pltpu.VMEM((total, width), jnp.bfloat16),
+            pltpu.VMEM((total, hidden_units), jnp.bfloat16),
+            pltpu.VMEM((total, hidden_units), jnp.bfloat16),
+            pltpu.SemaphoreType.DMA((count + len(rest),)),
+            pltpu.SemaphoreType.DMA((PIECES,)),
+            pltpu.SemaphoreType.DMA((PIECES,)),
+            pltpu.SemaphoreType.DMA((tiles,)),
+        ],
         compiler_params=pltpu.CompilerParams(vmem_limit_bytes=LIMIT),
-        cost_estimate=pl.CostEstimate(
-            flops=8 * 160 * width * hidden_units,
-            transcendentals=0,
-            bytes_accessed=12 * width * hidden_units,
-        ),
-        name="finish_up",
-    )(my_index, leaving, tile_owner, rows_x, pre_grad, old, m_up, v_up)
+        name="finish",
+    )(place, half, my_index, leaving, tile_owner, *arrays, *rest)
 
 
 def on_device(
@@ -503,33 +539,30 @@
     my_index = (column * 2 + half).reshape(1)
     leaver = leaving[0]
 
-    def adopt(tiles):
-        _, rows, units = tiles.shape
-        incoming = lax.all_to_all(tiles.reshape(16, 2, rows, units), ("y", "x"), 0, 0, tiled=True)
-        pair = lax.dynamic_index_in_dim(incoming, leaver // 2, 0, keepdims=False)
-        own = lax.dynamic_index_in_dim(pair, half, 0, keepdims=False)
-        other = lax.dynamic_index_in_dim(pair, 1 - half, 0, keepdims=False)
-        crossed = lax.ppermute(other, ALL, across_pairs())
-        return jnp.where(half == leaver % 2, own, crossed)[None]
-
-    update_down, tiles_down, rows_x, pre_grad = finish_down(
+    update_up, update_down, near, far = finish(
         place_ref,
+        half.reshape(1),
         my_index,
         leaving,
         tile_owner,
         blocks_of(LAST),
         w_up[0],
         w_down[0],
-        sums[1],
-        m_down[0],
-        v_down[0],
+        sums,
+        (m_up[0], v_up[0], m_down[0], v_down[0]),
     )
-    adopted_down = adopt(tiles_down)
-    update_up, tiles_up = finish_up(
-        my_index, leaving, tile_owner, rows_x, pre_grad, sums[0], m_up[0], v_up[0]
-    )
-    adopted_up = adopt(tiles_up)
-    return (update_up[None], update_down[None], adopted_up, adopted_down)
+
+    def from_leaver(tiles):
+        incoming = lax.all_to_all(tiles, ("y", "x"), 0, 0, tiled=True)
+        return lax.dynamic_index_in_dim(incoming, leaver // 2, 0, keepdims=False)
+
+    far, near = lax.optimization_barrier((far, near))
+    far = from_leaver(far)
+    crossed = lax.ppermute(far, ALL, across_pairs())
+    near = from_leaver(near)
+    mine = jnp.where(half == leaver % 2, near, crossed)[None]
+    units = w_up.shape[2]
+    return (update_up[None], update_down[None], mine[..., :units], mine[..., units:])
 
 
 def solution(mesh):

time: 336 us -> 312 us (0.929)
  the two profiles are of different devices: /device:TPU:96 before, /device:TPU:224 now
where the time goes in v4:
time: 312 us; the launch traced here: 311 us
  waiting for transfers between devices  163 us (52%)
  starting transfers between devices  59.3 us (19%)
  Pallas kernels  56.6 us (18%)
  blocking collectives  19.9 us (6%)
  local copies, waits for them, and re-layouts  6.11 us (2%)
  other arithmetic  4.45 us (1%)
    ppermute x18, waiting for transfers between devices, step(): return lax.ppermute(value, ALL, stream_pairs(places))  117 us
    pallas_call x4, Pallas kernels, absorb(): pl.pallas_call(body, out_shape=[shape, shape], in_specs=[SMEM] + [HBM] *...  32.7 us
    all_to_all x2, waiting for transfers between devices, on_device(): lax.all_to_all(sent.reshape(32, rows // 32, piece), ('co', 'y', 'x'), 0,...  30.6 us
    ppermute x18, starting transfers between devices, step(): return lax.ppermute(value, ALL, stream_pairs(places))  25.9 us
    all_to_all x1, blocking collectives, from_leaver(): incoming = lax.all_to_all(tiles, ('y', 'x'), 0, 0, tiled=True)  19.9 us
    ppermute x14, starting transfers between devices, swap(): return lax.ppermute(value, ALL, swap_pairs())  17.8 us
    all_to_all x1, waiting for transfers between devices, from_leaver(): incoming = lax.all_to_all(tiles, ('y', 'x'), 0, 0, tiled=True)  14.5 us
    all_to_all x2, starting transfers between devices, on_device(): lax.all_to_all(sent.reshape(32, rows // 32, piece), ('co', 'y', 'x'), 0,...  11.3 us
  transfers between devices with their start and end apart: 36, of which 13 were waited for; matrix products, arithmetic and copies ran while one was open for 1% of the time, Pallas kernels for 14%

profile of v4, /device:TPU:224, one launch (start us, length us, event | category | flops | bytes accessed | tf_op | source)
XLA Modules:
  0.0 310.6 jit_solution(12314190194922023953)
XLA Ops:
  0.6 3.7 %prepare.2 = bf16[512,896]{1,0:T(8,128)(2,1)} custom-call(s32[1]{0:T(128)} %bitcast.3.base_ref, bf16[128,3584]{1,0:T(8,128)(2,1)} %x_ref.3, bf16[128,3584]{1,0:T(8,128)(2,1)} %c_ref.3, f32[1,128]{1,0:T(1,128)} %bitcast.49, s32[1,128]{1,0:T(1,128)} %bitcast.51), custom_call_target="tpu_custom_call" | custom-call | tf_op jit(solution)/shard_map/prepare/pallas_call | solution.py:105
  4.4 7.3 %all-to-all-start = ((bf16[32,16,896]{2,1,0:T(8,128)(2,1)}), bf16[32,16,896]{2,1,0:T(8,128)(2,1)S(1)}, u32[]{:S(2)}, u32[]{:S(2)}) async-start(bf16[32,16,896]{2,1,0:T(8,128)(2,1)} %bitcast.44), calls=%async_computation | async-start | bytes 1835008 | tf_op jit(solution)/shard_map/all_to_all | solution.py:483
  11.7 4.5 %prepare.3 = bf16[768,896]{1,0:T(8,128)(2,1)} custom-call(s32[1]{0:T(128)} %bitcast.3.base_ref, bf16[128,3584]{1,0:T(8,128)(2,1)} %x_ref.3, bf16[128,3584]{1,0:T(8,128)(2,1)} %c_ref.3, f32[1,128]{1,0:T(1,128)} %bitcast.50, s32[1,128]{1,0:T(1,128)} %bitcast.52), custom_call_target="tpu_custom_call" | custom-call | tf_op jit(solution)/shard_map/prepare/pallas_call | solution.py:105
  16.3 11.8 %all-to-all-done = bf16[32,16,896]{2,1,0:T(8,128)(2,1)S(1)} async-done(((bf16[32,16,896]{2,1,0:T(8,128)(2,1)}), bf16[32,16,896]{2,1,0:T(8,128)(2,1)S(1)}, u32[]{:S(2)}, u32[]{:S(2)}) %all-to-all-start) | async-done | bytes 917536 | tf_op jit(solution)/shard_map/all_to_all | solution.py:483
  29.0 4.0 %all-to-all-start.1 = ((bf16[32,24,896]{2,1,0:T(8,128)(2,1)}), bf16[32,24,896]{2,1,0:T(8,128)(2,1)S(1)}, u32[]{:S(2)}, u32[]{:S(2)}) async-start(bf16[32,24,896]{2,1,0:T(8,128)(2,1)} %bitcast.41), calls=%async_computation.1 | async-start | bytes 2752512 | tf_op jit(solution)/shard_map/all_to_all | solution.py:483
  33.0 2.5 arrange.3.refs_0_
  35.5 18.7 %all-to-all-done.1 = bf16[32,24,896]{2,1,0:T(8,128)(2,1)S(1)} async-done(((bf16[32,24,896]{2,1,0:T(8,128)(2,1)}), bf16[32,24,896]{2,1,0:T(8,128)(2,1)S(1)}, u32[]{:S(2)}, u32[]{:S(2)}) %all-to-all-start.1) | async-done | bytes 1376288 | tf_op jit(solution)/shard_map/all_to_all | solution.py:483
  54.2 1.1 copy-done.2
  55.4 3.5 %arrange.2.refs_2_ = bf16[8,96,896]{2,1,0:T(8,128)(2,1)} custom-call(bf16[768,896]{1,0:T(8,128)(2,1)} %bitcast.42), custom_call_target="tpu_custom_call" | custom-call | tf_op jit(solution)/shard_map/arrange/pallas_call | solution.py:147
  58.9 4.8 %collective-permute-start.9 = (bf16[8,64,896]{2,1,0:T(8,128)(2,1)}, bf16[8,64,896]{2,1,0:T(8,128)(2,1)}, u32[]{:S(2)}, u32[]{:S(2)}) collective-permute-start(bf16[8,64,896]{2,1,0:T(8,128)(2,1)} %collective-permute-done.8.refs_2_), channel_id=1, source_target_pairs={{0,64},{2,66},{4,68},{6,70},{8,72},{10,74},{12,76},{14,78},{16,80}... | collective-permute-start | bytes 2752520 | tf_op jit(solution)/shard_map/ppermute | solution.py:471
  63.7 1.3 collective-permute-start.28
  65.0 12.4 %collective-permute-done.refs_4_ = bf16[8,96,896]{2,1,0:T(8,128)(2,1)S(1)} collective-permute-done((bf16[8,96,896]{2,1,0:T(8,128)(2,1)}, bf16[8,96,896]{2,1,0:T(8,128)(2,1)S(1)}, u32[]{:S(2)}, u32[]{:S(2)}) %collective-permute-start) | collective-permute-done | bytes 1376288 | tf_op jit(solution)/shard_map/ppermute | solution.py:471
  77.4 4.3 %collective-permute-start.1 = (bf16[8,96,896]{2,1,0:T(8,128)(2,1)S(1)}, bf16[8,96,896]{2,1,0:T(8,128)(2,1)}, u32[]{:S(2)}, u32[]{:S(2)}) collective-permute-start(bf16[8,96,896]{2,1,0:T(8,128)(2,1)S(1)} %collective-permute-done.refs_4_), channel_id=1, source_target_pairs={{0,64},{2,66},{4,68},{6,70},{8,72},{10,74},{12,76},{14,78},{16,80}... | collective-permute-start | bytes 4128776 | tf_op jit(solution)/shard_map/ppermute | solution.py:471
  81.7 1.3 collective-permute-start.30
  83.0 1.9 collective-permute-done.9
  84.9 1.6 collective-permute-start.10
  86.5 2.7 collective-permute-start.20
  89.2 0.9 copy-done.18
  90.1 1.3 broadcast_select_fusion.4.refs_4_
  91.4 5.9 %collective-permute-done.30 = bf16[8,64,896]{2,1,0:T(8,128)(2,1)} collective-permute-done((bf16[8,64,896]{2,1,0:T(8,128)(2,1)}, bf16[8,64,896]{2,1,0:T(8,128)(2,1)}, u32[]{:S(2)}, u32[]{:S(2)}) %collective-permute-start.30) | collective-permute-done | bytes 917536 | tf_op jit(solution)/shard_map/ppermute | solution.py:471
  97.3 1.3 collective-permute-start.23
  98.6 0.9 collective-permute-done.1
  100.3 1.3 broadcast_select_fusion.3.refs_6_
  101.6 13.4 %collective-permute-start.31 = (bf16[8,64,896]{2,1,0:T(8,128)(2,1)S(1)}, bf16[8,64,896]{2,1,0:T(8,128)(2,1)S(1)}, u32[]{:S(2)}, u32[]{:S(2)}) collective-permute-start(bf16[8,64,896]{2,1,0:T(8,128)(2,1)S(1)} %broadcast_select_fusion.3.refs_6_), channel_id=1, source_target_pairs={{0,32},{2,34},{4,36},{6,38},{8,40},{10,42},{12,44},{14,46},{16,48}... | collective-permute-start | bytes 2752520 | tf_op jit(solution)/shard_map/ppermute | solution.py:474
  115.9 9.9 %collective-permute-done.23 = bf16[8,64,896]{2,1,0:T(8,128)(2,1)S(1)} collective-permute-done((bf16[8,64,896]{2,1,0:T(8,128)(2,1)}, bf16[8,64,896]{2,1,0:T(8,128)(2,1)S(1)}, u32[]{:S(2)}, u32[]{:S(2)}) %collective-permute-start.23) | collective-permute-done | bytes 917536 | tf_op jit(solution)/shard_map/ppermute | solution.py:471
  125.8 1.3 collective-permute-start.18
  127.1 1.3 collective-permute-start.21
  129.2 1.3 collective-permute-start.14
  130.5 10.8 %collective-permute-done.18.refs_0_ = bf16[8,64,896]{2,1,0:T(8,128)(2,1)S(1)} collective-permute-done((bf16[8,64,896]{2,1,0:T(8,128)(2,1)}, bf16[8,64,896]{2,1,0:T(8,128)(2,1)S(1)}, u32[]{:S(2)}, u32[]{:S(2)}) %collective-permute-start.18) | collective-permute-done | bytes 917536 | tf_op jit(solution)/shard_map/ppermute | solution.py:471
  141.3 1.5 collective-permute-start.16
  143.0 13.0 %collective-permute-done.21 = bf16[8,96,896]{2,1,0:T(8,128)(2,1)S(1)} collective-permute-done((bf16[8,96,896]{2,1,0:T(8,128)(2,1)S(1)}, bf16[8,96,896]{2,1,0:T(8,128)(2,1)S(1)}, u32[]{:S(2)}, u32[]{:S(2)}) %collective-permute-start.21) | collective-permute-done | bytes 1376288 | tf_op jit(solution)/shard_map/ppermute | solution.py:471
  156.0 1.3 collective-permute-start.3
  157.3 1.3 collective-permute-start.6
  158.9 11.9 %collective-permute-done.14 = bf16[8,96,896]{2,1,0:T(8,128)(2,1)S(1)} collective-permute-done((bf16[8,96,896]{2,1,0:T(8,128)(2,1)S(1)}, bf16[8,96,896]{2,1,0:T(8,128)(2,1)S(1)}, u32[]{:S(2)}, u32[]{:S(2)}) %collective-permute-start.14) | collective-permute-done | bytes 1376288 | tf_op jit(solution)/shard_map/ppermute | solution.py:471
  171.3 14.2 %collective-permute-done.16 = bf16[8,96,896]{2,1,0:T(8,128)(2,1)S(1)} collective-permute-done((bf16[8,96,896]{2,1,0:T(8,128)(2,1)}, bf16[8,96,896]{2,1,0:T(8,128)(2,1)S(1)}, u32[]{:S(2)}, u32[]{:S(2)}) %collective-permute-start.16) | collective-permute-done | bytes 1376288 | tf_op jit(solution)/shard_map/ppermute | solution.py:471
  185.5 1.3 collective-permute-start.12
  187.0 1.4 broadcast_select_fusion.1.refs_4_
  188.6 36.3 %collective-permute-done.12.refs_0_ = bf16[8,64,896]{2,1,0:T(8,128)(2,1)} collective-permute-done((bf16[8,64,896]{2,1,0:T(8,128)(2,1)S(1)}, bf16[8,64,896]{2,1,0:T(8,128)(2,1)}, u32[]{:S(2)}, u32[]{:S(2)}) %collective-permute-start.12) | collective-permute-done | bytes 917536 | tf_op jit(solution)/shard_map/ppermute | solution.py:471
  225.6 1.1 copy-done.12
  227.8 8.8 %absorb.4 = (f32[128,3584]{1,0:T(8,128)}, f32[128,3584]{1,0:T(8,128)}) custom-call(s32[1]{0:T(128)} %bitcast.place_ref, bf16[8,64,896]{2,1,0:T(8,128)(2,1)} %arrange.3.refs_0_, bf16[8,64,896]{2,1,0:T(8,128)(2,1)} %copy-done.13, bf16[8,64,896]{2,1,0:T(8,128)(2,1)} %collective-permute-done.8.refs_2_, bf16[8,64,896]{2,1,0:T(8,128)(2,1)} %collective-permute-done.27.refs_3_, ...), custom_call_target="tpu_custom_call" | custom-call | flops 1644167168 | bytes 6422528 | tf_op jit(solution)/shard_map/absorb/pallas_call | solution.py:270
  236.6 8.5 %absorb.5 = (f32[128,3584]{1,0:T(8,128)}, f32[128,3584]{1,0:T(8,128)}) custom-call(s32[1]{0:T(128)} %bitcast.place_ref, bf16[8,64,896]{2,1,0:T(8,128)(2,1)} %copy-done.6, bf16[8,64,896]{2,1,0:T(8,128)(2,1)} %copy-done.16, bf16[8,96,896]{2,1,0:T(8,128)(2,1)} %arrange.2.refs_2_, ...), custom_call_target="tpu_custom_call", output_to_operand_aliasing={{0}: (9, {}), {1}: (10, {})} | custom-call | flops 1291845632 | bytes 5046272 | tf_op jit(solution)/shard_map/absorb/pallas_call | solution.py:270
  245.1 6.9 %absorb.6 = (f32[128,3584]{1,0:T(8,128)}, f32[128,3584]{1,0:T(8,128)}) custom-call(s32[1]{0:T(128)} %bitcast.place_ref, bf16[8,64,896]{2,1,0:T(8,128)(2,1)} %copy-done.15, bf16[8,64,896]{2,1,0:T(8,128)(2,1)} %copy-done.17, bf16[8,96,896]{2,1,0:T(8,128)(2,1)} %copy-done, ...), custom_call_target="tpu_custom_call", output_to_operand_aliasing={{0}: (7, {}), {1}: (8, {})} | custom-call | flops 939524096 | bytes 3670016 | tf_op jit(solution)/shard_map/absorb/pallas_call | solution.py:270
  252.0 8.5 %absorb.7 = (f32[128,3584]{1,0:T(8,128)}, f32[128,3584]{1,0:T(8,128)}) custom-call(s32[1]{0:T(128)} %bitcast.place_ref, bf16[8,64,896]{2,1,0:T(8,128)(2,1)} %collective-permute-done.12.refs_0_, bf16[8,64,896]{2,1,0:T(8,128)(2,1)} %collective-permute-done.13.refs_1_, bf16[8,96,896]{2,1,0:T(8,128)(2,1)} %copy-done.1, ...), custom_call_target="tpu_custom_call", output_to_operand_aliasing={{0}: (9, {}), {1}: (10, {})} | custom-call | flops 1291845632 | bytes 5046272 | tf_op jit(solution)/shard_map/absorb/pallas_call | solution.py:270
  260.6 1.2 copy-done.11
  261.7 9.5 %finish.1 = (bf16[3584,128]{1,0:T(8,128)(2,1)}, bf16[128,3584]{1,0:T(8,128)(2,1)}, bf16[16,112,256]{2,1,0:T(8,128)(2,1)}, bf16[16,112,256]{2,1,0:T(8,128)(2,1)}) custom-call(s32[1]{0:T(128)} %bitcast.place_ref, s32[1]{0:T(128)} %bitcast.1.half_ref, s32[1]{0:T(128)} %bitcast.2.me, s32[1]{0:T(128)} %copy.28.leave, s32[32]{0:T(128)} %owner.1, ...), custom_call_target="tpu_custom_call" | custom-call | tf_op jit(solution)/shard_map/finish/pallas_call | solution.py:416
  271.2 19.9 %all_to_all.20 = bf16[16,112,256]{2,1,0:T(8,128)(2,1)S(1)} all-to-all(bf16[16,112,256]{2,1,0:T(8,128)(2,1)} %get-tuple-element.35), channel_id=1, replica_groups=mesh['zl'=4,'co'=2,'y'=4,'x'=4,'zh'=2] {'y','x'}, dimensions={0} | all-to-all | bytes 1835008 | tf_op jit(solution)/shard_map/all_to_all | solution.py:556
  291.1 3.6 %all-to-all-start.2 = ((bf16[16,112,256]{2,1,0:T(8,128)(2,1)}), bf16[16,112,256]{2,1,0:T(8,128)(2,1)S(1)}, u32[]{:S(2)}, u32[]{:S(2)}) async-start(bf16[16,112,256]{2,1,0:T(8,128)(2,1)} %get-tuple-element.34), calls=%async_computation.2 | async-start | bytes 1835008 | tf_op jit(solution)/shard_map/all_to_all | solution.py:556
  295.5 14.5 %all-to-all-done.2 = bf16[16,112,256]{2,1,0:T(8,128)(2,1)S(1)} async-done(((bf16[16,112,256]{2,1,0:T(8,128)(2,1)}), bf16[16,112,256]{2,1,0:T(8,128)(2,1)S(1)}, u32[]{:S(2)}, u32[]{:S(2)}) %all-to-all-start.2) | async-done | bytes 917536 | tf_op jit(solution)/shard_map/all_to_all | solution.py:556
  (81 shorter events, 6.9 us)
Async XLA Ops:
  4.4 23.7 %all-to-all-start = ((bf16[32,16,896]{2,1,0:T(8,128)(2,1)}), bf16[32,16,896]{2,1,0:T(8,128)(2,1)S(1)}, u32[]{:S(2)}, u32[]{:S(2)}) async-start(bf16[32,16,896]{2,1,0:T(8,128)(2,1)} %bitcast.44), calls=%async_computation | async-start | bytes 1835008 | tf_op jit(solution)/shard_map/all_to_all | solution.py:483
  29.0 25.2 %all-to-all-start.1 = ((bf16[32,24,896]{2,1,0:T(8,128)(2,1)}), bf16[32,24,896]{2,1,0:T(8,128)(2,1)S(1)}, u32[]{:S(2)}, u32[]{:S(2)}) async-start(bf16[32,24,896]{2,1,0:T(8,128)(2,1)} %bitcast.41), calls=%async_computation.1 | async-start | bytes 2752512 | tf_op jit(solution)/shard_map/all_to_all | solution.py:483
  35.5 23.4 %collective-permute-start.8 = (bf16[8,64,896]{2,1,0:T(8,128)(2,1)}, bf16[8,64,896]{2,1,0:T(8,128)(2,1)}, u32[]{:S(2)}, u32[]{:S(2)}) collective-permute-start(bf16[8,64,896]{2,1,0:T(8,128)(2,1)} %arrange.3.refs_0_), channel_id=1, source_target_pairs={{0,64},{2,66},{4,68},{6,70},{8,72},{10,74},{12,76},{14,78},{16,80}... | collective-permute-start | bytes 2752520 | tf_op jit(solution)/shard_map/ppermute | solution.py:471
  58.9 18.5 %collective-permute-start = (bf16[8,96,896]{2,1,0:T(8,128)(2,1)}, bf16[8,96,896]{2,1,0:T(8,128)(2,1)S(1)}, u32[]{:S(2)}, u32[]{:S(2)}) collective-permute-start(bf16[8,96,896]{2,1,0:T(8,128)(2,1)} %arrange.2.refs_2_), channel_id=1, source_target_pairs={{0,64},{2,66},{4,68},{6,70},{8,72},{10,74},{12,76},{14,78},{16,80}... | collective-permute-start | bytes 4128776 | tf_op jit(solution)/shard_map/ppermute | solution.py:471
  58.9 4.8 %collective-permute-start.26 = (bf16[8,64,896]{2,1,0:T(8,128)(2,1)S(1)}, bf16[8,64,896]{2,1,0:T(8,128)(2,1)S(1)}, u32[]{:S(2)}, u32[]{:S(2)}) collective-permute-start(bf16[8,64,896]{2,1,0:T(8,128)(2,1)S(1)} %copy-done.3), channel_id=1, source_target_pairs={{0,32},{2,34},{4,36},{6,38},{8,40},{10,42},{12,44},{14,46},{16,48}... | collective-permute-start | bytes 2752520 | tf_op jit(solution)/shard_map/ppermute | solution.py:474
  58.9 26.0 %collective-permute-start.9 = (bf16[8,64,896]{2,1,0:T(8,128)(2,1)}, bf16[8,64,896]{2,1,0:T(8,128)(2,1)}, u32[]{:S(2)}, u32[]{:S(2)}) collective-permute-start(bf16[8,64,896]{2,1,0:T(8,128)(2,1)} %collective-permute-done.8.refs_2_), channel_id=1, source_target_pairs={{0,64},{2,66},{4,68},{6,70},{8,72},{10,74},{12,76},{14,78},{16,80}... | collective-permute-start | bytes 2752520 | tf_op jit(solution)/shard_map/ppermute | solution.py:471
  63.7 21.1 %copy-start.13 = (bf16[8,64,896]{2,1,0:T(8,128)(2,1)}, bf16[8,64,896]{2,1,0:T(8,128)(2,1)S(1)}, u32[]{:S(2)}) copy-start(bf16[8,64,896]{2,1,0:T(8,128)(2,1)S(1)} %collective-permute-done.26.refs_1_) | copy-start | bytes 2752516
  63.7 25.4 %collective-permute-start.28 = (bf16[8,64,896]{2,1,0:T(8,128)(2,1)S(1)}, bf16[8,64,896]{2,1,0:T(8,128)(2,1)S(1)}, u32[]{:S(2)}, u32[]{:S(2)}) collective-permute-start(bf16[8,64,896]{2,1,0:T(8,128)(2,1)S(1)} %collective-permute-done.26.refs_1_), channel_id=1, source_target_pairs={{96,32},{98,34},{100,36},{102,38},{104,40},{106,42},{108,44},{110,... | collective-permute-start | bytes 2752520 | tf_op jit(solution)/shard_map/ppermute | solution.py:471
  77.4 51.8 %copy-start.8 = (bf16[8,96,896]{2,1,0:T(8,128)(2,1)}, bf16[8,96,896]{2,1,0:T(8,128)(2,1)S(1)}, u32[]{:S(2)}) copy-start(bf16[8,96,896]{2,1,0:T(8,128)(2,1)S(1)} %collective-permute-done.refs_4_) | copy-start | bytes 4128772
  77.4 22.1 %collective-permute-start.1 = (bf16[8,96,896]{2,1,0:T(8,128)(2,1)S(1)}, bf16[8,96,896]{2,1,0:T(8,128)(2,1)}, u32[]{:S(2)}, u32[]{:S(2)}) collective-permute-start(bf16[8,96,896]{2,1,0:T(8,128)(2,1)S(1)} %collective-permute-done.refs_4_), channel_id=1, source_target_pairs={{0,64},{2,66},{4,68},{6,70},{8,72},{10,74},{12,76},{14,78},{16,80}... | collective-permute-start | bytes 4128776 | tf_op jit(solution)/shard_map/ppermute | solution.py:471
  81.7 15.6 %collective-permute-start.30 = (bf16[8,64,896]{2,1,0:T(8,128)(2,1)}, bf16[8,64,896]{2,1,0:T(8,128)(2,1)}, u32[]{:S(2)}, u32[]{:S(2)}) collective-permute-start(bf16[8,64,896]{2,1,0:T(8,128)(2,1)} %collective-permute-done.8.refs_2_), channel_id=1, source_target_pairs={{96,32},{98,34},{100,36},{102,38},{104,40},{106,42},{108,44},{110,... | collective-permute-start | bytes 2752520 | tf_op jit(solution)/shard_map/ppermute | solution.py:471
  84.9 12.4 %collective-permute-start.10 = (bf16[8,64,896]{2,1,0:T(8,128)(2,1)}, bf16[8,64,896]{2,1,0:T(8,128)(2,1)}, u32[]{:S(2)}, u32[]{:S(2)}) collective-permute-start(bf16[8,64,896]{2,1,0:T(8,128)(2,1)} %collective-permute-done.9), channel_id=1, source_target_pairs={{0,64},{2,66},{4,68},{6,70},{8,72},{10,74},{12,76},{14,78},{16,80}... | collective-permute-start | bytes 2752520 | tf_op jit(solution)/shard_map/ppermute | solution.py:471
  86.5 28.5 %collective-permute-start.20 = (bf16[8,96,896]{2,1,0:T(8,128)(2,1)}, bf16[8,96,896]{2,1,0:T(8,128)(2,1)S(1)}, u32[]{:S(2)}, u32[]{:S(2)}) collective-permute-start(bf16[8,96,896]{2,1,0:T(8,128)(2,1)} %arrange.2.refs_2_), channel_id=1, source_target_pairs={{0,32},{2,34},{4,36},{6,38},{8,40},{10,42},{12,44},{14,46},{16,48}... | collective-permute-start | bytes 4128776 | tf_op jit(solution)/shard_map/ppermute | solution.py:474
  90.1 11.5 %collective-permute-start.27 = (bf16[8,64,896]{2,1,0:T(8,128)(2,1)}, bf16[8,64,896]{2,1,0:T(8,128)(2,1)}, u32[]{:S(2)}, u32[]{:S(2)}) collective-permute-start(bf16[8,64,896]{2,1,0:T(8,128)(2,1)} %collective-permute-done.8.refs_2_), channel_id=1, source_target_pairs={{0,32},{2,34},{4,36},{6,38},{8,40},{10,42},{12,44},{14,46},{16,48}... | collective-permute-start | bytes 2752520 | tf_op jit(solution)/shard_map/ppermute | solution.py:474
  91.4 10.2 %copy-start.4 = (bf16[8,64,896]{2,1,0:T(8,128)(2,1)}, bf16[8,64,896]{2,1,0:T(8,128)(2,1)S(1)}, u32[]{:S(2)}) copy-start(bf16[8,64,896]{2,1,0:T(8,128)(2,1)S(1)} %broadcast_select_fusion.4.refs_4_) | copy-start | bytes 2752516
  97.3 18.5 %collective-permute-start.29 = (bf16[8,64,896]{2,1,0:T(8,128)(2,1)S(1)}, bf16[8,64,896]{2,1,0:T(8,128)(2,1)}, u32[]{:S(2)}, u32[]{:S(2)}) collective-permute-start(bf16[8,64,896]{2,1,0:T(8,128)(2,1)S(1)} %broadcast_select_fusion.4.refs_4_), channel_id=1, source_target_pairs={{0,32},{2,34},{4,36},{6,38},{8,40},{10,42},{12,44},{14,46},{16,48}... | collective-permute-start | bytes 2752520 | tf_op jit(solution)/shard_map/ppermute | solution.py:474
  97.3 28.5 %collective-permute-start.23 = (bf16[8,64,896]{2,1,0:T(8,128)(2,1)}, bf16[8,64,896]{2,1,0:T(8,128)(2,1)S(1)}, u32[]{:S(2)}, u32[]{:S(2)}) collective-permute-start(bf16[8,64,896]{2,1,0:T(8,128)(2,1)} %collective-permute-done.9), channel_id=1, source_target_pairs={{96,32},{98,34},{100,36},{102,38},{104,40},{106,42},{108,44},{110,... | collective-permute-start | bytes 2752520 | tf_op jit(solution)/shard_map/ppermute | solution.py:471
  99.5 28.9 %collective-permute-start.2 = (bf16[8,96,896]{2,1,0:T(8,128)(2,1)}, bf16[8,96,896]{2,1,0:T(8,128)(2,1)S(1)}, u32[]{:S(2)}, u32[]{:S(2)}) collective-permute-start(bf16[8,96,896]{2,1,0:T(8,128)(2,1)} %collective-permute-done.1), channel_id=1, source_target_pairs={{0,64},{2,66},{4,68},{6,70},{8,72},{10,74},{12,76},{14,78},{16,80}... | collective-permute-start | bytes 4128776 | tf_op jit(solution)/shard_map/ppermute | solution.py:471
  101.6 41.3 %copy-start.5 = (bf16[8,64,896]{2,1,0:T(8,128)(2,1)}, bf16[8,64,896]{2,1,0:T(8,128)(2,1)S(1)}, u32[]{:S(2)}) copy-start(bf16[8,64,896]{2,1,0:T(8,128)(2,1)S(1)} %broadcast_select_fusion.3.refs_6_) | copy-start | bytes 2752516
  101.6 25.5 %collective-permute-start.31 = (bf16[8,64,896]{2,1,0:T(8,128)(2,1)S(1)}, bf16[8,64,896]{2,1,0:T(8,128)(2,1)S(1)}, u32[]{:S(2)}, u32[]{:S(2)}) collective-permute-start(bf16[8,64,896]{2,1,0:T(8,128)(2,1)S(1)} %broadcast_select_fusion.3.refs_6_), channel_id=1, source_target_pairs={{0,32},{2,34},{4,36},{6,38},{8,40},{10,42},{12,44},{14,46},{16,48}... | collective-permute-start | bytes 2752520 | tf_op jit(solution)/shard_map/ppermute | solution.py:474
  115.0 27.9 %copy-start.9 = (bf16[8,96,896]{2,1,0:T(8,128)(2,1)}, bf16[8,96,896]{2,1,0:T(8,128)(2,1)S(1)}, u32[]{:S(2)}) copy-start(bf16[8,96,896]{2,1,0:T(8,128)(2,1)S(1)} %collective-permute-done.20.refs_3_) | copy-start | bytes 4128772
  115.0 14.2 %collective-permute-start.11 = (bf16[8,64,896]{2,1,0:T(8,128)(2,1)}, bf16[8,64,896]{2,1,0:T(8,128)(2,1)S(1)}, u32[]{:S(2)}, u32[]{:S(2)}) collective-permute-start(bf16[8,64,896]{2,1,0:T(8,128)(2,1)} %collective-permute-done.10), channel_id=1, source_target_pairs={{64,128},{66,130},{68,132},{70,134},{72,136},{74,138},{76,140},{78... | collective-permute-start | bytes 2752520 | tf_op jit(solution)/shard_map/ppermute | solution.py:471
  115.7 27.2 %collective-permute-start.25 = (bf16[8,96,896]{2,1,0:T(8,128)(2,1)S(1)}, bf16[8,96,896]{2,1,0:T(8,128)(2,1)S(1)}, u32[]{:S(2)}, u32[]{:S(2)}) collective-permute-start(bf16[8,96,896]{2,1,0:T(8,128)(2,1)S(1)} %collective-permute-done.refs_4_), channel_id=1, source_target_pairs={{0,32},{2,34},{4,36},{6,38},{8,40},{10,42},{12,44},{14,46},{16,48}... | collective-permute-start | bytes 4128776 | tf_op jit(solution)/shard_map/ppermute | solution.py:474
  125.8 15.5 %collective-permute-start.18 = (bf16[8,64,896]{2,1,0:T(8,128)(2,1)}, bf16[8,64,896]{2,1,0:T(8,128)(2,1)S(1)}, u32[]{:S(2)}, u32[]{:S(2)}) collective-permute-start(bf16[8,64,896]{2,1,0:T(8,128)(2,1)} %collective-permute-done.10), channel_id=1, source_target_pairs={{96,32},{98,34},{100,36},{102,38},{104,40},{106,42},{108,44},{110,... | collective-permute-start | bytes 2752520 | tf_op jit(solution)/shard_map/ppermute | solution.py:471
  127.1 30.2 %copy-start.14 = (bf16[8,64,896]{2,1,0:T(8,128)(2,1)}, bf16[8,64,896]{2,1,0:T(8,128)(2,1)S(1)}, u32[]{:S(2)}) copy-start(bf16[8,64,896]{2,1,0:T(8,128)(2,1)S(1)} %collective-permute-done.31.refs_7_) | copy-start | bytes 2752516
  127.1 28.9 %collective-permute-start.21 = (bf16[8,96,896]{2,1,0:T(8,128)(2,1)S(1)}, bf16[8,96,896]{2,1,0:T(8,128)(2,1)S(1)}, u32[]{:S(2)}, u32[]{:S(2)}) collective-permute-start(bf16[8,96,896]{2,1,0:T(8,128)(2,1)S(1)} %collective-permute-done.20.refs_3_), channel_id=1, source_target_pairs={{96,32},{98,34},{100,36},{102,38},{104,40},{106,42},{108,44},{110,... | collective-permute-start | bytes 4128776 | tf_op jit(solution)/shard_map/ppermute | solution.py:471
  128.4 28.9 %collective-permute-start.5 = (bf16[8,96,896]{2,1,0:T(8,128)(2,1)S(1)}, bf16[8,96,896]{2,1,0:T(8,128)(2,1)S(1)}, u32[]{:S(2)}, u32[]{:S(2)}) collective-permute-start(bf16[8,96,896]{2,1,0:T(8,128)(2,1)S(1)} %collective-permute-done.2), channel_id=1, source_target_pairs={{64,128},{66,130},{68,132},{70,134},{72,136},{74,138},{76,140},{78... | collective-permute-start | bytes 4128776 | tf_op jit(solution)/shard_map/ppermute | solution.py:471
  129.2 41.6 %collective-permute-start.14 = (bf16[8,96,896]{2,1,0:T(8,128)(2,1)S(1)}, bf16[8,96,896]{2,1,0:T(8,128)(2,1)S(1)}, u32[]{:S(2)}, u32[]{:S(2)}) collective-permute-start(bf16[8,96,896]{2,1,0:T(8,128)(2,1)S(1)} %collective-permute-done.refs_4_), channel_id=1, source_target_pairs={{96,32},{98,34},{100,36},{102,38},{104,40},{106,42},{108,44},{110,... | collective-permute-start | bytes 4128776 | tf_op jit(solution)/shard_map/ppermute | solution.py:471
  141.3 45.7 %copy-start.15 = (bf16[8,64,896]{2,1,0:T(8,128)(2,1)}, bf16[8,64,896]{2,1,0:T(8,128)(2,1)S(1)}, u32[]{:S(2)}) copy-start(bf16[8,64,896]{2,1,0:T(8,128)(2,1)S(1)} %collective-permute-done.18.refs_0_) | copy-start | bytes 2752516
  141.3 44.2 %collective-permute-start.16 = (bf16[8,96,896]{2,1,0:T(8,128)(2,1)}, bf16[8,96,896]{2,1,0:T(8,128)(2,1)S(1)}, u32[]{:S(2)}, u32[]{:S(2)}) collective-permute-start(bf16[8,96,896]{2,1,0:T(8,128)(2,1)} %collective-permute-done.1), channel_id=1, source_target_pairs={{96,32},{98,34},{100,36},{102,38},{104,40},{106,42},{108,44},{110,... | collective-permute-start | bytes 4128776 | tf_op jit(solution)/shard_map/ppermute | solution.py:471
  142.9 16.0 %copy-start.6 = (bf16[8,64,896]{2,1,0:T(8,128)(2,1)}, bf16[8,64,896]{2,1,0:T(8,128)(2,1)S(1)}, u32[]{:S(2)}) copy-start(bf16[8,64,896]{2,1,0:T(8,128)(2,1)S(1)} %broadcast_select_fusion.5.refs_0_) | copy-start | bytes 2752516
  142.9 14.4 %copy-start.10 = (bf16[8,96,896]{2,1,0:T(8,128)(2,1)}, bf16[8,96,896]{2,1,0:T(8,128)(2,1)S(1)}, u32[]{:S(2)}) copy-start(bf16[8,96,896]{2,1,0:T(8,128)(2,1)S(1)} %collective-permute-done.25.refs_5_) | copy-start | bytes 4128772
  142.9 27.9 %collective-permute-start.24 = (bf16[8,64,896]{2,1,0:T(8,128)(2,1)S(1)}, bf16[8,64,896]{2,1,0:T(8,128)(2,1)S(1)}, u32[]{:S(2)}, u32[]{:S(2)}) collective-permute-start(bf16[8,64,896]{2,1,0:T(8,128)(2,1)S(1)} %broadcast_select_fusion.5.refs_0_), channel_id=1, source_target_pairs={{0,32},{2,34},{4,36},{6,38},{8,40},{10,42},{12,44},{14,46},{16,48}... | collective-permute-start | bytes 2752520 | tf_op jit(solution)/shard_map/ppermute | solution.py:474
  156.0 68.9 %collective-permute-start.3 = (bf16[8,96,896]{2,1,0:T(8,128)(2,1)S(1)}, bf16[8,96,896]{2,1,0:T(8,128)(2,1)}, u32[]{:S(2)}, u32[]{:S(2)}) collective-permute-start(bf16[8,96,896]{2,1,0:T(8,128)(2,1)S(1)} %collective-permute-done.2), channel_id=1, source_target_pairs={{96,32},{98,34},{100,36},{102,38},{104,40},{106,42},{108,44},{110,... | collective-permute-start | bytes 4128776 | tf_op jit(solution)/shard_map/ppermute | solution.py:471
  157.3 68.1 %collective-permute-start.6 = (bf16[8,96,896]{2,1,0:T(8,128)(2,1)S(1)}, bf16[8,96,896]{2,1,0:T(8,128)(2,1)}, u32[]{:S(2)}, u32[]{:S(2)}) collective-permute-start(bf16[8,96,896]{2,1,0:T(8,128)(2,1)S(1)} %collective-permute-done.5), channel_id=1, source_target_pairs={{96,32},{98,34},{100,36},{102,38},{104,40},{106,42},{108,44},{110,... | collective-permute-start | bytes 4128776 | tf_op jit(solution)/shard_map/ppermute | solution.py:471
  158.9 28.1 %copy-start = (bf16[8,96,896]{2,1,0:T(8,128)(2,1)}, bf16[8,96,896]{2,1,0:T(8,128)(2,1)S(1)}, u32[]{:S(2)}) copy-start(bf16[8,96,896]{2,1,0:T(8,128)(2,1)S(1)} %broadcast_select_fusion.refs_2_) | copy-start | bytes 4128772
  170.8 17.6 %collective-permute-start.19 = (bf16[8,64,896]{2,1,0:T(8,128)(2,1)S(1)}, bf16[8,64,896]{2,1,0:T(8,128)(2,1)S(1)}, u32[]{:S(2)}, u32[]{:S(2)}) collective-permute-start(bf16[8,64,896]{2,1,0:T(8,128)(2,1)S(1)} %collective-permute-done.18.refs_0_), channel_id=1, source_target_pairs={{0,32},{2,34},{4,36},{6,38},{8,40},{10,42},{12,44},{14,46},{16,48}... | collective-permute-start | bytes 2752520 | tf_op jit(solution)/shard_map/ppermute | solution.py:474
  170.8 16.2 %copy-start.16 = (bf16[8,64,896]{2,1,0:T(8,128)(2,1)}, bf16[8,64,896]{2,1,0:T(8,128)(2,1)S(1)}, u32[]{:S(2)}) copy-start(bf16[8,64,896]{2,1,0:T(8,128)(2,1)S(1)} %collective-permute-done.24.refs_1_) | copy-start | bytes 2752516
  170.8 54.8 %collective-permute-start.22 = (bf16[8,96,896]{2,1,0:T(8,128)(2,1)S(1)}, bf16[8,96,896]{2,1,0:T(8,128)(2,1)S(1)}, u32[]{:S(2)}, u32[]{:S(2)}) collective-permute-start(bf16[8,96,896]{2,1,0:T(8,128)(2,1)S(1)} %broadcast_select_fusion.refs_2_), channel_id=1, source_target_pairs={{0,32},{2,34},{4,36},{6,38},{8,40},{10,42},{12,44},{14,46},{16,48}... | collective-permute-start | bytes 4128776 | tf_op jit(solution)/shard_map/ppermute | solution.py:474
  185.5 39.4 %collective-permute-start.12 = (bf16[8,64,896]{2,1,0:T(8,128)(2,1)S(1)}, bf16[8,64,896]{2,1,0:T(8,128)(2,1)}, u32[]{:S(2)}, u32[]{:S(2)}) collective-permute-start(bf16[8,64,896]{2,1,0:T(8,128)(2,1)S(1)} %collective-permute-done.11), channel_id=1, source_target_pairs={{96,32},{98,34},{100,36},{102,38},{104,40},{106,42},{108,44},{110,... | collective-permute-start | bytes 2752520 | tf_op jit(solution)/shard_map/ppermute | solution.py:471
  188.6 37.0 %copy-start.17 = (bf16[8,64,896]{2,1,0:T(8,128)(2,1)}, bf16[8,64,896]{2,1,0:T(8,128)(2,1)S(1)}, u32[]{:S(2)}) copy-start(bf16[8,64,896]{2,1,0:T(8,128)(2,1)S(1)} %collective-permute-done.19.refs_1_) | copy-start | bytes 2752516
  188.6 63.4 %collective-permute-start.15 = (bf16[8,96,896]{2,1,0:T(8,128)(2,1)S(1)}, bf16[8,96,896]{2,1,0:T(8,128)(2,1)}, u32[]{:S(2)}, u32[]{:S(2)}) collective-permute-start(bf16[8,96,896]{2,1,0:T(8,128)(2,1)S(1)} %broadcast_select_fusion.2.refs_2_), channel_id=1, source_target_pairs={{0,32},{2,34},{4,36},{6,38},{8,40},{10,42},{12,44},{14,46},{16,48}... | collective-permute-start | bytes 4128776 | tf_op jit(solution)/shard_map/ppermute | solution.py:474
  224.9 27.1 %collective-permute-start.17 = (bf16[8,96,896]{2,1,0:T(8,128)(2,1)}, bf16[8,96,896]{2,1,0:T(8,128)(2,1)}, u32[]{:S(2)}, u32[]{:S(2)}) collective-permute-start(bf16[8,96,896]{2,1,0:T(8,128)(2,1)} %broadcast_select_fusion.1.refs_4_), channel_id=1, source_target_pairs={{0,32},{2,34},{4,36},{6,38},{8,40},{10,42},{12,44},{14,46},{16,48}... | collective-permute-start | bytes 4128776 | tf_op jit(solution)/shard_map/ppermute | solution.py:474
  224.9 35.6 %collective-permute-start.4 = (bf16[8,96,896]{2,1,0:T(8,128)(2,1)}, bf16[8,96,896]{2,1,0:T(8,128)(2,1)S(1)}, u32[]{:S(2)}, u32[]{:S(2)}) collective-permute-start(bf16[8,96,896]{2,1,0:T(8,128)(2,1)} %collective-permute-done.3.refs_0_), channel_id=1, source_target_pairs={{0,32},{2,34},{4,36},{6,38},{8,40},{10,42},{12,44},{14,46},{16,48}... | collective-permute-start | bytes 4128776 | tf_op jit(solution)/shard_map/ppermute | solution.py:474
  225.5 35.1 %collective-permute-start.7 = (bf16[8,96,896]{2,1,0:T(8,128)(2,1)}, bf16[8,96,896]{2,1,0:T(8,128)(2,1)}, u32[]{:S(2)}, u32[]{:S(2)}) collective-permute-start(bf16[8,96,896]{2,1,0:T(8,128)(2,1)} %collective-permute-done.6.refs_2_), channel_id=1, source_target_pairs={{0,32},{2,34},{4,36},{6,38},{8,40},{10,42},{12,44},{14,46},{16,48}... | collective-permute-start | bytes 4128776 | tf_op jit(solution)/shard_map/ppermute | solution.py:474
  226.7 25.3 %collective-permute-start.13 = (bf16[8,64,896]{2,1,0:T(8,128)(2,1)}, bf16[8,64,896]{2,1,0:T(8,128)(2,1)}, u32[]{:S(2)}, u32[]{:S(2)}) collective-permute-start(bf16[8,64,896]{2,1,0:T(8,128)(2,1)} %collective-permute-done.12.refs_0_), channel_id=1, source_target_pairs={{0,32},{2,34},{4,36},{6,38},{8,40},{10,42},{12,44},{14,46},{16,48}... | collective-permute-start | bytes 2752520 | tf_op jit(solution)/shard_map/ppermute | solution.py:474
  291.1 18.9 %all-to-all-start.2 = ((bf16[16,112,256]{2,1,0:T(8,128)(2,1)}), bf16[16,112,256]{2,1,0:T(8,128)(2,1)S(1)}, u32[]{:S(2)}, u32[]{:S(2)}) async-start(bf16[16,112,256]{2,1,0:T(8,128)(2,1)} %get-tuple-element.34), calls=%async_computation.2 | async-start | bytes 1835008 | tf_op jit(solution)/shard_map/all_to_all | solution.py:556
  294.8 15.2 %collective-permute-start.32 = (bf16[112,256]{1,0:T(8,128)(2,1)S(1)}, bf16[112,256]{1,0:T(8,128)(2,1)S(1)}, u32[]{:S(2)}, u32[]{:S(2)}) collective-permute-start(bf16[112,256]{1,0:T(8,128)(2,1)S(1)} %dynamic-slice_bitcast_fusion), channel_id=1, source_target_pairs={{0,1},{2,3},{4,5},{6,7},{8,9},{10,11},{12,13},{14,15},{16,17},{18,... | collective-permute-start | bytes 172040 | tf_op jit(solution)/shard_map/ppermute | solution.py:561
  (7 other events, 10.4 us)

commit v5 on v4

--- a/solution.py
+++ b/solution.py
@@ -14,8 +14,9 @@
 ALL = ("zl", "co", "y", "x", "zh")
 SLOT_GROUPS = ((0, 2), (2, 3))
 TAGS = ("a", "b")
-SUMS = ("ao1p2q3r", "a4 bo1p", "a5 b2q", "a6 b3r4")
-LAST = "b56"
+UNSORTED = ("a",)
+SUMS = ("ao1p2q3r", "a4 bo1p", "a56 b2q3r", "b45")
+LAST = "b6"
 PIECES = 4
 VMEM = pl.BlockSpec(memory_space=pltpu.VMEM)
 SMEM = pl.BlockSpec(memory_space=pltpu.SMEM)
@@ -163,23 +164,63 @@
     return arrays
 
 
+def rows_in(block):
+    return block.shape[1] if len(block.shape) == 3 else block.shape[0] // (2 * PIECES)
+
+
 def gather_rows(at, blocks, refs, held_x, held_c):
     refs = list(refs)
-    piece = refs[0].shape[2]
+    piece = refs[0].shape[-1]
     offset = 0
-    for test, _, second in blocks:
+    orders = {}
+    for test, first, second in blocks:
         first_ref = refs.pop(0)
         second_ref = refs.pop(0) if second is not None else None
-        count = first_ref.shape[1]
-        for q in range(2 * PIECES):
-            part = first_ref[q]
-            if second_ref is not None:
-                part = jnp.where(test(at), part, second_ref[q])
-            elif test is not None and q >= PIECES:
-                part = jnp.where(test(at), part, jnp.zeros_like(part))
-            held = held_x if q < PIECES else held_c
-            left = (q % PIECES) * piece
-            held[offset : offset + count, left : left + piece] = part
+        count = rows_in(first)
+        if len(first.shape) == 3:
+            for q in range(2 * PIECES):
+                part = first_ref[q]
+                if second_ref is not None:
+                    part = jnp.where(test(at), part, second_ref[q])
+                elif test is not None and q >= PIECES:
+                    part = jnp.where(test(at), part, jnp.zeros_like(part))
+                held = held_x if q < PIECES else held_c
+                left = (q % PIECES) * piece
+                held[offset : offset + count, left : left + piece] = part
+        else:
+            slots = count // 32
+            if slots not in orders:
+                orders[slots] = sorter(slots)
+            order = orders[slots]
+            rows, some = 8 * count // 2, count // 2
+
+            def sort_half(
+                half,
+                carry,
+                first_ref=first_ref,
+                second_ref=second_ref,
+                order=order,
+                test=test,
+                offset=offset,
+                rows=rows,
+                some=some,
+            ):
+                span = pl.ds(pl.multiple_of(half * rows, rows), rows)
+                block = first_ref[span, :]
+                if second_ref is not None:
+                    block = jnp.where(test(at), block, second_ref[span, :])
+                ordered = jnp.dot(order, block, preferred_element_type=jnp.float32)
+                target = pl.ds(pl.multiple_of(offset + half * some, 16), some)
+                for q in range(2 * PIECES):
+                    part = ordered[q * some : (q + 1) * some, :]
+                    if second_ref is None and test is not None and q >= PIECES:
+                        part = jnp.where(test(at), part, 0.0)
+                    held = held_x if q < PIECES else held_c
+                    left = (q % PIECES) * piece
+                    held[target, left : left + piece] = part.astype(jnp.bfloat16)
+                return carry
+
+            lax.fori_loop(0, 2, sort_half, 0)
         offset += count
 
 
@@ -209,7 +250,7 @@
 def absorb(place, blocks, w_up, w_down, sums):
     arrays = flatten(blocks)
     width, hidden_units = w_up.shape
-    total = sum(first.shape[1] for _, first, _ in blocks)
+    total = sum(rows_in(first) for _, first, _ in blocks)
     have = sums is not None
     steps = 7
     step = width // steps
@@ -341,7 +382,7 @@
     rest = (w_up, w_down, sums[1], moments[2], moments[3], sums[0], moments[0], moments[1])
 
     def body(place_ref, half_ref, me, leave, owner, *refs):
-        rows_in, refs = refs[: len(arrays)], refs[len(arrays) :]
+        block_refs, refs = refs[: len(arrays)], refs[len(arrays) :]
         rest_in, refs = refs[: len(rest)], refs[len(rest) :]
         out_up, out_down, out_near, out_far = refs[:4]
         refs = refs[4:]
@@ -350,7 +391,7 @@
         up_ref, down_ref, old_down, md, vd, old_up, mu, vu = rest_vmem
         moved_up, moved_down, both, held_x, held_c, held_pre, held_hid = refs[:7]
         sems, up_sems, down_sems, tile_sems = refs[7:]
-        starts, waits = pick_copies(place_ref[0], blocks, rows_in, rows_vmem, sems)
+        starts, waits = pick_copies(place_ref[0], blocks, block_refs, rows_vmem, sems)
         others = [
             pltpu.make_async_copy(source, target, sems.at[count + i])
             for i, (source, target) in enumerate(zip(rest_in, rest_vmem))
@@ -490,7 +531,8 @@
 
     for ch in chunks:
         tag = ch["tag"]
-        ch[0] = arrange(ch[0], ch["slots"])
+        if tag not in UNSORTED:
+            ch[0] = arrange(ch[0], ch["slots"])
         ch[1] = step(ch[0], (0, 1, 2, 3))
         ch["s0"] = swap(ch[0])
         x2 = step(ch["s0"], (2,))

time: 312 us -> 330 us (1.058)
  the two profiles are of different devices: /device:TPU:224 before, /device:TPU:33 now
where the time goes in v5:
time: 330 us; the launch traced here: 324 us
  waiting for transfers between devices  135 us (41%)
  starting transfers between devices  72 us (22%)
  Pallas kernels  60.5 us (18%)
  blocking collectives  45.1 us (14%)
  other arithmetic  5.66 us (2%)
  local copies, waits for them, and re-layouts  3.63 us (1%)
    ppermute x18, waiting for transfers between devices, step(): return lax.ppermute(value, ALL, stream_pairs(places))  114 us
    ppermute x18, starting transfers between devices, step(): return lax.ppermute(value, ALL, stream_pairs(places))  47.4 us
    pallas_call x4, Pallas kernels, absorb(): pl.pallas_call(body, out_shape=[shape, shape], in_specs=[SMEM] + [HBM] *...  39.7 us
    all_to_all x1, blocking collectives, on_device(): lax.all_to_all(sent.reshape(32, rows // 32, piece), ('co', 'y', 'x'), 0,...  25.9 us
    all_to_all x1, blocking collectives, from_leaver(): incoming = lax.all_to_all(tiles, ('y', 'x'), 0, 0, tiled=True)  19.2 us
    all_to_all x1, waiting for transfers between devices, on_device(): lax.all_to_all(sent.reshape(32, rows // 32, piece), ('co', 'y', 'x'), 0,...  10.6 us
    all_to_all x1, waiting for transfers between devices, from_leaver(): incoming = lax.all_to_all(tiles, ('y', 'x'), 0, 0, tiled=True)  9.8 us
    pallas_call x1, Pallas kernels, finish(): pl.pallas_call(body, out_shape=[jax.ShapeDtypeStruct((width, hidden_units...  9.14 us
  transfers between devices with their start and end apart: 35, of which 15 were waited for; matrix products, arithmetic and copies ran while one was open for 2% of the time, Pallas kernels for 14%

profile of v5, /device:TPU:33, one launch (start us, length us, event | category | flops | bytes accessed | tf_op | source)
XLA Modules:
  0.0 323.5 jit_solution(17290047689564272175)
XLA Ops:
  0.6 3.7 %prepare.2 = bf16[512,896]{1,0:T(8,128)(2,1)} custom-call(s32[1]{0:T(128)} %bitcast.3.base_ref, bf16[128,3584]{1,0:T(8,128)(2,1)} %x_ref.3, bf16[128,3584]{1,0:T(8,128)(2,1)} %c_ref.3, f32[1,128]{1,0:T(1,128)} %bitcast.51, s32[1,128]{1,0:T(1,128)} %bitcast.53), custom_call_target="tpu_custom_call" | custom-call | tf_op jit(solution)/shard_map/prepare/pallas_call | solution.py:106
  4.4 7.8 %all-to-all-start = ((bf16[32,16,896]{2,1,0:T(8,128)(2,1)}), bf16[32,16,896]{2,1,0:T(8,128)(2,1)S(1)}, u32[]{:S(2)}, u32[]{:S(2)}) async-start(bf16[32,16,896]{2,1,0:T(8,128)(2,1)} %bitcast.46), calls=%async_computation | async-start | bytes 1835008 | tf_op jit(solution)/shard_map/all_to_all | solution.py:524
  12.2 4.5 %prepare.3 = bf16[768,896]{1,0:T(8,128)(2,1)} custom-call(s32[1]{0:T(128)} %bitcast.3.base_ref, bf16[128,3584]{1,0:T(8,128)(2,1)} %x_ref.3, bf16[128,3584]{1,0:T(8,128)(2,1)} %c_ref.3, f32[1,128]{1,0:T(1,128)} %bitcast.52, s32[1,128]{1,0:T(1,128)} %bitcast.54), custom_call_target="tpu_custom_call" | custom-call | tf_op jit(solution)/shard_map/prepare/pallas_call | solution.py:106
  16.7 10.6 %all-to-all-done = bf16[32,16,896]{2,1,0:T(8,128)(2,1)S(1)} async-done(((bf16[32,16,896]{2,1,0:T(8,128)(2,1)}), bf16[32,16,896]{2,1,0:T(8,128)(2,1)S(1)}, u32[]{:S(2)}, u32[]{:S(2)}) %all-to-all-start) | async-done | bytes 917536 | tf_op jit(solution)/shard_map/all_to_all | solution.py:524
  27.3 25.9 %all_to_all.20 = bf16[32,24,896]{2,1,0:T(8,128)(2,1)} all-to-all(bf16[32,24,896]{2,1,0:T(8,128)(2,1)} %bitcast.41), channel_id=1, replica_groups=mesh['zl'=4,'co'=2,'y'=4,'x'=4,'zh'=2] {'co','y','x'}, dimensions={0} | all-to-all | bytes 2752512 | tf_op jit(solution)/shard_map/all_to_all | solution.py:524
  53.2 3.4 %arrange.1.refs_2_ = bf16[8,96,896]{2,1,0:T(8,128)(2,1)} custom-call(bf16[768,896]{1,0:T(8,128)(2,1)} %bitcast.42), custom_call_target="tpu_custom_call" | custom-call | tf_op jit(solution)/shard_map/arrange/pallas_call | solution.py:148
  56.7 5.4 %collective-permute-start.10 = (bf16[512,896]{1,0:T(8,128)(2,1)S(1)}, bf16[512,896]{1,0:T(8,128)(2,1)}, u32[]{:S(2)}, u32[]{:S(2)}) collective-permute-start(bf16[512,896]{1,0:T(8,128)(2,1)S(1)} %bitcast.43), channel_id=1, source_target_pairs={{0,64},{2,66},{4,68},{6,70},{8,72},{10,74},{12,76},{14,78},{16,80}... | collective-permute-start | bytes 2752520 | tf_op jit(solution)/shard_map/ppermute | solution.py:512
  62.1 22.4 %collective-permute-done.10.refs_2_ = bf16[512,896]{1,0:T(8,128)(2,1)} collective-permute-done((bf16[512,896]{1,0:T(8,128)(2,1)S(1)}, bf16[512,896]{1,0:T(8,128)(2,1)}, u32[]{:S(2)}, u32[]{:S(2)}) %collective-permute-start.10) | collective-permute-done | bytes 917536 | tf_op jit(solution)/shard_map/ppermute | solution.py:512
  85.8 1.3 collective-permute-start.1
  88.0 10.8 %collective-permute-start.28 = (bf16[512,896]{1,0:T(8,128)(2,1)S(1)}, bf16[512,896]{1,0:T(8,128)(2,1)S(1)}, u32[]{:S(2)}, u32[]{:S(2)}) collective-permute-start(bf16[512,896]{1,0:T(8,128)(2,1)S(1)} %collective-permute-done.26.refs_1_), channel_id=1, source_target_pairs={{96,32},{98,34},{100,36},{102,38},{104,40},{106,42},{108,44},{110,... | collective-permute-start | bytes 2752520 | tf_op jit(solution)/shard_map/ppermute | solution.py:512
  98.9 2.2 collective-permute-start.30
  102.4 6.6 %collective-permute-done.28 = bf16[512,896]{1,0:T(8,128)(2,1)S(1)} collective-permute-done((bf16[512,896]{1,0:T(8,128)(2,1)S(1)}, bf16[512,896]{1,0:T(8,128)(2,1)S(1)}, u32[]{:S(2)}, u32[]{:S(2)}) %collective-permute-start.28) | collective-permute-done | bytes 917536 | tf_op jit(solution)/shard_map/ppermute | solution.py:512
  110.0 4.1 %collective-permute-done.1 = bf16[8,96,896]{2,1,0:T(8,128)(2,1)} collective-permute-done((bf16[8,96,896]{2,1,0:T(8,128)(2,1)S(1)}, bf16[8,96,896]{2,1,0:T(8,128)(2,1)}, u32[]{:S(2)}, u32[]{:S(2)}) %collective-permute-start.1) | collective-permute-done | bytes 1376288 | tf_op jit(solution)/shard_map/ppermute | solution.py:512
  115.4 1.3 broadcast_select_fusion.4.refs_4_
  116.7 2.3 collective-permute-done.30
  119.0 3.0 collective-permute-start.29
  122.0 2.0 collective-permute-done.12
  123.9 2.4 collective-permute-start.23
  126.3 1.3 broadcast_select_fusion.3.refs_6_
  127.7 2.9 collective-permute-start.31
  130.6 1.3 collective-permute-start.15
  131.9 1.4 collective-permute-start.25
  133.3 3.6 %collective-permute-done.23 = bf16[512,896]{1,0:T(8,128)(2,1)S(1)} collective-permute-done((bf16[512,896]{1,0:T(8,128)(2,1)}, bf16[512,896]{1,0:T(8,128)(2,1)S(1)}, u32[]{:S(2)}, u32[]{:S(2)}) %collective-permute-start.23) | collective-permute-done | bytes 917536 | tf_op jit(solution)/shard_map/ppermute | solution.py:512
  136.9 3.8 %collective-permute-start.21 = (bf16[8,96,896]{2,1,0:T(8,128)(2,1)S(1)}, bf16[8,96,896]{2,1,0:T(8,128)(2,1)S(1)}, u32[]{:S(2)}, u32[]{:S(2)}) collective-permute-start(bf16[8,96,896]{2,1,0:T(8,128)(2,1)S(1)} %collective-permute-done.refs_4_), channel_id=1, source_target_pairs={{96,32},{98,34},{100,36},{102,38},{104,40},{106,42},{108,44},{110,... | collective-permute-start | bytes 4128776 | tf_op jit(solution)/shard_map/ppermute | solution.py:512
  140.7 1.3 collective-permute-start.13
  142.1 6.0 %collective-permute-done.15 = bf16[512,896]{1,0:T(8,128)(2,1)S(1)} collective-permute-done((bf16[512,896]{1,0:T(8,128)(2,1)}, bf16[512,896]{1,0:T(8,128)(2,1)S(1)}, u32[]{:S(2)}, u32[]{:S(2)}) %collective-permute-start.15) | collective-permute-done | bytes 917536 | tf_op jit(solution)/shard_map/ppermute | solution.py:512
  148.1 1.4 collective-permute-start.19
  149.5 1.3 collective-permute-start.3
  151.0 14.8 %collective-permute-done.13.refs_0_ = bf16[512,896]{1,0:T(8,128)(2,1)S(1)} collective-permute-done((bf16[512,896]{1,0:T(8,128)(2,1)}, bf16[512,896]{1,0:T(8,128)(2,1)S(1)}, u32[]{:S(2)}, u32[]{:S(2)}) %collective-permute-start.13) | collective-permute-done | bytes 917536 | tf_op jit(solution)/shard_map/ppermute | solution.py:512
  165.8 4.7 %collective-permute-start.16 = (bf16[512,896]{1,0:T(8,128)(2,1)S(1)}, bf16[512,896]{1,0:T(8,128)(2,1)}, u32[]{:S(2)}, u32[]{:S(2)}) collective-permute-start(bf16[512,896]{1,0:T(8,128)(2,1)S(1)} %collective-permute-done.15), channel_id=1, source_target_pairs={{96,32},{98,34},{100,36},{102,38},{104,40},{106,42},{108,44},{110,... | collective-permute-start | bytes 2752520 | tf_op jit(solution)/shard_map/ppermute | solution.py:512
  170.5 1.4 collective-permute-start.6
  171.9 8.5 %collective-permute-done.19 = bf16[8,96,896]{2,1,0:T(8,128)(2,1)S(1)} collective-permute-done((bf16[8,96,896]{2,1,0:T(8,128)(2,1)S(1)}, bf16[8,96,896]{2,1,0:T(8,128)(2,1)S(1)}, u32[]{:S(2)}, u32[]{:S(2)}) %collective-permute-start.19) | collective-permute-done | bytes 1376288 | tf_op jit(solution)/shard_map/ppermute | solution.py:512
  180.4 4.9 %collective-permute-start.8 = (bf16[8,96,896]{2,1,0:T(8,128)(2,1)S(1)}, bf16[8,96,896]{2,1,0:T(8,128)(2,1)}, u32[]{:S(2)}, u32[]{:S(2)}) collective-permute-start(bf16[8,96,896]{2,1,0:T(8,128)(2,1)S(1)} %collective-permute-done.2), channel_id=1, source_target_pairs={{96,32},{98,34},{100,36},{102,38},{104,40},{106,42},{108,44},{110,... | collective-permute-start | bytes 4128776 | tf_op jit(solution)/shard_map/ppermute | solution.py:512
  185.4 1.4 collective-permute-start.4
  186.7 1.5 broadcast_select_fusion.1.refs_4_
  188.4 1.8 collective-permute-done.16.refs_2_
  191.5 13.6 %collective-permute-done.6 = bf16[8,96,896]{2,1,0:T(8,128)(2,1)S(1)} collective-permute-done((bf16[8,96,896]{2,1,0:T(8,128)(2,1)}, bf16[8,96,896]{2,1,0:T(8,128)(2,1)S(1)}, u32[]{:S(2)}, u32[]{:S(2)}) %collective-permute-start.6) | collective-permute-done | bytes 1376288 | tf_op jit(solution)/shard_map/ppermute | solution.py:512
  205.9 13.9 %collective-permute-done.8.refs_2_ = bf16[8,96,896]{2,1,0:T(8,128)(2,1)} collective-permute-done((bf16[8,96,896]{2,1,0:T(8,128)(2,1)S(1)}, bf16[8,96,896]{2,1,0:T(8,128)(2,1)}, u32[]{:S(2)}, u32[]{:S(2)}) %collective-permute-start.8) | collective-permute-done | bytes 1376288 | tf_op jit(solution)/shard_map/ppermute | solution.py:512
  219.7 14.7 %collective-permute-done.4.refs_0_ = bf16[8,96,896]{2,1,0:T(8,128)(2,1)S(1)} collective-permute-done((bf16[8,96,896]{2,1,0:T(8,128)(2,1)S(1)}, bf16[8,96,896]{2,1,0:T(8,128)(2,1)S(1)}, u32[]{:S(2)}, u32[]{:S(2)}) %collective-permute-start.4) | collective-permute-done | bytes 1376288 | tf_op jit(solution)/shard_map/ppermute | solution.py:512
  236.7 12.7 %absorb.4 = (f32[128,3584]{1,0:T(8,128)}, f32[128,3584]{1,0:T(8,128)}) custom-call(s32[1]{0:T(128)} %bitcast.place_ref, bf16[512,896]{1,0:T(8,128)(2,1)} %bitcast.45, bf16[512,896]{1,0:T(8,128)(2,1)} %copy-done.11, bf16[512,896]{1,0:T(8,128)(2,1)} %collective-permute-done.10.refs_2_, bf16[512,896]{1,0:T(8,128)(2,1)} %collective-permute-done.27.refs_3_, ...), custom_call_target="tpu_custom_call" | custom-call | flops 1644167168 | bytes 6422528 | tf_op jit(solution)/shard_map/absorb/pallas_call | solution.py:311
  249.5 9.1 %absorb.5 = (f32[128,3584]{1,0:T(8,128)}, f32[128,3584]{1,0:T(8,128)}) custom-call(s32[1]{0:T(128)} %bitcast.place_ref, bf16[512,896]{1,0:T(8,128)(2,1)} %copy-done.5, bf16[512,896]{1,0:T(8,128)(2,1)} %copy-done.14, bf16[8,96,896]{2,1,0:T(8,128)(2,1)} %arrange.1.refs_2_, ...), custom_call_target="tpu_custom_call", output_to_operand_aliasing={{0}: (9, {}), {1}: (10, {})} | custom-call | flops 1291845632 | bytes 5046272 | tf_op jit(solution)/shard_map/absorb/pallas_call | solution.py:311
  258.6 10.9 %absorb.6 = (f32[128,3584]{1,0:T(8,128)}, f32[128,3584]{1,0:T(8,128)}) custom-call(s32[1]{0:T(128)} %bitcast.place_ref, bf16[512,896]{1,0:T(8,128)(2,1)} %copy-done.13, bf16[512,896]{1,0:T(8,128)(2,1)} %copy-done.15, bf16[512,896]{1,0:T(8,128)(2,1)} %collective-permute-done.16.refs_2_, ...), custom_call_target="tpu_custom_call", output_to_operand_aliasing={{0}: (11, {}), {1}: (12, {})} | custom-call | flops 1879048192 | bytes 7340032 | tf_op jit(solution)/shard_map/absorb/pallas_call | solution.py:311
  269.4 7.1 %absorb.7 = (f32[128,3584]{1,0:T(8,128)}, f32[128,3584]{1,0:T(8,128)}) custom-call(s32[1]{0:T(128)} %bitcast.place_ref, bf16[8,96,896]{2,1,0:T(8,128)(2,1)} %copy-done.1, bf16[8,96,896]{2,1,0:T(8,128)(2,1)} %collective-permute-done.7.refs_1_, bf16[8,96,896]{2,1,0:T(8,128)(2,1)} %collective-permute-done.8.refs_2_, ...), custom_call_target="tpu_custom_call", output_to_operand_aliasing={{0}: (7, {}), {1}: (8, {})} | custom-call | flops 704643072 | bytes 2752512 | tf_op jit(solution)/shard_map/absorb/pallas_call | solution.py:311
  276.5 9.1 %finish.1 = (bf16[3584,128]{1,0:T(8,128)(2,1)}, bf16[128,3584]{1,0:T(8,128)(2,1)}, bf16[16,112,256]{2,1,0:T(8,128)(2,1)}, bf16[16,112,256]{2,1,0:T(8,128)(2,1)}) custom-call(s32[1]{0:T(128)} %bitcast.place_ref, s32[1]{0:T(128)} %bitcast.1.half_ref, s32[1]{0:T(128)} %bitcast.2.me, s32[1]{0:T(128)} %copy.28.leave, s32[32]{0:T(128)} %owner.1, ...), custom_call_target="tpu_custom_call" | custom-call | tf_op jit(solution)/shard_map/finish/pallas_call | solution.py:457
  285.7 19.2 %all_to_all.21 = bf16[16,112,256]{2,1,0:T(8,128)(2,1)S(1)} all-to-all(bf16[16,112,256]{2,1,0:T(8,128)(2,1)} %get-tuple-element.35), channel_id=1, replica_groups=mesh['zl'=4,'co'=2,'y'=4,'x'=4,'zh'=2] {'y','x'}, dimensions={0} | all-to-all | bytes 1835008 | tf_op jit(solution)/shard_map/all_to_all | solution.py:598
  304.9 3.6 %all-to-all-start.2 = ((bf16[16,112,256]{2,1,0:T(8,128)(2,1)}), bf16[16,112,256]{2,1,0:T(8,128)(2,1)S(1)}, u32[]{:S(2)}, u32[]{:S(2)}) async-start(bf16[16,112,256]{2,1,0:T(8,128)(2,1)} %get-tuple-element.34), calls=%async_computation.2 | async-start | bytes 1835008 | tf_op jit(solution)/shard_map/all_to_all | solution.py:598
  308.5 4.5 %collective-permute-start.32 = (bf16[112,256]{1,0:T(8,128)(2,1)S(1)}, bf16[112,256]{1,0:T(8,128)(2,1)S(1)}, u32[]{:S(2)}, u32[]{:S(2)}) collective-permute-start(bf16[112,256]{1,0:T(8,128)(2,1)S(1)} %dynamic-slice_bitcast_fusion), channel_id=1, source_target_pairs={{0,1},{2,3},{4,5},{6,7},{8,9},{10,11},{12,13},{14,15},{16,17},{18,... | collective-permute-start | bytes 172040 | tf_op jit(solution)/shard_map/ppermute | solution.py:603
  313.1 9.8 %all-to-all-done.2 = bf16[16,112,256]{2,1,0:T(8,128)(2,1)S(1)} async-done(((bf16[16,112,256]{2,1,0:T(8,128)(2,1)}), bf16[16,112,256]{2,1,0:T(8,128)(2,1)S(1)}, u32[]{:S(2)}, u32[]{:S(2)}) %all-to-all-start.2) | async-done | bytes 917536 | tf_op jit(solution)/shard_map/all_to_all | solution.py:598
  (75 shorter events, 10.3 us)
Async XLA Ops:
  4.4 22.9 %all-to-all-start = ((bf16[32,16,896]{2,1,0:T(8,128)(2,1)}), bf16[32,16,896]{2,1,0:T(8,128)(2,1)S(1)}, u32[]{:S(2)}, u32[]{:S(2)}) async-start(bf16[32,16,896]{2,1,0:T(8,128)(2,1)} %bitcast.46), calls=%async_computation | async-start | bytes 1835008 | tf_op jit(solution)/shard_map/all_to_all | solution.py:524
  27.3 34.7 %copy-start.2 = (bf16[32,16,896]{2,1,0:T(8,128)(2,1)}, bf16[32,16,896]{2,1,0:T(8,128)(2,1)S(1)}, u32[]{:S(2)}) copy-start(bf16[32,16,896]{2,1,0:T(8,128)(2,1)S(1)} %all-to-all-done) | copy-start | bytes 2752516
  56.7 29.1 %collective-permute-start = (bf16[8,96,896]{2,1,0:T(8,128)(2,1)}, bf16[8,96,896]{2,1,0:T(8,128)(2,1)S(1)}, u32[]{:S(2)}, u32[]{:S(2)}) collective-permute-start(bf16[8,96,896]{2,1,0:T(8,128)(2,1)} %arrange.1.refs_2_), channel_id=1, source_target_pairs={{0,64},{2,66},{4,68},{6,70},{8,72},{10,74},{12,76},{14,78},{16,80}... | collective-permute-start | bytes 4128776 | tf_op jit(solution)/shard_map/ppermute | solution.py:512
  56.7 27.8 %collective-permute-start.10 = (bf16[512,896]{1,0:T(8,128)(2,1)S(1)}, bf16[512,896]{1,0:T(8,128)(2,1)}, u32[]{:S(2)}, u32[]{:S(2)}) collective-permute-start(bf16[512,896]{1,0:T(8,128)(2,1)S(1)} %bitcast.43), channel_id=1, source_target_pairs={{0,64},{2,66},{4,68},{6,70},{8,72},{10,74},{12,76},{14,78},{16,80}... | collective-permute-start | bytes 2752520 | tf_op jit(solution)/shard_map/ppermute | solution.py:512
  62.1 25.0 %collective-permute-start.26 = (bf16[512,896]{1,0:T(8,128)(2,1)S(1)}, bf16[512,896]{1,0:T(8,128)(2,1)S(1)}, u32[]{:S(2)}, u32[]{:S(2)}) collective-permute-start(bf16[512,896]{1,0:T(8,128)(2,1)S(1)} %bitcast.44), channel_id=1, source_target_pairs={{0,32},{2,34},{4,36},{6,38},{8,40},{10,42},{12,44},{14,46},{16,48}... | collective-permute-start | bytes 2752520 | tf_op jit(solution)/shard_map/ppermute | solution.py:515
  84.4 16.7 %collective-permute-start.11 = (bf16[512,896]{1,0:T(8,128)(2,1)}, bf16[512,896]{1,0:T(8,128)(2,1)}, u32[]{:S(2)}, u32[]{:S(2)}) collective-permute-start(bf16[512,896]{1,0:T(8,128)(2,1)} %collective-permute-done.10.refs_2_), channel_id=1, source_target_pairs={{0,64},{2,66},{4,68},{6,70},{8,72},{10,74},{12,76},{14,78},{16,80}... | collective-permute-start | bytes 2752520 | tf_op jit(solution)/shard_map/ppermute | solution.py:512
  85.7 51.2 %copy-start.6 = (bf16[8,96,896]{2,1,0:T(8,128)(2,1)}, bf16[8,96,896]{2,1,0:T(8,128)(2,1)S(1)}, u32[]{:S(2)}) copy-start(bf16[8,96,896]{2,1,0:T(8,128)(2,1)S(1)} %collective-permute-done.refs_4_) | copy-start | bytes 4128772
  85.8 28.4 %collective-permute-start.1 = (bf16[8,96,896]{2,1,0:T(8,128)(2,1)S(1)}, bf16[8,96,896]{2,1,0:T(8,128)(2,1)}, u32[]{:S(2)}, u32[]{:S(2)}) collective-permute-start(bf16[8,96,896]{2,1,0:T(8,128)(2,1)S(1)} %collective-permute-done.refs_4_), channel_id=1, source_target_pairs={{0,64},{2,66},{4,68},{6,70},{8,72},{10,74},{12,76},{14,78},{16,80}... | collective-permute-start | bytes 4128776 | tf_op jit(solution)/shard_map/ppermute | solution.py:512
  88.0 21.1 %collective-permute-start.28 = (bf16[512,896]{1,0:T(8,128)(2,1)S(1)}, bf16[512,896]{1,0:T(8,128)(2,1)S(1)}, u32[]{:S(2)}, u32[]{:S(2)}) collective-permute-start(bf16[512,896]{1,0:T(8,128)(2,1)S(1)} %collective-permute-done.26.refs_1_), channel_id=1, source_target_pairs={{96,32},{98,34},{100,36},{102,38},{104,40},{106,42},{108,44},{110,... | collective-permute-start | bytes 2752520 | tf_op jit(solution)/shard_map/ppermute | solution.py:512
  98.8 31.8 %collective-permute-start.18 = (bf16[8,96,896]{2,1,0:T(8,128)(2,1)}, bf16[8,96,896]{2,1,0:T(8,128)(2,1)S(1)}, u32[]{:S(2)}, u32[]{:S(2)}) collective-permute-start(bf16[8,96,896]{2,1,0:T(8,128)(2,1)} %arrange.1.refs_2_), channel_id=1, source_target_pairs={{0,32},{2,34},{4,36},{6,38},{8,40},{10,42},{12,44},{14,46},{16,48}... | collective-permute-start | bytes 4128776 | tf_op jit(solution)/shard_map/ppermute | solution.py:515
  98.9 20.1 %collective-permute-start.30 = (bf16[512,896]{1,0:T(8,128)(2,1)}, bf16[512,896]{1,0:T(8,128)(2,1)}, u32[]{:S(2)}, u32[]{:S(2)}) collective-permute-start(bf16[512,896]{1,0:T(8,128)(2,1)} %collective-permute-done.10.refs_2_), channel_id=1, source_target_pairs={{96,32},{98,34},{100,36},{102,38},{104,40},{106,42},{108,44},{110,... | collective-permute-start | bytes 2752520 | tf_op jit(solution)/shard_map/ppermute | solution.py:512
  101.1 22.8 %collective-permute-start.12 = (bf16[512,896]{1,0:T(8,128)(2,1)}, bf16[512,896]{1,0:T(8,128)(2,1)}, u32[]{:S(2)}, u32[]{:S(2)}) collective-permute-start(bf16[512,896]{1,0:T(8,128)(2,1)} %collective-permute-done.11), channel_id=1, source_target_pairs={{0,64},{2,66},{4,68},{6,70},{8,72},{10,74},{12,76},{14,78},{16,80}... | collective-permute-start | bytes 2752520 | tf_op jit(solution)/shard_map/ppermute | solution.py:512
  110.0 17.7 %collective-permute-start.27 = (bf16[512,896]{1,0:T(8,128)(2,1)}, bf16[512,896]{1,0:T(8,128)(2,1)}, u32[]{:S(2)}, u32[]{:S(2)}) collective-permute-start(bf16[512,896]{1,0:T(8,128)(2,1)} %collective-permute-done.10.refs_2_), channel_id=1, source_target_pairs={{0,32},{2,34},{4,36},{6,38},{8,40},{10,42},{12,44},{14,46},{16,48}... | collective-permute-start | bytes 2752520 | tf_op jit(solution)/shard_map/ppermute | solution.py:515
  114.1 35.4 %collective-permute-start.2 = (bf16[8,96,896]{2,1,0:T(8,128)(2,1)}, bf16[8,96,896]{2,1,0:T(8,128)(2,1)S(1)}, u32[]{:S(2)}, u32[]{:S(2)}) collective-permute-start(bf16[8,96,896]{2,1,0:T(8,128)(2,1)} %collective-permute-done.1), channel_id=1, source_target_pairs={{0,64},{2,66},{4,68},{6,70},{8,72},{10,74},{12,76},{14,78},{16,80}... | collective-permute-start | bytes 4128776 | tf_op jit(solution)/shard_map/ppermute | solution.py:512
  116.7 10.9 %copy-start.3 = (bf16[512,896]{1,0:T(8,128)(2,1)}, bf16[512,896]{1,0:T(8,128)(2,1)S(1)}, u32[]{:S(2)}) copy-start(bf16[512,896]{1,0:T(8,128)(2,1)S(1)} %broadcast_select_fusion.4.refs_4_) | copy-start | bytes 2752516
  119.0 12.9 %collective-permute-start.29 = (bf16[512,896]{1,0:T(8,128)(2,1)S(1)}, bf16[512,896]{1,0:T(8,128)(2,1)}, u32[]{:S(2)}, u32[]{:S(2)}) collective-permute-start(bf16[512,896]{1,0:T(8,128)(2,1)S(1)} %broadcast_select_fusion.4.refs_4_), channel_id=1, source_target_pairs={{0,32},{2,34},{4,36},{6,38},{8,40},{10,42},{12,44},{14,46},{16,48}... | collective-permute-start | bytes 2752520 | tf_op jit(solution)/shard_map/ppermute | solution.py:515
  123.9 13.0 %collective-permute-start.23 = (bf16[512,896]{1,0:T(8,128)(2,1)}, bf16[512,896]{1,0:T(8,128)(2,1)S(1)}, u32[]{:S(2)}, u32[]{:S(2)}) collective-permute-start(bf16[512,896]{1,0:T(8,128)(2,1)} %collective-permute-done.11), channel_id=1, source_target_pairs={{96,32},{98,34},{100,36},{102,38},{104,40},{106,42},{108,44},{110,... | collective-permute-start | bytes 2752520 | tf_op jit(solution)/shard_map/ppermute | solution.py:512
  127.6 23.3 %copy-start.4 = (bf16[512,896]{1,0:T(8,128)(2,1)}, bf16[512,896]{1,0:T(8,128)(2,1)S(1)}, u32[]{:S(2)}) copy-start(bf16[512,896]{1,0:T(8,128)(2,1)S(1)} %broadcast_select_fusion.3.refs_6_) | copy-start | bytes 2752516
  127.7 13.0 %collective-permute-start.31 = (bf16[512,896]{1,0:T(8,128)(2,1)S(1)}, bf16[512,896]{1,0:T(8,128)(2,1)S(1)}, u32[]{:S(2)}, u32[]{:S(2)}) collective-permute-start(bf16[512,896]{1,0:T(8,128)(2,1)S(1)} %broadcast_select_fusion.3.refs_6_), channel_id=1, source_target_pairs={{0,32},{2,34},{4,36},{6,38},{8,40},{10,42},{12,44},{14,46},{16,48}... | collective-permute-start | bytes 2752520 | tf_op jit(solution)/shard_map/ppermute | solution.py:515
  130.6 20.3 %copy-start.7 = (bf16[8,96,896]{2,1,0:T(8,128)(2,1)}, bf16[8,96,896]{2,1,0:T(8,128)(2,1)S(1)}, u32[]{:S(2)}) copy-start(bf16[8,96,896]{2,1,0:T(8,128)(2,1)S(1)} %collective-permute-done.18.refs_3_) | copy-start | bytes 4128772
  130.6 17.5 %collective-permute-start.15 = (bf16[512,896]{1,0:T(8,128)(2,1)}, bf16[512,896]{1,0:T(8,128)(2,1)S(1)}, u32[]{:S(2)}, u32[]{:S(2)}) collective-permute-start(bf16[512,896]{1,0:T(8,128)(2,1)} %collective-permute-done.12), channel_id=1, source_target_pairs={{64,128},{66,130},{68,132},{70,134},{72,136},{74,138},{76,140},{78... | collective-permute-start | bytes 2752520 | tf_op jit(solution)/shard_map/ppermute | solution.py:512
  131.9 33.9 %collective-permute-start.25 = (bf16[8,96,896]{2,1,0:T(8,128)(2,1)S(1)}, bf16[8,96,896]{2,1,0:T(8,128)(2,1)S(1)}, u32[]{:S(2)}, u32[]{:S(2)}) collective-permute-start(bf16[8,96,896]{2,1,0:T(8,128)(2,1)S(1)} %collective-permute-done.refs_4_), channel_id=1, source_target_pairs={{0,32},{2,34},{4,36},{6,38},{8,40},{10,42},{12,44},{14,46},{16,48}... | collective-permute-start | bytes 4128776 | tf_op jit(solution)/shard_map/ppermute | solution.py:515
  136.9 33.6 %collective-permute-start.21 = (bf16[8,96,896]{2,1,0:T(8,128)(2,1)S(1)}, bf16[8,96,896]{2,1,0:T(8,128)(2,1)S(1)}, u32[]{:S(2)}, u32[]{:S(2)}) collective-permute-start(bf16[8,96,896]{2,1,0:T(8,128)(2,1)S(1)} %collective-permute-done.refs_4_), channel_id=1, source_target_pairs={{96,32},{98,34},{100,36},{102,38},{104,40},{106,42},{108,44},{110,... | collective-permute-start | bytes 4128776 | tf_op jit(solution)/shard_map/ppermute | solution.py:512
  140.7 8.8 %copy-start.12 = (bf16[512,896]{1,0:T(8,128)(2,1)}, bf16[512,896]{1,0:T(8,128)(2,1)S(1)}, u32[]{:S(2)}) copy-start(bf16[512,896]{1,0:T(8,128)(2,1)S(1)} %collective-permute-done.31.refs_7_) | copy-start | bytes 2752516
  140.7 25.1 %collective-permute-start.13 = (bf16[512,896]{1,0:T(8,128)(2,1)}, bf16[512,896]{1,0:T(8,128)(2,1)S(1)}, u32[]{:S(2)}, u32[]{:S(2)}) collective-permute-start(bf16[512,896]{1,0:T(8,128)(2,1)} %collective-permute-done.12), channel_id=1, source_target_pairs={{96,32},{98,34},{100,36},{102,38},{104,40},{106,42},{108,44},{110,... | collective-permute-start | bytes 2752520 | tf_op jit(solution)/shard_map/ppermute | solution.py:512
  148.1 32.3 %collective-permute-start.19 = (bf16[8,96,896]{2,1,0:T(8,128)(2,1)S(1)}, bf16[8,96,896]{2,1,0:T(8,128)(2,1)S(1)}, u32[]{:S(2)}, u32[]{:S(2)}) collective-permute-start(bf16[8,96,896]{2,1,0:T(8,128)(2,1)S(1)} %collective-permute-done.18.refs_3_), channel_id=1, source_target_pairs={{96,32},{98,34},{100,36},{102,38},{104,40},{106,42},{108,44},{110,... | collective-permute-start | bytes 4128776 | tf_op jit(solution)/shard_map/ppermute | solution.py:512
  149.5 35.8 %collective-permute-start.3 = (bf16[8,96,896]{2,1,0:T(8,128)(2,1)S(1)}, bf16[8,96,896]{2,1,0:T(8,128)(2,1)S(1)}, u32[]{:S(2)}, u32[]{:S(2)}) collective-permute-start(bf16[8,96,896]{2,1,0:T(8,128)(2,1)S(1)} %collective-permute-done.2), channel_id=1, source_target_pairs={{64,128},{66,130},{68,132},{70,134},{72,136},{74,138},{76,140},{78... | collective-permute-start | bytes 4128776 | tf_op jit(solution)/shard_map/ppermute | solution.py:512
  150.9 37.3 %copy-start.5 = (bf16[512,896]{1,0:T(8,128)(2,1)}, bf16[512,896]{1,0:T(8,128)(2,1)S(1)}, u32[]{:S(2)}) copy-start(bf16[512,896]{1,0:T(8,128)(2,1)S(1)} %broadcast_select_fusion.5.refs_0_) | copy-start | bytes 2752516
  165.8 25.7 %copy-start.13 = (bf16[512,896]{1,0:T(8,128)(2,1)}, bf16[512,896]{1,0:T(8,128)(2,1)S(1)}, u32[]{:S(2)}) copy-start(bf16[512,896]{1,0:T(8,128)(2,1)S(1)} %collective-permute-done.13.refs_0_) | copy-start | bytes 2752516
  165.8 22.5 %collective-permute-start.24 = (bf16[512,896]{1,0:T(8,128)(2,1)S(1)}, bf16[512,896]{1,0:T(8,128)(2,1)S(1)}, u32[]{:S(2)}, u32[]{:S(2)}) collective-permute-start(bf16[512,896]{1,0:T(8,128)(2,1)S(1)} %broadcast_select_fusion.5.refs_0_), channel_id=1, source_target_pairs={{0,32},{2,34},{4,36},{6,38},{8,40},{10,42},{12,44},{14,46},{16,48}... | collective-permute-start | bytes 2752520 | tf_op jit(solution)/shard_map/ppermute | solution.py:515
  165.8 19.6 %copy-start.8 = (bf16[8,96,896]{2,1,0:T(8,128)(2,1)}, bf16[8,96,896]{2,1,0:T(8,128)(2,1)S(1)}, u32[]{:S(2)}) copy-start(bf16[8,96,896]{2,1,0:T(8,128)(2,1)S(1)} %collective-permute-done.25.refs_5_) | copy-start | bytes 4128772
  165.8 24.4 %collective-permute-start.16 = (bf16[512,896]{1,0:T(8,128)(2,1)S(1)}, bf16[512,896]{1,0:T(8,128)(2,1)}, u32[]{:S(2)}, u32[]{:S(2)}) collective-permute-start(bf16[512,896]{1,0:T(8,128)(2,1)S(1)} %collective-permute-done.15), channel_id=1, source_target_pairs={{96,32},{98,34},{100,36},{102,38},{104,40},{106,42},{108,44},{110,... | collective-permute-start | bytes 2752520 | tf_op jit(solution)/shard_map/ppermute | solution.py:512
  170.5 34.6 %collective-permute-start.6 = (bf16[8,96,896]{2,1,0:T(8,128)(2,1)}, bf16[8,96,896]{2,1,0:T(8,128)(2,1)S(1)}, u32[]{:S(2)}, u32[]{:S(2)}) collective-permute-start(bf16[8,96,896]{2,1,0:T(8,128)(2,1)} %collective-permute-done.1), channel_id=1, source_target_pairs={{96,32},{98,34},{100,36},{102,38},{104,40},{106,42},{108,44},{110,... | collective-permute-start | bytes 4128776 | tf_op jit(solution)/shard_map/ppermute | solution.py:512
  180.4 39.3 %collective-permute-start.8 = (bf16[8,96,896]{2,1,0:T(8,128)(2,1)S(1)}, bf16[8,96,896]{2,1,0:T(8,128)(2,1)}, u32[]{:S(2)}, u32[]{:S(2)}) collective-permute-start(bf16[8,96,896]{2,1,0:T(8,128)(2,1)S(1)} %collective-permute-done.2), channel_id=1, source_target_pairs={{96,32},{98,34},{100,36},{102,38},{104,40},{106,42},{108,44},{110,... | collective-permute-start | bytes 4128776 | tf_op jit(solution)/shard_map/ppermute | solution.py:512
  185.4 49.1 %collective-permute-start.4 = (bf16[8,96,896]{2,1,0:T(8,128)(2,1)S(1)}, bf16[8,96,896]{2,1,0:T(8,128)(2,1)S(1)}, u32[]{:S(2)}, u32[]{:S(2)}) collective-permute-start(bf16[8,96,896]{2,1,0:T(8,128)(2,1)S(1)} %collective-permute-done.3), channel_id=1, source_target_pairs={{96,32},{98,34},{100,36},{102,38},{104,40},{106,42},{108,44},{110,... | collective-permute-start | bytes 4128776 | tf_op jit(solution)/shard_map/ppermute | solution.py:512
  188.3 3.2 copy-start
  188.3 46.2 %collective-permute-start.20 = (bf16[8,96,896]{2,1,0:T(8,128)(2,1)S(1)}, bf16[8,96,896]{2,1,0:T(8,128)(2,1)S(1)}, u32[]{:S(2)}, u32[]{:S(2)}) collective-permute-start(bf16[8,96,896]{2,1,0:T(8,128)(2,1)S(1)} %broadcast_select_fusion.1.refs_4_), channel_id=1, source_target_pairs={{0,32},{2,34},{4,36},{6,38},{8,40},{10,42},{12,44},{14,46},{16,48}... | collective-permute-start | bytes 4128776 | tf_op jit(solution)/shard_map/ppermute | solution.py:515
  190.3 15.0 %collective-permute-start.14 = (bf16[512,896]{1,0:T(8,128)(2,1)S(1)}, bf16[512,896]{1,0:T(8,128)(2,1)S(1)}, u32[]{:S(2)}, u32[]{:S(2)}) collective-permute-start(bf16[512,896]{1,0:T(8,128)(2,1)S(1)} %collective-permute-done.13.refs_0_), channel_id=1, source_target_pairs={{0,32},{2,34},{4,36},{6,38},{8,40},{10,42},{12,44},{14,46},{16,48}... | collective-permute-start | bytes 2752520 | tf_op jit(solution)/shard_map/ppermute | solution.py:515
  205.1 53.4 %collective-permute-start.22 = (bf16[8,96,896]{2,1,0:T(8,128)(2,1)}, bf16[8,96,896]{2,1,0:T(8,128)(2,1)}, u32[]{:S(2)}, u32[]{:S(2)}) collective-permute-start(bf16[8,96,896]{2,1,0:T(8,128)(2,1)} %broadcast_select_fusion.refs_6_), channel_id=1, source_target_pairs={{0,32},{2,34},{4,36},{6,38},{8,40},{10,42},{12,44},{14,46},{16,48}... | collective-permute-start | bytes 4128776 | tf_op jit(solution)/shard_map/ppermute | solution.py:515
  205.3 44.2 %copy-start.1 = (bf16[8,96,896]{2,1,0:T(8,128)(2,1)}, bf16[8,96,896]{2,1,0:T(8,128)(2,1)S(1)}, u32[]{:S(2)}) copy-start(bf16[8,96,896]{2,1,0:T(8,128)(2,1)S(1)} %broadcast_select_fusion.2.refs_0_) | copy-start | bytes 4128772
  205.3 29.2 %copy-start.15 = (bf16[512,896]{1,0:T(8,128)(2,1)}, bf16[512,896]{1,0:T(8,128)(2,1)S(1)}, u32[]{:S(2)}) copy-start(bf16[512,896]{1,0:T(8,128)(2,1)S(1)} %collective-permute-done.14.refs_1_) | copy-start | bytes 2752516
  205.3 64.1 %collective-permute-start.7 = (bf16[8,96,896]{2,1,0:T(8,128)(2,1)S(1)}, bf16[8,96,896]{2,1,0:T(8,128)(2,1)}, u32[]{:S(2)}, u32[]{:S(2)}) collective-permute-start(bf16[8,96,896]{2,1,0:T(8,128)(2,1)S(1)} %broadcast_select_fusion.2.refs_0_), channel_id=1, source_target_pairs={{0,32},{2,34},{4,36},{6,38},{8,40},{10,42},{12,44},{14,46},{16,48}... | collective-permute-start | bytes 4128776 | tf_op jit(solution)/shard_map/ppermute | solution.py:515
  219.7 49.7 %collective-permute-start.9 = (bf16[8,96,896]{2,1,0:T(8,128)(2,1)}, bf16[8,96,896]{2,1,0:T(8,128)(2,1)}, u32[]{:S(2)}, u32[]{:S(2)}) collective-permute-start(bf16[8,96,896]{2,1,0:T(8,128)(2,1)} %collective-permute-done.8.refs_2_), channel_id=1, source_target_pairs={{0,32},{2,34},{4,36},{6,38},{8,40},{10,42},{12,44},{14,46},{16,48}... | collective-permute-start | bytes 4128776 | tf_op jit(solution)/shard_map/ppermute | solution.py:515
  234.5 15.0 %copy-start.9 = (bf16[8,96,896]{2,1,0:T(8,128)(2,1)}, bf16[8,96,896]{2,1,0:T(8,128)(2,1)S(1)}, u32[]{:S(2)}) copy-start(bf16[8,96,896]{2,1,0:T(8,128)(2,1)S(1)} %collective-permute-done.4.refs_0_) | copy-start | bytes 4128772
  234.5 42.0 %collective-permute-start.5 = (bf16[8,96,896]{2,1,0:T(8,128)(2,1)S(1)}, bf16[8,96,896]{2,1,0:T(8,128)(2,1)}, u32[]{:S(2)}, u32[]{:S(2)}) collective-permute-start(bf16[8,96,896]{2,1,0:T(8,128)(2,1)S(1)} %collective-permute-done.4.refs_0_), channel_id=1, source_target_pairs={{0,32},{2,34},{4,36},{6,38},{8,40},{10,42},{12,44},{14,46},{16,48}... | collective-permute-start | bytes 4128776 | tf_op jit(solution)/shard_map/ppermute | solution.py:515
  235.6 22.9 %collective-permute-start.17 = (bf16[512,896]{1,0:T(8,128)(2,1)}, bf16[512,896]{1,0:T(8,128)(2,1)}, u32[]{:S(2)}, u32[]{:S(2)}) collective-permute-start(bf16[512,896]{1,0:T(8,128)(2,1)} %collective-permute-done.16.refs_2_), channel_id=1, source_target_pairs={{0,32},{2,34},{4,36},{6,38},{8,40},{10,42},{12,44},{14,46},{16,48}... | collective-permute-start | bytes 2752520 | tf_op jit(solution)/shard_map/ppermute | solution.py:515
  304.9 18.0 %all-to-all-start.2 = ((bf16[16,112,256]{2,1,0:T(8,128)(2,1)}), bf16[16,112,256]{2,1,0:T(8,128)(2,1)S(1)}, u32[]{:S(2)}, u32[]{:S(2)}) async-start(bf16[16,112,256]{2,1,0:T(8,128)(2,1)} %get-tuple-element.34), calls=%async_computation.2 | async-start | bytes 1835008 | tf_op jit(solution)/shard_map/all_to_all | solution.py:598
  308.5 14.3 %collective-permute-start.32 = (bf16[112,256]{1,0:T(8,128)(2,1)S(1)}, bf16[112,256]{1,0:T(8,128)(2,1)S(1)}, u32[]{:S(2)}, u32[]{:S(2)}) collective-permute-start(bf16[112,256]{1,0:T(8,128)(2,1)S(1)} %dynamic-slice_bitcast_fusion), channel_id=1, source_target_pairs={{0,1},{2,3},{4,5},{6,7},{8,9},{10,11},{12,13},{14,15},{16,17},{18,... | collective-permute-start | bytes 172040 | tf_op jit(solution)/shard_map/ppermute | solution.py:603
  (4 other events, 6.2 us)

commit v6 on v5

--- a/solution.py
+++ b/solution.py
@@ -408,7 +408,7 @@
         for copy in others[:2]:
             copy.wait()
         row_terms(up_ref, down_ref, held_x, held_c, held_pre, held_hid, total)
-        for copy in others[2:]:
+        for copy in others[2:5]:
             copy.wait()
 
         def leave_steps(j):
@@ -424,12 +424,17 @@
                 both.at[span, :], out.at[owner[t] >> 1], tile_sems.at[t]
             )
 
-        def columns(j, carry):
+        def down_columns(j, carry):
             span = pl.ds(pl.multiple_of(j * step, step), step)
             grad = old_down[:, span] + column_sums(held_hid[...], held_c[:, span])
             step_down = adam_step(grad, md[:, span], vd[:, span])
             both[span, hidden_units:] = step_down.T.astype(jnp.bfloat16)
             moved_down[:, span] = jnp.where(keep, step_down, 0.0).astype(jnp.bfloat16)
+            leave_steps(j)[1].start()
+            return carry
+
+        def up_columns(j, carry):
+            span = pl.ds(pl.multiple_of(j * step, step), step)
             grad = old_up[:, span] + column_sums(held_pre[...], held_x[:, span])
             step_up = adam_step(grad.T, mu[span, :], vu[span, :])
             both[span, :hidden_units] = step_up.astype(jnp.bfloat16)
@@ -439,8 +444,7 @@
                 near = (owner[t] & 1) == half_ref[0]
                 pl.when(near)(tile_copy(t, out_near).start)
                 pl.when(jnp.logical_not(near))(tile_copy(t, out_far).start)
-            for copy in leave_steps(j):
-                copy.start()
+            leave_steps(j)[0].start()
             return carry
 
         def drain(j, carry):
@@ -450,7 +454,10 @@
                 tile_copy(j * each + k, out_near).wait()
             return carry
 
-        lax.fori_loop(0, PIECES, columns, 0)
+        lax.fori_loop(0, PIECES, down_columns, 0)
+        for copy in others[5:]:
+            copy.wait()
+        lax.fori_loop(0, PIECES, up_columns, 0)
         lax.fori_loop(0, PIECES, drain, 0)
 
     tile_shape = jax.ShapeDtypeStruct((tiles // 2, tile_rows, 2 * hidden_units), jnp.bfloat16)

time: 330 us -> 330 us (level)
  no operation moved by 1% of the time
where the time goes in v6:
time: 330 us; the launch traced here: 323 us
  waiting for transfers between devices  135 us (41%)
  starting transfers between devices  72 us (22%)
  Pallas kernels  60.4 us (18%)
  blocking collectives  45.1 us (14%)
  other arithmetic  5.66 us (2%)
  local copies, waits for them, and re-layouts  3.63 us (1%)
    ppermute x18, waiting for transfers between devices, step(): return lax.ppermute(value, ALL, stream_pairs(places))  114 us
    ppermute x18, starting transfers between devices, step(): return lax.ppermute(value, ALL, stream_pairs(places))  47.4 us
    pallas_call x4, Pallas kernels, absorb(): pl.pallas_call(body, out_shape=[shape, shape], in_specs=[SMEM] + [HBM] *...  39.7 us
    all_to_all x1, blocking collectives, on_device(): lax.all_to_all(sent.reshape(32, rows // 32, piece), ('co', 'y', 'x'), 0,...  25.9 us
    all_to_all x1, blocking collectives, from_leaver(): incoming = lax.all_to_all(tiles, ('y', 'x'), 0, 0, tiled=True)  19.2 us
    all_to_all x1, waiting for transfers between devices, on_device(): lax.all_to_all(sent.reshape(32, rows // 32, piece), ('co', 'y', 'x'), 0,...  10.6 us
    all_to_all x1, waiting for transfers between devices, from_leaver(): incoming = lax.all_to_all(tiles, ('y', 'x'), 0, 0, tiled=True)  9.8 us
    pallas_call x1, Pallas kernels, finish(): pl.pallas_call(body, out_shape=[jax.ShapeDtypeStruct((width, hidden_units...  9.04 us
  transfers between devices with their start and end apart: 35, of which 15 were waited for; matrix products, arithmetic and copies ran while one was open for 2% of the time, Pallas kernels for 14%

profile of v6, /device:TPU:33, one launch (start us, length us, event | category | flops | bytes accessed | tf_op | source)
XLA Modules:
  0.0 323.4 jit_solution(9414144162775818385)
XLA Ops:
  0.6 3.7 %prepare.2 = bf16[512,896]{1,0:T(8,128)(2,1)} custom-call(s32[1]{0:T(128)} %bitcast.3.base_ref, bf16[128,3584]{1,0:T(8,128)(2,1)} %x_ref.3, bf16[128,3584]{1,0:T(8,128)(2,1)} %c_ref.3, f32[1,128]{1,0:T(1,128)} %bitcast.51, s32[1,128]{1,0:T(1,128)} %bitcast.53), custom_call_target="tpu_custom_call" | custom-call | tf_op jit(solution)/shard_map/prepare/pallas_call | solution.py:106
  4.4 7.8 %all-to-all-start = ((bf16[32,16,896]{2,1,0:T(8,128)(2,1)}), bf16[32,16,896]{2,1,0:T(8,128)(2,1)S(1)}, u32[]{:S(2)}, u32[]{:S(2)}) async-start(bf16[32,16,896]{2,1,0:T(8,128)(2,1)} %bitcast.46), calls=%async_computation | async-start | bytes 1835008 | tf_op jit(solution)/shard_map/all_to_all | solution.py:531
  12.2 4.5 %prepare.3 = bf16[768,896]{1,0:T(8,128)(2,1)} custom-call(s32[1]{0:T(128)} %bitcast.3.base_ref, bf16[128,3584]{1,0:T(8,128)(2,1)} %x_ref.3, bf16[128,3584]{1,0:T(8,128)(2,1)} %c_ref.3, f32[1,128]{1,0:T(1,128)} %bitcast.52, s32[1,128]{1,0:T(1,128)} %bitcast.54), custom_call_target="tpu_custom_call" | custom-call | tf_op jit(solution)/shard_map/prepare/pallas_call | solution.py:106
  16.7 10.6 %all-to-all-done = bf16[32,16,896]{2,1,0:T(8,128)(2,1)S(1)} async-done(((bf16[32,16,896]{2,1,0:T(8,128)(2,1)}), bf16[32,16,896]{2,1,0:T(8,128)(2,1)S(1)}, u32[]{:S(2)}, u32[]{:S(2)}) %all-to-all-start) | async-done | bytes 917536 | tf_op jit(solution)/shard_map/all_to_all | solution.py:531
  27.3 25.9 %all_to_all.20 = bf16[32,24,896]{2,1,0:T(8,128)(2,1)} all-to-all(bf16[32,24,896]{2,1,0:T(8,128)(2,1)} %bitcast.41), channel_id=1, replica_groups=mesh['zl'=4,'co'=2,'y'=4,'x'=4,'zh'=2] {'co','y','x'}, dimensions={0} | all-to-all | bytes 2752512 | tf_op jit(solution)/shard_map/all_to_all | solution.py:531
  53.2 3.4 %arrange.1.refs_2_ = bf16[8,96,896]{2,1,0:T(8,128)(2,1)} custom-call(bf16[768,896]{1,0:T(8,128)(2,1)} %bitcast.42), custom_call_target="tpu_custom_call" | custom-call | tf_op jit(solution)/shard_map/arrange/pallas_call | solution.py:148
  56.7 5.4 %collective-permute-start.10 = (bf16[512,896]{1,0:T(8,128)(2,1)S(1)}, bf16[512,896]{1,0:T(8,128)(2,1)}, u32[]{:S(2)}, u32[]{:S(2)}) collective-permute-start(bf16[512,896]{1,0:T(8,128)(2,1)S(1)} %bitcast.43), channel_id=1, source_target_pairs={{0,64},{2,66},{4,68},{6,70},{8,72},{10,74},{12,76},{14,78},{16,80}... | collective-permute-start | bytes 2752520 | tf_op jit(solution)/shard_map/ppermute | solution.py:519
  62.1 22.4 %collective-permute-done.10.refs_2_ = bf16[512,896]{1,0:T(8,128)(2,1)} collective-permute-done((bf16[512,896]{1,0:T(8,128)(2,1)S(1)}, bf16[512,896]{1,0:T(8,128)(2,1)}, u32[]{:S(2)}, u32[]{:S(2)}) %collective-permute-start.10) | collective-permute-done | bytes 917536 | tf_op jit(solution)/shard_map/ppermute | solution.py:519
  85.8 1.3 collective-permute-start.1
  88.0 10.8 %collective-permute-start.28 = (bf16[512,896]{1,0:T(8,128)(2,1)S(1)}, bf16[512,896]{1,0:T(8,128)(2,1)S(1)}, u32[]{:S(2)}, u32[]{:S(2)}) collective-permute-start(bf16[512,896]{1,0:T(8,128)(2,1)S(1)} %collective-permute-done.26.refs_1_), channel_id=1, source_target_pairs={{96,32},{98,34},{100,36},{102,38},{104,40},{106,42},{108,44},{110,... | collective-permute-start | bytes 2752520 | tf_op jit(solution)/shard_map/ppermute | solution.py:519
  98.9 2.2 collective-permute-start.30
  102.4 6.6 %collective-permute-done.28 = bf16[512,896]{1,0:T(8,128)(2,1)S(1)} collective-permute-done((bf16[512,896]{1,0:T(8,128)(2,1)S(1)}, bf16[512,896]{1,0:T(8,128)(2,1)S(1)}, u32[]{:S(2)}, u32[]{:S(2)}) %collective-permute-start.28) | collective-permute-done | bytes 917536 | tf_op jit(solution)/shard_map/ppermute | solution.py:519
  110.0 4.1 %collective-permute-done.1 = bf16[8,96,896]{2,1,0:T(8,128)(2,1)} collective-permute-done((bf16[8,96,896]{2,1,0:T(8,128)(2,1)S(1)}, bf16[8,96,896]{2,1,0:T(8,128)(2,1)}, u32[]{:S(2)}, u32[]{:S(2)}) %collective-permute-start.1) | collective-permute-done | bytes 1376288 | tf_op jit(solution)/shard_map/ppermute | solution.py:519
  115.4 1.3 broadcast_select_fusion.4.refs_4_
  116.7 2.3 collective-permute-done.30
  119.0 3.0 collective-permute-start.29
  122.0 2.0 collective-permute-done.12
  123.9 2.4 collective-permute-start.23
  126.3 1.3 broadcast_select_fusion.3.refs_6_
  127.7 2.9 collective-permute-start.31
  130.6 1.3 collective-permute-start.15
  131.9 1.4 collective-permute-start.25
  133.3 3.6 %collective-permute-done.23 = bf16[512,896]{1,0:T(8,128)(2,1)S(1)} collective-permute-done((bf16[512,896]{1,0:T(8,128)(2,1)}, bf16[512,896]{1,0:T(8,128)(2,1)S(1)}, u32[]{:S(2)}, u32[]{:S(2)}) %collective-permute-start.23) | collective-permute-done | bytes 917536 | tf_op jit(solution)/shard_map/ppermute | solution.py:519
  136.9 3.8 %collective-permute-start.21 = (bf16[8,96,896]{2,1,0:T(8,128)(2,1)S(1)}, bf16[8,96,896]{2,1,0:T(8,128)(2,1)S(1)}, u32[]{:S(2)}, u32[]{:S(2)}) collective-permute-start(bf16[8,96,896]{2,1,0:T(8,128)(2,1)S(1)} %collective-permute-done.refs_4_), channel_id=1, source_target_pairs={{96,32},{98,34},{100,36},{102,38},{104,40},{106,42},{108,44},{110,... | collective-permute-start | bytes 4128776 | tf_op jit(solution)/shard_map/ppermute | solution.py:519
  140.7 1.3 collective-permute-start.13
  142.1 6.0 %collective-permute-done.15 = bf16[512,896]{1,0:T(8,128)(2,1)S(1)} collective-permute-done((bf16[512,896]{1,0:T(8,128)(2,1)}, bf16[512,896]{1,0:T(8,128)(2,1)S(1)}, u32[]{:S(2)}, u32[]{:S(2)}) %collective-permute-start.15) | collective-permute-done | bytes 917536 | tf_op jit(solution)/shard_map/ppermute | solution.py:519
  148.1 1.4 collective-permute-start.19
  149.5 1.3 collective-permute-start.3
  151.0 14.8 %collective-permute-done.13.refs_0_ = bf16[512,896]{1,0:T(8,128)(2,1)S(1)} collective-permute-done((bf16[512,896]{1,0:T(8,128)(2,1)}, bf16[512,896]{1,0:T(8,128)(2,1)S(1)}, u32[]{:S(2)}, u32[]{:S(2)}) %collective-permute-start.13) | collective-permute-done | bytes 917536 | tf_op jit(solution)/shard_map/ppermute | solution.py:519
  165.8 4.7 %collective-permute-start.16 = (bf16[512,896]{1,0:T(8,128)(2,1)S(1)}, bf16[512,896]{1,0:T(8,128)(2,1)}, u32[]{:S(2)}, u32[]{:S(2)}) collective-permute-start(bf16[512,896]{1,0:T(8,128)(2,1)S(1)} %collective-permute-done.15), channel_id=1, source_target_pairs={{96,32},{98,34},{100,36},{102,38},{104,40},{106,42},{108,44},{110,... | collective-permute-start | bytes 2752520 | tf_op jit(solution)/shard_map/ppermute | solution.py:519
  170.5 1.4 collective-permute-start.6
  171.9 8.5 %collective-permute-done.19 = bf16[8,96,896]{2,1,0:T(8,128)(2,1)S(1)} collective-permute-done((bf16[8,96,896]{2,1,0:T(8,128)(2,1)S(1)}, bf16[8,96,896]{2,1,0:T(8,128)(2,1)S(1)}, u32[]{:S(2)}, u32[]{:S(2)}) %collective-permute-start.19) | collective-permute-done | bytes 1376288 | tf_op jit(solution)/shard_map/ppermute | solution.py:519
  180.4 4.9 %collective-permute-start.8 = (bf16[8,96,896]{2,1,0:T(8,128)(2,1)S(1)}, bf16[8,96,896]{2,1,0:T(8,128)(2,1)}, u32[]{:S(2)}, u32[]{:S(2)}) collective-permute-start(bf16[8,96,896]{2,1,0:T(8,128)(2,1)S(1)} %collective-permute-done.2), channel_id=1, source_target_pairs={{96,32},{98,34},{100,36},{102,38},{104,40},{106,42},{108,44},{110,... | collective-permute-start | bytes 4128776 | tf_op jit(solution)/shard_map/ppermute | solution.py:519
  185.4 1.4 collective-permute-start.4
  186.7 1.5 broadcast_select_fusion.1.refs_4_
  188.4 1.8 collective-permute-done.16.refs_2_
  191.5 13.6 %collective-permute-done.6 = bf16[8,96,896]{2,1,0:T(8,128)(2,1)S(1)} collective-permute-done((bf16[8,96,896]{2,1,0:T(8,128)(2,1)}, bf16[8,96,896]{2,1,0:T(8,128)(2,1)S(1)}, u32[]{:S(2)}, u32[]{:S(2)}) %collective-permute-start.6) | collective-permute-done | bytes 1376288 | tf_op jit(solution)/shard_map/ppermute | solution.py:519
  205.9 13.9 %collective-permute-done.8.refs_2_ = bf16[8,96,896]{2,1,0:T(8,128)(2,1)} collective-permute-done((bf16[8,96,896]{2,1,0:T(8,128)(2,1)S(1)}, bf16[8,96,896]{2,1,0:T(8,128)(2,1)}, u32[]{:S(2)}, u32[]{:S(2)}) %collective-permute-start.8) | collective-permute-done | bytes 1376288 | tf_op jit(solution)/shard_map/ppermute | solution.py:519
  219.7 14.7 %collective-permute-done.4.refs_0_ = bf16[8,96,896]{2,1,0:T(8,128)(2,1)S(1)} collective-permute-done((bf16[8,96,896]{2,1,0:T(8,128)(2,1)S(1)}, bf16[8,96,896]{2,1,0:T(8,128)(2,1)S(1)}, u32[]{:S(2)}, u32[]{:S(2)}) %collective-permute-start.4) | collective-permute-done | bytes 1376288 | tf_op jit(solution)/shard_map/ppermute | solution.py:519
  236.7 12.7 %absorb.4 = (f32[128,3584]{1,0:T(8,128)}, f32[128,3584]{1,0:T(8,128)}) custom-call(s32[1]{0:T(128)} %bitcast.place_ref, bf16[512,896]{1,0:T(8,128)(2,1)} %bitcast.45, bf16[512,896]{1,0:T(8,128)(2,1)} %copy-done.11, bf16[512,896]{1,0:T(8,128)(2,1)} %collective-permute-done.10.refs_2_, bf16[512,896]{1,0:T(8,128)(2,1)} %collective-permute-done.27.refs_3_, ...), custom_call_target="tpu_custom_call" | custom-call | flops 1644167168 | bytes 6422528 | tf_op jit(solution)/shard_map/absorb/pallas_call | solution.py:311
  249.5 9.1 %absorb.5 = (f32[128,3584]{1,0:T(8,128)}, f32[128,3584]{1,0:T(8,128)}) custom-call(s32[1]{0:T(128)} %bitcast.place_ref, bf16[512,896]{1,0:T(8,128)(2,1)} %copy-done.5, bf16[512,896]{1,0:T(8,128)(2,1)} %copy-done.14, bf16[8,96,896]{2,1,0:T(8,128)(2,1)} %arrange.1.refs_2_, ...), custom_call_target="tpu_custom_call", output_to_operand_aliasing={{0}: (9, {}), {1}: (10, {})} | custom-call | flops 1291845632 | bytes 5046272 | tf_op jit(solution)/shard_map/absorb/pallas_call | solution.py:311
  258.6 10.9 %absorb.6 = (f32[128,3584]{1,0:T(8,128)}, f32[128,3584]{1,0:T(8,128)}) custom-call(s32[1]{0:T(128)} %bitcast.place_ref, bf16[512,896]{1,0:T(8,128)(2,1)} %copy-done.13, bf16[512,896]{1,0:T(8,128)(2,1)} %copy-done.15, bf16[512,896]{1,0:T(8,128)(2,1)} %collective-permute-done.16.refs_2_, ...), custom_call_target="tpu_custom_call", output_to_operand_aliasing={{0}: (11, {}), {1}: (12, {})} | custom-call | flops 1879048192 | bytes 7340032 | tf_op jit(solution)/shard_map/absorb/pallas_call | solution.py:311
  269.4 7.1 %absorb.7 = (f32[128,3584]{1,0:T(8,128)}, f32[128,3584]{1,0:T(8,128)}) custom-call(s32[1]{0:T(128)} %bitcast.place_ref, bf16[8,96,896]{2,1,0:T(8,128)(2,1)} %copy-done.1, bf16[8,96,896]{2,1,0:T(8,128)(2,1)} %collective-permute-done.7.refs_1_, bf16[8,96,896]{2,1,0:T(8,128)(2,1)} %collective-permute-done.8.refs_2_, ...), custom_call_target="tpu_custom_call", output_to_operand_aliasing={{0}: (7, {}), {1}: (8, {})} | custom-call | flops 704643072 | bytes 2752512 | tf_op jit(solution)/shard_map/absorb/pallas_call | solution.py:311
  276.5 9.0 %finish.1 = (bf16[3584,128]{1,0:T(8,128)(2,1)}, bf16[128,3584]{1,0:T(8,128)(2,1)}, bf16[16,112,256]{2,1,0:T(8,128)(2,1)}, bf16[16,112,256]{2,1,0:T(8,128)(2,1)}) custom-call(s32[1]{0:T(128)} %bitcast.place_ref, s32[1]{0:T(128)} %bitcast.1.half_ref, s32[1]{0:T(128)} %bitcast.2.me, s32[1]{0:T(128)} %copy.28.leave, s32[32]{0:T(128)} %owner.1, ...), custom_call_target="tpu_custom_call" | custom-call | tf_op jit(solution)/shard_map/finish/pallas_call | solution.py:464
  285.6 19.2 %all_to_all.21 = bf16[16,112,256]{2,1,0:T(8,128)(2,1)S(1)} all-to-all(bf16[16,112,256]{2,1,0:T(8,128)(2,1)} %get-tuple-element.35), channel_id=1, replica_groups=mesh['zl'=4,'co'=2,'y'=4,'x'=4,'zh'=2] {'y','x'}, dimensions={0} | all-to-all | bytes 1835008 | tf_op jit(solution)/shard_map/all_to_all | solution.py:605
  304.8 3.6 %all-to-all-start.2 = ((bf16[16,112,256]{2,1,0:T(8,128)(2,1)}), bf16[16,112,256]{2,1,0:T(8,128)(2,1)S(1)}, u32[]{:S(2)}, u32[]{:S(2)}) async-start(bf16[16,112,256]{2,1,0:T(8,128)(2,1)} %get-tuple-element.34), calls=%async_computation.2 | async-start | bytes 1835008 | tf_op jit(solution)/shard_map/all_to_all | solution.py:605
  308.5 4.5 %collective-permute-start.32 = (bf16[112,256]{1,0:T(8,128)(2,1)S(1)}, bf16[112,256]{1,0:T(8,128)(2,1)S(1)}, u32[]{:S(2)}, u32[]{:S(2)}) collective-permute-start(bf16[112,256]{1,0:T(8,128)(2,1)S(1)} %dynamic-slice_bitcast_fusion), channel_id=1, source_target_pairs={{0,1},{2,3},{4,5},{6,7},{8,9},{10,11},{12,13},{14,15},{16,17},{18,... | collective-permute-start | bytes 172040 | tf_op jit(solution)/shard_map/ppermute | solution.py:610
  313.0 9.8 %all-to-all-done.2 = bf16[16,112,256]{2,1,0:T(8,128)(2,1)S(1)} async-done(((bf16[16,112,256]{2,1,0:T(8,128)(2,1)}), bf16[16,112,256]{2,1,0:T(8,128)(2,1)S(1)}, u32[]{:S(2)}, u32[]{:S(2)}) %all-to-all-start.2) | async-done | bytes 917536 | tf_op jit(solution)/shard_map/all_to_all | solution.py:605
  (75 shorter events, 10.3 us)
Async XLA Ops:
  4.4 22.9 %all-to-all-start = ((bf16[32,16,896]{2,1,0:T(8,128)(2,1)}), bf16[32,16,896]{2,1,0:T(8,128)(2,1)S(1)}, u32[]{:S(2)}, u32[]{:S(2)}) async-start(bf16[32,16,896]{2,1,0:T(8,128)(2,1)} %bitcast.46), calls=%async_computation | async-start | bytes 1835008 | tf_op jit(solution)/shard_map/all_to_all | solution.py:531
  27.3 34.7 %copy-start.2 = (bf16[32,16,896]{2,1,0:T(8,128)(2,1)}, bf16[32,16,896]{2,1,0:T(8,128)(2,1)S(1)}, u32[]{:S(2)}) copy-start(bf16[32,16,896]{2,1,0:T(8,128)(2,1)S(1)} %all-to-all-done) | copy-start | bytes 2752516
  56.7 29.1 %collective-permute-start = (bf16[8,96,896]{2,1,0:T(8,128)(2,1)}, bf16[8,96,896]{2,1,0:T(8,128)(2,1)S(1)}, u32[]{:S(2)}, u32[]{:S(2)}) collective-permute-start(bf16[8,96,896]{2,1,0:T(8,128)(2,1)} %arrange.1.refs_2_), channel_id=1, source_target_pairs={{0,64},{2,66},{4,68},{6,70},{8,72},{10,74},{12,76},{14,78},{16,80}... | collective-permute-start | bytes 4128776 | tf_op jit(solution)/shard_map/ppermute | solution.py:519
  56.7 27.8 %collective-permute-start.10 = (bf16[512,896]{1,0:T(8,128)(2,1)S(1)}, bf16[512,896]{1,0:T(8,128)(2,1)}, u32[]{:S(2)}, u32[]{:S(2)}) collective-permute-start(bf16[512,896]{1,0:T(8,128)(2,1)S(1)} %bitcast.43), channel_id=1, source_target_pairs={{0,64},{2,66},{4,68},{6,70},{8,72},{10,74},{12,76},{14,78},{16,80}... | collective-permute-start | bytes 2752520 | tf_op jit(solution)/shard_map/ppermute | solution.py:519
  62.1 25.0 %collective-permute-start.26 = (bf16[512,896]{1,0:T(8,128)(2,1)S(1)}, bf16[512,896]{1,0:T(8,128)(2,1)S(1)}, u32[]{:S(2)}, u32[]{:S(2)}) collective-permute-start(bf16[512,896]{1,0:T(8,128)(2,1)S(1)} %bitcast.44), channel_id=1, source_target_pairs={{0,32},{2,34},{4,36},{6,38},{8,40},{10,42},{12,44},{14,46},{16,48}... | collective-permute-start | bytes 2752520 | tf_op jit(solution)/shard_map/ppermute | solution.py:522
  84.4 16.7 %collective-permute-start.11 = (bf16[512,896]{1,0:T(8,128)(2,1)}, bf16[512,896]{1,0:T(8,128)(2,1)}, u32[]{:S(2)}, u32[]{:S(2)}) collective-permute-start(bf16[512,896]{1,0:T(8,128)(2,1)} %collective-permute-done.10.refs_2_), channel_id=1, source_target_pairs={{0,64},{2,66},{4,68},{6,70},{8,72},{10,74},{12,76},{14,78},{16,80}... | collective-permute-start | bytes 2752520 | tf_op jit(solution)/shard_map/ppermute | solution.py:519
  85.7 51.2 %copy-start.6 = (bf16[8,96,896]{2,1,0:T(8,128)(2,1)}, bf16[8,96,896]{2,1,0:T(8,128)(2,1)S(1)}, u32[]{:S(2)}) copy-start(bf16[8,96,896]{2,1,0:T(8,128)(2,1)S(1)} %collective-permute-done.refs_4_) | copy-start | bytes 4128772
  85.8 28.4 %collective-permute-start.1 = (bf16[8,96,896]{2,1,0:T(8,128)(2,1)S(1)}, bf16[8,96,896]{2,1,0:T(8,128)(2,1)}, u32[]{:S(2)}, u32[]{:S(2)}) collective-permute-start(bf16[8,96,896]{2,1,0:T(8,128)(2,1)S(1)} %collective-permute-done.refs_4_), channel_id=1, source_target_pairs={{0,64},{2,66},{4,68},{6,70},{8,72},{10,74},{12,76},{14,78},{16,80}... | collective-permute-start | bytes 4128776 | tf_op jit(solution)/shard_map/ppermute | solution.py:519
  88.0 21.1 %collective-permute-start.28 = (bf16[512,896]{1,0:T(8,128)(2,1)S(1)}, bf16[512,896]{1,0:T(8,128)(2,1)S(1)}, u32[]{:S(2)}, u32[]{:S(2)}) collective-permute-start(bf16[512,896]{1,0:T(8,128)(2,1)S(1)} %collective-permute-done.26.refs_1_), channel_id=1, source_target_pairs={{96,32},{98,34},{100,36},{102,38},{104,40},{106,42},{108,44},{110,... | collective-permute-start | bytes 2752520 | tf_op jit(solution)/shard_map/ppermute | solution.py:519
  98.8 31.8 %collective-permute-start.18 = (bf16[8,96,896]{2,1,0:T(8,128)(2,1)}, bf16[8,96,896]{2,1,0:T(8,128)(2,1)S(1)}, u32[]{:S(2)}, u32[]{:S(2)}) collective-permute-start(bf16[8,96,896]{2,1,0:T(8,128)(2,1)} %arrange.1.refs_2_), channel_id=1, source_target_pairs={{0,32},{2,34},{4,36},{6,38},{8,40},{10,42},{12,44},{14,46},{16,48}... | collective-permute-start | bytes 4128776 | tf_op jit(solution)/shard_map/ppermute | solution.py:522
  98.9 20.1 %collective-permute-start.30 = (bf16[512,896]{1,0:T(8,128)(2,1)}, bf16[512,896]{1,0:T(8,128)(2,1)}, u32[]{:S(2)}, u32[]{:S(2)}) collective-permute-start(bf16[512,896]{1,0:T(8,128)(2,1)} %collective-permute-done.10.refs_2_), channel_id=1, source_target_pairs={{96,32},{98,34},{100,36},{102,38},{104,40},{106,42},{108,44},{110,... | collective-permute-start | bytes 2752520 | tf_op jit(solution)/shard_map/ppermute | solution.py:519
  101.1 22.8 %collective-permute-start.12 = (bf16[512,896]{1,0:T(8,128)(2,1)}, bf16[512,896]{1,0:T(8,128)(2,1)}, u32[]{:S(2)}, u32[]{:S(2)}) collective-permute-start(bf16[512,896]{1,0:T(8,128)(2,1)} %collective-permute-done.11), channel_id=1, source_target_pairs={{0,64},{2,66},{4,68},{6,70},{8,72},{10,74},{12,76},{14,78},{16,80}... | collective-permute-start | bytes 2752520 | tf_op jit(solution)/shard_map/ppermute | solution.py:519
  110.0 17.7 %collective-permute-start.27 = (bf16[512,896]{1,0:T(8,128)(2,1)}, bf16[512,896]{1,0:T(8,128)(2,1)}, u32[]{:S(2)}, u32[]{:S(2)}) collective-permute-start(bf16[512,896]{1,0:T(8,128)(2,1)} %collective-permute-done.10.refs_2_), channel_id=1, source_target_pairs={{0,32},{2,34},{4,36},{6,38},{8,40},{10,42},{12,44},{14,46},{16,48}... | collective-permute-start | bytes 2752520 | tf_op jit(solution)/shard_map/ppermute | solution.py:522
  114.1 35.4 %collective-permute-start.2 = (bf16[8,96,896]{2,1,0:T(8,128)(2,1)}, bf16[8,96,896]{2,1,0:T(8,128)(2,1)S(1)}, u32[]{:S(2)}, u32[]{:S(2)}) collective-permute-start(bf16[8,96,896]{2,1,0:T(8,128)(2,1)} %collective-permute-done.1), channel_id=1, source_target_pairs={{0,64},{2,66},{4,68},{6,70},{8,72},{10,74},{12,76},{14,78},{16,80}... | collective-permute-start | bytes 4128776 | tf_op jit(solution)/shard_map/ppermute | solution.py:519
  116.7 10.9 %copy-start.3 = (bf16[512,896]{1,0:T(8,128)(2,1)}, bf16[512,896]{1,0:T(8,128)(2,1)S(1)}, u32[]{:S(2)}) copy-start(bf16[512,896]{1,0:T(8,128)(2,1)S(1)} %broadcast_select_fusion.4.refs_4_) | copy-start | bytes 2752516
  119.0 12.9 %collective-permute-start.29 = (bf16[512,896]{1,0:T(8,128)(2,1)S(1)}, bf16[512,896]{1,0:T(8,128)(2,1)}, u32[]{:S(2)}, u32[]{:S(2)}) collective-permute-start(bf16[512,896]{1,0:T(8,128)(2,1)S(1)} %broadcast_select_fusion.4.refs_4_), channel_id=1, source_target_pairs={{0,32},{2,34},{4,36},{6,38},{8,40},{10,42},{12,44},{14,46},{16,48}... | collective-permute-start | bytes 2752520 | tf_op jit(solution)/shard_map/ppermute | solution.py:522
  123.9 13.0 %collective-permute-start.23 = (bf16[512,896]{1,0:T(8,128)(2,1)}, bf16[512,896]{1,0:T(8,128)(2,1)S(1)}, u32[]{:S(2)}, u32[]{:S(2)}) collective-permute-start(bf16[512,896]{1,0:T(8,128)(2,1)} %collective-permute-done.11), channel_id=1, source_target_pairs={{96,32},{98,34},{100,36},{102,38},{104,40},{106,42},{108,44},{110,... | collective-permute-start | bytes 2752520 | tf_op jit(solution)/shard_map/ppermute | solution.py:519
  127.6 23.3 %copy-start.4 = (bf16[512,896]{1,0:T(8,128)(2,1)}, bf16[512,896]{1,0:T(8,128)(2,1)S(1)}, u32[]{:S(2)}) copy-start(bf16[512,896]{1,0:T(8,128)(2,1)S(1)} %broadcast_select_fusion.3.refs_6_) | copy-start | bytes 2752516
  127.7 13.0 %collective-permute-start.31 = (bf16[512,896]{1,0:T(8,128)(2,1)S(1)}, bf16[512,896]{1,0:T(8,128)(2,1)S(1)}, u32[]{:S(2)}, u32[]{:S(2)}) collective-permute-start(bf16[512,896]{1,0:T(8,128)(2,1)S(1)} %broadcast_select_fusion.3.refs_6_), channel_id=1, source_target_pairs={{0,32},{2,34},{4,36},{6,38},{8,40},{10,42},{12,44},{14,46},{16,48}... | collective-permute-start | bytes 2752520 | tf_op jit(solution)/shard_map/ppermute | solution.py:522
  130.6 20.3 %copy-start.7 = (bf16[8,96,896]{2,1,0:T(8,128)(2,1)}, bf16[8,96,896]{2,1,0:T(8,128)(2,1)S(1)}, u32[]{:S(2)}) copy-start(bf16[8,96,896]{2,1,0:T(8,128)(2,1)S(1)} %collective-permute-done.18.refs_3_) | copy-start | bytes 4128772
  130.6 17.5 %collective-permute-start.15 = (bf16[512,896]{1,0:T(8,128)(2,1)}, bf16[512,896]{1,0:T(8,128)(2,1)S(1)}, u32[]{:S(2)}, u32[]{:S(2)}) collective-permute-start(bf16[512,896]{1,0:T(8,128)(2,1)} %collective-permute-done.12), channel_id=1, source_target_pairs={{64,128},{66,130},{68,132},{70,134},{72,136},{74,138},{76,140},{78... | collective-permute-start | bytes 2752520 | tf_op jit(solution)/shard_map/ppermute | solution.py:519
  131.9 33.9 %collective-permute-start.25 = (bf16[8,96,896]{2,1,0:T(8,128)(2,1)S(1)}, bf16[8,96,896]{2,1,0:T(8,128)(2,1)S(1)}, u32[]{:S(2)}, u32[]{:S(2)}) collective-permute-start(bf16[8,96,896]{2,1,0:T(8,128)(2,1)S(1)} %collective-permute-done.refs_4_), channel_id=1, source_target_pairs={{0,32},{2,34},{4,36},{6,38},{8,40},{10,42},{12,44},{14,46},{16,48}... | collective-permute-start | bytes 4128776 | tf_op jit(solution)/shard_map/ppermute | solution.py:522
  136.9 33.6 %collective-permute-start.21 = (bf16[8,96,896]{2,1,0:T(8,128)(2,1)S(1)}, bf16[8,96,896]{2,1,0:T(8,128)(2,1)S(1)}, u32[]{:S(2)}, u32[]{:S(2)}) collective-permute-start(bf16[8,96,896]{2,1,0:T(8,128)(2,1)S(1)} %collective-permute-done.refs_4_), channel_id=1, source_target_pairs={{96,32},{98,34},{100,36},{102,38},{104,40},{106,42},{108,44},{110,... | collective-permute-start | bytes 4128776 | tf_op jit(solution)/shard_map/ppermute | solution.py:519
  140.7 8.8 %copy-start.12 = (bf16[512,896]{1,0:T(8,128)(2,1)}, bf16[512,896]{1,0:T(8,128)(2,1)S(1)}, u32[]{:S(2)}) copy-start(bf16[512,896]{1,0:T(8,128)(2,1)S(1)} %collective-permute-done.31.refs_7_) | copy-start | bytes 2752516
  140.7 25.1 %collective-permute-start.13 = (bf16[512,896]{1,0:T(8,128)(2,1)}, bf16[512,896]{1,0:T(8,128)(2,1)S(1)}, u32[]{:S(2)}, u32[]{:S(2)}) collective-permute-start(bf16[512,896]{1,0:T(8,128)(2,1)} %collective-permute-done.12), channel_id=1, source_target_pairs={{96,32},{98,34},{100,36},{102,38},{104,40},{106,42},{108,44},{110,... | collective-permute-start | bytes 2752520 | tf_op jit(solution)/shard_map/ppermute | solution.py:519
  148.1 32.3 %collective-permute-start.19 = (bf16[8,96,896]{2,1,0:T(8,128)(2,1)S(1)}, bf16[8,96,896]{2,1,0:T(8,128)(2,1)S(1)}, u32[]{:S(2)}, u32[]{:S(2)}) collective-permute-start(bf16[8,96,896]{2,1,0:T(8,128)(2,1)S(1)} %collective-permute-done.18.refs_3_), channel_id=1, source_target_pairs={{96,32},{98,34},{100,36},{102,38},{104,40},{106,42},{108,44},{110,... | collective-permute-start | bytes 4128776 | tf_op jit(solution)/shard_map/ppermute | solution.py:519
  149.5 35.8 %collective-permute-start.3 = (bf16[8,96,896]{2,1,0:T(8,128)(2,1)S(1)}, bf16[8,96,896]{2,1,0:T(8,128)(2,1)S(1)}, u32[]{:S(2)}, u32[]{:S(2)}) collective-permute-start(bf16[8,96,896]{2,1,0:T(8,128)(2,1)S(1)} %collective-permute-done.2), channel_id=1, source_target_pairs={{64,128},{66,130},{68,132},{70,134},{72,136},{74,138},{76,140},{78... | collective-permute-start | bytes 4128776 | tf_op jit(solution)/shard_map/ppermute | solution.py:519
  150.9 37.3 %copy-start.5 = (bf16[512,896]{1,0:T(8,128)(2,1)}, bf16[512,896]{1,0:T(8,128)(2,1)S(1)}, u32[]{:S(2)}) copy-start(bf16[512,896]{1,0:T(8,128)(2,1)S(1)} %broadcast_select_fusion.5.refs_0_) | copy-start | bytes 2752516
  165.8 25.7 %copy-start.13 = (bf16[512,896]{1,0:T(8,128)(2,1)}, bf16[512,896]{1,0:T(8,128)(2,1)S(1)}, u32[]{:S(2)}) copy-start(bf16[512,896]{1,0:T(8,128)(2,1)S(1)} %collective-permute-done.13.refs_0_) | copy-start | bytes 2752516
  165.8 22.5 %collective-permute-start.24 = (bf16[512,896]{1,0:T(8,128)(2,1)S(1)}, bf16[512,896]{1,0:T(8,128)(2,1)S(1)}, u32[]{:S(2)}, u32[]{:S(2)}) collective-permute-start(bf16[512,896]{1,0:T(8,128)(2,1)S(1)} %broadcast_select_fusion.5.refs_0_), channel_id=1, source_target_pairs={{0,32},{2,34},{4,36},{6,38},{8,40},{10,42},{12,44},{14,46},{16,48}... | collective-permute-start | bytes 2752520 | tf_op jit(solution)/shard_map/ppermute | solution.py:522
  165.8 19.6 %copy-start.8 = (bf16[8,96,896]{2,1,0:T(8,128)(2,1)}, bf16[8,96,896]{2,1,0:T(8,128)(2,1)S(1)}, u32[]{:S(2)}) copy-start(bf16[8,96,896]{2,1,0:T(8,128)(2,1)S(1)} %collective-permute-done.25.refs_5_) | copy-start | bytes 4128772
  165.8 24.4 %collective-permute-start.16 = (bf16[512,896]{1,0:T(8,128)(2,1)S(1)}, bf16[512,896]{1,0:T(8,128)(2,1)}, u32[]{:S(2)}, u32[]{:S(2)}) collective-permute-start(bf16[512,896]{1,0:T(8,128)(2,1)S(1)} %collective-permute-done.15), channel_id=1, source_target_pairs={{96,32},{98,34},{100,36},{102,38},{104,40},{106,42},{108,44},{110,... | collective-permute-start | bytes 2752520 | tf_op jit(solution)/shard_map/ppermute | solution.py:519
  170.5 34.6 %collective-permute-start.6 = (bf16[8,96,896]{2,1,0:T(8,128)(2,1)}, bf16[8,96,896]{2,1,0:T(8,128)(2,1)S(1)}, u32[]{:S(2)}, u32[]{:S(2)}) collective-permute-start(bf16[8,96,896]{2,1,0:T(8,128)(2,1)} %collective-permute-done.1), channel_id=1, source_target_pairs={{96,32},{98,34},{100,36},{102,38},{104,40},{106,42},{108,44},{110,... | collective-permute-start | bytes 4128776 | tf_op jit(solution)/shard_map/ppermute | solution.py:519
  180.4 39.3 %collective-permute-start.8 = (bf16[8,96,896]{2,1,0:T(8,128)(2,1)S(1)}, bf16[8,96,896]{2,1,0:T(8,128)(2,1)}, u32[]{:S(2)}, u32[]{:S(2)}) collective-permute-start(bf16[8,96,896]{2,1,0:T(8,128)(2,1)S(1)} %collective-permute-done.2), channel_id=1, source_target_pairs={{96,32},{98,34},{100,36},{102,38},{104,40},{106,42},{108,44},{110,... | collective-permute-start | bytes 4128776 | tf_op jit(solution)/shard_map/ppermute | solution.py:519
  185.4 49.1 %collective-permute-start.4 = (bf16[8,96,896]{2,1,0:T(8,128)(2,1)S(1)}, bf16[8,96,896]{2,1,0:T(8,128)(2,1)S(1)}, u32[]{:S(2)}, u32[]{:S(2)}) collective-permute-start(bf16[8,96,896]{2,1,0:T(8,128)(2,1)S(1)} %collective-permute-done.3), channel_id=1, source_target_pairs={{96,32},{98,34},{100,36},{102,38},{104,40},{106,42},{108,44},{110,... | collective-permute-start | bytes 4128776 | tf_op jit(solution)/shard_map/ppermute | solution.py:519
  188.3 3.2 copy-start
  188.3 46.2 %collective-permute-start.20 = (bf16[8,96,896]{2,1,0:T(8,128)(2,1)S(1)}, bf16[8,96,896]{2,1,0:T(8,128)(2,1)S(1)}, u32[]{:S(2)}, u32[]{:S(2)}) collective-permute-start(bf16[8,96,896]{2,1,0:T(8,128)(2,1)S(1)} %broadcast_select_fusion.1.refs_4_), channel_id=1, source_target_pairs={{0,32},{2,34},{4,36},{6,38},{8,40},{10,42},{12,44},{14,46},{16,48}... | collective-permute-start | bytes 4128776 | tf_op jit(solution)/shard_map/ppermute | solution.py:522
  190.3 15.0 %collective-permute-start.14 = (bf16[512,896]{1,0:T(8,128)(2,1)S(1)}, bf16[512,896]{1,0:T(8,128)(2,1)S(1)}, u32[]{:S(2)}, u32[]{:S(2)}) collective-permute-start(bf16[512,896]{1,0:T(8,128)(2,1)S(1)} %collective-permute-done.13.refs_0_), channel_id=1, source_target_pairs={{0,32},{2,34},{4,36},{6,38},{8,40},{10,42},{12,44},{14,46},{16,48}... | collective-permute-start | bytes 2752520 | tf_op jit(solution)/shard_map/ppermute | solution.py:522
  205.1 53.4 %collective-permute-start.22 = (bf16[8,96,896]{2,1,0:T(8,128)(2,1)}, bf16[8,96,896]{2,1,0:T(8,128)(2,1)}, u32[]{:S(2)}, u32[]{:S(2)}) collective-permute-start(bf16[8,96,896]{2,1,0:T(8,128)(2,1)} %broadcast_select_fusion.refs_6_), channel_id=1, source_target_pairs={{0,32},{2,34},{4,36},{6,38},{8,40},{10,42},{12,44},{14,46},{16,48}... | collective-permute-start | bytes 4128776 | tf_op jit(solution)/shard_map/ppermute | solution.py:522
  205.3 44.2 %copy-start.1 = (bf16[8,96,896]{2,1,0:T(8,128)(2,1)}, bf16[8,96,896]{2,1,0:T(8,128)(2,1)S(1)}, u32[]{:S(2)}) copy-start(bf16[8,96,896]{2,1,0:T(8,128)(2,1)S(1)} %broadcast_select_fusion.2.refs_0_) | copy-start | bytes 4128772
  205.3 29.2 %copy-start.15 = (bf16[512,896]{1,0:T(8,128)(2,1)}, bf16[512,896]{1,0:T(8,128)(2,1)S(1)}, u32[]{:S(2)}) copy-start(bf16[512,896]{1,0:T(8,128)(2,1)S(1)} %collective-permute-done.14.refs_1_) | copy-start | bytes 2752516
  205.3 64.1 %collective-permute-start.7 = (bf16[8,96,896]{2,1,0:T(8,128)(2,1)S(1)}, bf16[8,96,896]{2,1,0:T(8,128)(2,1)}, u32[]{:S(2)}, u32[]{:S(2)}) collective-permute-start(bf16[8,96,896]{2,1,0:T(8,128)(2,1)S(1)} %broadcast_select_fusion.2.refs_0_), channel_id=1, source_target_pairs={{0,32},{2,34},{4,36},{6,38},{8,40},{10,42},{12,44},{14,46},{16,48}... | collective-permute-start | bytes 4128776 | tf_op jit(solution)/shard_map/ppermute | solution.py:522
  219.7 49.7 %collective-permute-start.9 = (bf16[8,96,896]{2,1,0:T(8,128)(2,1)}, bf16[8,96,896]{2,1,0:T(8,128)(2,1)}, u32[]{:S(2)}, u32[]{:S(2)}) collective-permute-start(bf16[8,96,896]{2,1,0:T(8,128)(2,1)} %collective-permute-done.8.refs_2_), channel_id=1, source_target_pairs={{0,32},{2,34},{4,36},{6,38},{8,40},{10,42},{12,44},{14,46},{16,48}... | collective-permute-start | bytes 4128776 | tf_op jit(solution)/shard_map/ppermute | solution.py:522
  234.5 15.0 %copy-start.9 = (bf16[8,96,896]{2,1,0:T(8,128)(2,1)}, bf16[8,96,896]{2,1,0:T(8,128)(2,1)S(1)}, u32[]{:S(2)}) copy-start(bf16[8,96,896]{2,1,0:T(8,128)(2,1)S(1)} %collective-permute-done.4.refs_0_) | copy-start | bytes 4128772
  234.5 42.0 %collective-permute-start.5 = (bf16[8,96,896]{2,1,0:T(8,128)(2,1)S(1)}, bf16[8,96,896]{2,1,0:T(8,128)(2,1)}, u32[]{:S(2)}, u32[]{:S(2)}) collective-permute-start(bf16[8,96,896]{2,1,0:T(8,128)(2,1)S(1)} %collective-permute-done.4.refs_0_), channel_id=1, source_target_pairs={{0,32},{2,34},{4,36},{6,38},{8,40},{10,42},{12,44},{14,46},{16,48}... | collective-permute-start | bytes 4128776 | tf_op jit(solution)/shard_map/ppermute | solution.py:522
  235.6 22.9 %collective-permute-start.17 = (bf16[512,896]{1,0:T(8,128)(2,1)}, bf16[512,896]{1,0:T(8,128)(2,1)}, u32[]{:S(2)}, u32[]{:S(2)}) collective-permute-start(bf16[512,896]{1,0:T(8,128)(2,1)} %collective-permute-done.16.refs_2_), channel_id=1, source_target_pairs={{0,32},{2,34},{4,36},{6,38},{8,40},{10,42},{12,44},{14,46},{16,48}... | collective-permute-start | bytes 2752520 | tf_op jit(solution)/shard_map/ppermute | solution.py:522
  304.8 18.0 %all-to-all-start.2 = ((bf16[16,112,256]{2,1,0:T(8,128)(2,1)}), bf16[16,112,256]{2,1,0:T(8,128)(2,1)S(1)}, u32[]{:S(2)}, u32[]{:S(2)}) async-start(bf16[16,112,256]{2,1,0:T(8,128)(2,1)} %get-tuple-element.34), calls=%async_computation.2 | async-start | bytes 1835008 | tf_op jit(solution)/shard_map/all_to_all | solution.py:605
  308.5 14.3 %collective-permute-start.32 = (bf16[112,256]{1,0:T(8,128)(2,1)S(1)}, bf16[112,256]{1,0:T(8,128)(2,1)S(1)}, u32[]{:S(2)}, u32[]{:S(2)}) collective-permute-start(bf16[112,256]{1,0:T(8,128)(2,1)S(1)} %dynamic-slice_bitcast_fusion), channel_id=1, source_target_pairs={{0,1},{2,3},{4,5},{6,7},{8,9},{10,11},{12,13},{14,15},{16,17},{18,... | collective-permute-start | bytes 172040 | tf_op jit(solution)/shard_map/ppermute | solution.py:610
  (4 other events, 6.2 us)
